TPU v7x, 32 devices: a whole 2x2x4 slice. The times are simulated.
32 devices in a mesh: seq: 8 (over z, y), head: 4 (over x, core).
Axes of the slice: x: 2, y: 2, z: 4, core: 2. Of those that a mesh axis runs over, the one named last changes fastest.
Arguments:
- tokens: bfloat16 [8192, 1536], P('seq', 'head'), may hold values from -6 to 6
- segment_ids: int32 [8192], replicated, may hold values from 0 to 7, never falling along the last dimension, each value on 1 to 2000 neighbouring positions
- first_gain: float32 [1536], P('head'), may hold values from 0.5 to 1.5
- proj_zx: bfloat16 [1536, 2, 3072], P(None, None, 'head'), may hold values from -0.15625 to 0.15625
- proj_bc: bfloat16 [1536, 256], replicated, may hold values from -0.15625 to 0.15625
- proj_step: bfloat16 [1536, 48], P(None, 'head'), may hold values from -0.3125 to 0.3125
- conv_inner: float32 [4, 3072], P(None, 'head'), may hold values from -3 to 3
- conv_inner_bias: float32 [3072], P('head'), may hold values from -1.8 to 1.8
- conv_state: float32 [4, 256], replicated, may hold values from -3 to 3
- conv_state_bias: float32 [256], replicated, may hold values from -1.8 to 1.8
- step_bias: float32 [48], P('head'), may hold values from -5 to 0
- decay_log: float32 [48], P('head'), may hold values from -8 to 1
- skip_scale: float32 [48], P('head'), may hold values from 0.5 to 1.5
- gated_gain: float32 [3072], P('head'), may hold values from 0.5 to 1.5
- proj_out: bfloat16 [3072, 1536], P('head'), may hold values from -0.109375 to 0.109375
- second_gain: float32 [1536], P('head'), may hold values from 0.5 to 1.5
- proj_qkv: bfloat16 [1536, 3, 1536], P(None, None, 'head'), may hold values from -0.15625 to 0.15625
- attention_out: bfloat16 [1536, 1536], P('head'), may hold values from -0.625 to 0.625
- cotangent: bfloat16 [8192, 1536], P('seq', 'head'), may hold values from -6 to 6
Outputs:
- output: bfloat16 [8192, 1536], P('seq', 'head')
- grad_tokens: bfloat16 [8192, 1536], P('seq', 'head')
- grad_first_gain: float32 [1536], P('head')
- grad_proj_zx: float32 [1536, 2, 3072], P('seq', None, 'head')
- grad_proj_bc: float32 [1536, 256], P(None, ('seq', 'head'))
- grad_proj_step: float32 [1536, 48], P('seq', 'head')
- grad_conv_inner: float32 [4, 3072], P(None, 'head')
- grad_conv_inner_bias: float32 [3072], P('head')
- grad_conv_state: float32 [4, 256], P(None, ('seq', 'head'))
- grad_conv_state_bias: float32 [256], P(('seq', 'head'))
- grad_step_bias: float32 [48], P('head')
- grad_decay_log: float32 [48], P('head')
- grad_skip_scale: float32 [48], P('head')
- grad_gated_gain: float32 [3072], P('head')
- grad_proj_out: float32 [3072, 1536], P('head', 'seq')
- grad_second_gain: float32 [1536], P('head')
- grad_proj_qkv: float32 [1536, 3, 1536], P('seq', None, 'head')
- grad_attention_out: float32 [1536, 1536], P('head', 'seq')
Inputs may be any that keep to these rules, and one draw needn't show every extreme that they name: `segment_ids`: ids never fall along the sequence; a document (run of equal ids) has at most 2000 tokens, and some document has exactly 2000.
All inputs are finite; a program needn't handle non-finite values.
Results may differ from a plain program's by a relative error of at most 0.03.
Values may be sent and summed in bfloat16 or wider, within the bound.
A program may use at most 448 MiB of HBM per device.

v0:
```python
from functools import partial
import math

import jax
import jax.numpy as jnp
from jax import lax
from jax.sharding import PartitionSpec as P

D = 1536
ATT_DIM = 64
SPAN = 256
CONV = 4
DOC_MAX = 2000
INNER = 3072


epsilon = 1e-05
highest = lax.Precision.HIGHEST
masked_score = -1e30


def from_behind(value, axis, by):
    count = lax.axis_size(axis)
    pairs = [(i, i + by) for i in range(count) if 0 <= i + by < count]
    return lax.ppermute(value, axis, pairs)


def entering_2(value, axis, join, neutral):
    place = lax.axis_index(axis)
    gathered = jax.tree.map(
        lambda a, kind: lax.all_gather(a.astype(kind), axis), value, (jnp.bfloat16, jnp.bfloat16)
    )
    state = jax.tree.map(lambda a, e: jnp.zeros_like(a) + jnp.asarray(e, a.dtype), value, neutral)

    def entering_one(step, state):
        return join(
            state,
            jax.tree.map(
                lambda a, own: lax.dynamic_index_in_dim(a, step, 0, False).astype(own.dtype),
                gathered,
                value,
            ),
        )

    return lax.fori_loop(0, place, entering_one, state)


def prefix(value, axis, join, neutral):
    count = lax.axis_size(axis)
    place = lax.axis_index(axis)
    ahead = count - 1 - place
    gathered = jax.tree.map(
        lambda a, kind: lax.all_gather(a.astype(kind), axis),
        value,
        jax.tree.map(lambda a: jnp.bfloat16 if a.dtype == jnp.float32 else a.dtype, value),
    )
    state = jax.tree.map(lambda a, e: jnp.zeros_like(a) + jnp.asarray(e, a.dtype), value, neutral)

    def prefix_one(step, state):
        source = count - 1 - step
        return join(
            state,
            jax.tree.map(
                lambda a, own: lax.dynamic_index_in_dim(a, source, 0, False).astype(own.dtype),
                gathered,
                value,
            ),
        )

    return lax.fori_loop(0, ahead, prefix_one, state)


def head_totals(values):
    return lax.psum(values, "head")


def head_gather(values):
    return lax.all_gather(values, "head", axis=1, tiled=True)


def head_scatter(values):
    return lax.psum_scatter(values, "head", scatter_dimension=1, tiled=True)


def shard_norm(hidden, summed, gain, full_width):
    return hidden * lax.rsqrt(summed[:, None] / full_width + epsilon) * gain


def gate_piece(ssd_out, gate_z):
    return ssd_out * jax.nn.silu(gate_z)


def conv_piece(conv_input, edge_rows, conv_weight, conv_bias, local_seg, edge_seg):
    row_count = conv_input.shape[0]
    padded = jnp.concatenate([edge_rows, conv_input], axis=0)
    padded_seg = jnp.concatenate([edge_seg, local_seg])
    summed = jnp.zeros(conv_input.shape, jnp.float32) + conv_bias[None, :]
    for tap_index in range(conv_weight.shape[0]):
        kept = (padded_seg[tap_index : tap_index + row_count] == local_seg).astype(jnp.float32)
        summed = (
            summed
            + conv_weight[tap_index][None, :]
            * padded[tap_index : tap_index + row_count]
            * kept[:, None]
        )
    return jax.nn.silu(summed)


def ssd_span(ssd_state, span_data):
    values, state_b, state_c, step_sizes, decay_rates, seg_block, prev_seg = span_data
    length = seg_block.shape[0]
    cumulative = jnp.cumsum(decay_rates, axis=0)
    causal = jnp.arange(length)[:, None] >= jnp.arange(length)[None, :]
    allowed = ((seg_block[:, None] == seg_block[None, :]) & causal).astype(jnp.float32)[:, :, None]
    spread = cumulative[:, None, :] - cumulative[None, :, :]
    decay_pairs = jnp.exp(jnp.where(allowed > 0, spread, 0.0)) * allowed
    intersection = jnp.dot(
        state_c, state_b.T, precision=highest, preferred_element_type=jnp.float32
    )
    mixing = intersection[:, :, None] * decay_pairs * step_sizes[None, :, :]
    within = jnp.einsum("tsh,shp->thp", mixing, values, precision=highest)
    entering = jnp.exp(cumulative) * (seg_block == prev_seg).astype(jnp.float32)[:, None]
    carried = (
        jnp.einsum("tn,hpn->thp", state_c, ssd_state, precision=highest) * entering[:, :, None]
    )
    last_seg = seg_block[length - 1]
    tail_weight = (
        jnp.exp(cumulative[length - 1][None, :] - cumulative)
        * (seg_block == last_seg).astype(jnp.float32)[:, None]
        * step_sizes
    )
    fresh = jnp.einsum("shp,sn->hpn", tail_weight[:, :, None] * values, state_b, precision=highest)
    through = jnp.exp(cumulative[length - 1]) * (last_seg == prev_seg).astype(jnp.float32)
    return (ssd_state * through[:, None, None] + fresh, within + carried)


def local_ssd(inner_u, state_bc, step_raw, step_bias, decay_log, skip_scale, local_seg, span_prev):
    row_count, head_count = step_raw.shape
    head_size = inner_u.shape[1] // head_count
    state_width = state_bc.shape[1] // 2
    blocks = row_count // SPAN
    values = inner_u.reshape(row_count, head_count, head_size)
    step_sizes = jax.nn.softplus(step_raw + step_bias)
    decay_rates = -jnp.exp(decay_log) * step_sizes
    start_state = jnp.zeros((head_count, head_size, state_width), jnp.float32)
    inputs = (
        values.reshape(blocks, SPAN, head_count, head_size),
        state_bc[:, :state_width].reshape(blocks, SPAN, state_width),
        state_bc[:, state_width:].reshape(blocks, SPAN, state_width),
        step_sizes.reshape(blocks, SPAN, head_count),
        decay_rates.reshape(blocks, SPAN, head_count),
        local_seg.reshape(blocks, SPAN),
        span_prev,
    )
    end_state, outputs = lax.scan(ssd_span, start_state, inputs)
    outputs = outputs.reshape(row_count, head_count, head_size) + skip_scale[None, :, None] * values
    through = jnp.exp(jnp.sum(decay_rates, axis=0)) * (
        local_seg[row_count - 1] == span_prev[0]
    ).astype(jnp.float32)
    return (outputs.reshape(row_count, head_count * head_size), end_state, through)


def carry_in(state_bc, step_raw, step_bias, decay_log, entering, local_seg, prev_seg):
    row_count = step_raw.shape[0]
    state_width = state_bc.shape[1] // 2
    step_sizes = jax.nn.softplus(step_raw + step_bias)
    cumulative = jnp.cumsum(-jnp.exp(decay_log) * step_sizes, axis=0)
    opened = jnp.exp(cumulative) * (local_seg == prev_seg).astype(jnp.float32)[:, None]
    carried = (
        jnp.einsum("tn,hpn->thp", state_bc[:, state_width:], entering, precision=highest)
        * opened[:, :, None]
    )
    return carried.reshape(row_count, -1)


def combine(earlier, later):
    return (earlier[0] * later[0], later[1] + later[0][:, None, None] * earlier[1])


def per_device(
    tokens,
    segment_ids,
    first_gain,
    proj_zx,
    proj_bc,
    proj_step,
    conv_inner,
    conv_inner_bias,
    conv_state,
    conv_state_bias,
    step_bias,
    decay_log,
    skip_scale,
    gated_gain,
    proj_out,
    second_gain,
    proj_qkv,
    attention_out,
    cotangent,
):
    tok_rows = tokens.shape[0]
    inner_local = proj_zx.shape[2]
    att_local = proj_qkv.shape[2]
    att_heads = att_local // ATT_DIM
    score_scale = 1.0 / math.sqrt(ATT_DIM)
    reach_count = (DOC_MAX - 2) // tok_rows + 1
    row_start = lax.axis_index("seq") * tok_rows
    offsets = jnp.arange(tok_rows, dtype=jnp.int32)
    query_pos = row_start + offsets
    local_seg = lax.dynamic_slice_in_dim(segment_ids, row_start, tok_rows)
    padded_seg = jnp.concatenate([jnp.full((CONV - 1,), -1, jnp.int32), segment_ids])
    edge_seg = lax.dynamic_slice_in_dim(padded_seg, row_start, CONV - 1)
    prev_seg = edge_seg[CONV - 2]
    span_prev = jnp.concatenate([edge_seg[CONV - 2 :], local_seg[SPAN - 1 :: SPAN][:-1]])
    hidden_zero = tokens.astype(jnp.float32)
    total_zero = head_totals(jnp.sum(hidden_zero * hidden_zero, axis=1))
    first_norm, first_pull = jax.vjp(
        partial(shard_norm, full_width=D), hidden_zero, total_zero, first_gain
    )
    first_full = head_gather(first_norm.astype(jnp.bfloat16))
    zx_weight = proj_zx.reshape(D, 2 * inner_local)
    zx_proj = jnp.dot(first_full, zx_weight, preferred_element_type=jnp.float32)
    gate_z = zx_proj[:, :inner_local]
    bc_proj = jnp.dot(first_full, proj_bc, preferred_element_type=jnp.float32)
    step_raw = jnp.dot(first_full, proj_step, preferred_element_type=jnp.float32)
    conv_input = jnp.concatenate([zx_proj[:, inner_local:], bc_proj], axis=1)
    edge_start = tok_rows - (CONV - 1)
    edge_rows = from_behind(conv_input[edge_start:], "seq", 1)
    conv_weight = jnp.concatenate([conv_inner, conv_state], axis=1)
    conv_bias = jnp.concatenate([conv_inner_bias, conv_state_bias])
    conv_output, conv_pull = jax.vjp(
        partial(conv_piece, local_seg=local_seg, edge_seg=edge_seg),
        conv_input,
        edge_rows,
        conv_weight,
        conv_bias,
    )
    inner_u = conv_output[:, :inner_local]
    state_bc = conv_output[:, inner_local:]
    ssd_parts, ssd_pull = jax.vjp(
        partial(local_ssd, local_seg=local_seg, span_prev=span_prev),
        inner_u,
        state_bc,
        step_raw,
        step_bias,
        decay_log,
        skip_scale,
    )
    ssd_zero, end_state, through = ssd_parts
    identity = (jnp.ones_like(through), jnp.zeros_like(end_state))
    entering = entering_2((through, end_state), "seq", combine, identity)[1]
    carried, carry_pull = jax.vjp(
        partial(carry_in, local_seg=local_seg, prev_seg=prev_seg),
        state_bc,
        step_raw,
        step_bias,
        decay_log,
        entering,
    )
    mixed, gate_pull = jax.vjp(gate_piece, ssd_zero + carried, gate_z)
    total_gate = head_totals(jnp.sum(mixed * mixed, axis=1))
    gated, gated_pull = jax.vjp(
        partial(shard_norm, full_width=INNER), mixed, total_gate, gated_gain
    )
    gated_low = gated.astype(jnp.bfloat16)
    hidden_one = hidden_zero + head_scatter(
        jnp.dot(gated_low, proj_out, preferred_element_type=jnp.float32)
    )
    total_one = head_totals(jnp.sum(hidden_one * hidden_one, axis=1))
    second_norm, second_pull = jax.vjp(
        partial(shard_norm, full_width=D), hidden_one, total_one, second_gain
    )
    second_full = head_gather(second_norm.astype(jnp.bfloat16))
    qkv_weight = proj_qkv.reshape(D, 3 * att_local)
    projected = jnp.dot(second_full, qkv_weight, preferred_element_type=jnp.float32).astype(
        jnp.bfloat16
    )
    queries = projected[:, :att_local].reshape(tok_rows, att_heads, ATT_DIM)
    key_value = jnp.stack([projected[:, att_local : 2 * att_local], projected[:, 2 * att_local :]])[
        None
    ]
    moved_pieces = [key_value]
    for back_steps in range(1, reach_count + 1):
        moved_pieces.append(from_behind(key_value, "seq", back_steps))
    pair_pieces = jnp.concatenate(moved_pieces, axis=0)
    piece_first = row_start - jnp.arange(reach_count + 1, dtype=jnp.int32) * tok_rows
    key_pos = piece_first[:, None] + offsets[None, :]
    key_seg = jnp.where(
        key_pos >= 0, jnp.take(segment_ids, jnp.clip(key_pos, 0, segment_ids.shape[0] - 1)), -1
    )
    piece_inputs = (pair_pieces, key_seg, key_pos)

    def scores_of(pair_piece, seg_piece, pos_piece):
        key_heads = pair_piece[0].reshape(tok_rows, att_heads, ATT_DIM)
        scores = (
            jnp.einsum("qhd,khd->hqk", queries, key_heads, preferred_element_type=jnp.float32)
            * score_scale
        )
        allowed = (local_seg[:, None] == seg_piece[None, :]) & (
            pos_piece[None, :] <= query_pos[:, None]
        )
        return (scores, allowed[None], key_heads)

    def stats_step(running, piece_data):
        row_top, row_mass = running
        scores, allowed, unused = scores_of(*piece_data)
        masked = jnp.where(allowed, scores, masked_score)
        new_top = jnp.maximum(row_top, jnp.max(masked, axis=2))
        row_mass = row_mass * jnp.exp(row_top - new_top) + jnp.sum(
            jnp.where(allowed, jnp.exp(masked - new_top[:, :, None]), 0.0), axis=2
        )
        return ((new_top, row_mass), None)

    start_top = jnp.full((att_heads, tok_rows), masked_score, jnp.float32)
    (row_top, row_mass), unused = lax.scan(
        stats_step, (start_top, jnp.zeros_like(start_top)), piece_inputs
    )

    def probs_of(scores, allowed):
        return jnp.where(allowed, jnp.exp(scores - row_top[:, :, None]) / row_mass[:, :, None], 0.0)

    def output_step(accum, piece_data):
        scores, allowed, unused = scores_of(*piece_data)
        weights = probs_of(scores, allowed).astype(jnp.bfloat16)
        value_heads = piece_data[0][1].reshape(tok_rows, att_heads, ATT_DIM)
        return (
            accum
            + jnp.einsum("hqk,khd->qhd", weights, value_heads, preferred_element_type=jnp.float32),
            None,
        )

    attended, unused = lax.scan(
        output_step, jnp.zeros((tok_rows, att_heads, ATT_DIM), jnp.float32), piece_inputs
    )
    attended_low = attended.reshape(tok_rows, att_local).astype(jnp.bfloat16)
    output = hidden_one + head_scatter(
        jnp.dot(attended_low, attention_out, preferred_element_type=jnp.float32)
    )
    cot_full = head_gather(cotangent)
    grad_attention_out = jnp.einsum(
        "ti,td->id", attended_low, cot_full, preferred_element_type=jnp.float32
    )
    back_attended = jnp.einsum(
        "td,id->ti", cot_full, attention_out, preferred_element_type=jnp.float32
    ).astype(jnp.bfloat16)
    back_heads = back_attended.reshape(tok_rows, att_heads, ATT_DIM)
    row_delta = jnp.einsum("qhd,qhd->hq", back_heads.astype(jnp.float32), attended)

    def grad_step(back_query, piece_data):
        scores, allowed, key_heads = scores_of(*piece_data)
        value_heads = piece_data[0][1].reshape(tok_rows, att_heads, ATT_DIM)
        weights = probs_of(scores, allowed)
        back_weights = jnp.einsum(
            "qhd,khd->hqk", back_heads, value_heads, preferred_element_type=jnp.float32
        )
        back_scores = (weights * (back_weights - row_delta[:, :, None])).astype(jnp.bfloat16)
        back_query = (
            back_query
            + jnp.einsum("hqk,khd->qhd", back_scores, key_heads, preferred_element_type=jnp.float32)
            * score_scale
        )
        back_key = (
            jnp.einsum("hqk,qhd->khd", back_scores, queries, preferred_element_type=jnp.float32)
            * score_scale
        )
        back_value = jnp.einsum(
            "hqk,qhd->khd",
            weights.astype(jnp.bfloat16),
            back_heads,
            preferred_element_type=jnp.float32,
        )
        return (
            back_query,
            jnp.stack(
                [back_key.reshape(tok_rows, att_local), back_value.reshape(tok_rows, att_local)]
            ),
        )

    back_query, back_pieces = lax.scan(
        grad_step, jnp.zeros((tok_rows, att_heads, ATT_DIM), jnp.float32), piece_inputs
    )
    back_pair = back_pieces[0]
    for back_steps in range(1, reach_count + 1):
        back_pair = back_pair + from_behind(
            back_pieces[back_steps].astype(jnp.bfloat16), "seq", -back_steps
        ).astype(jnp.float32)
    back_projected = jnp.concatenate(
        [back_query.reshape(tok_rows, att_local), back_pair[0], back_pair[1]], axis=1
    ).astype(jnp.bfloat16)
    grad_proj_qkv = jnp.einsum(
        "td,tc->dc", second_full, back_projected, preferred_element_type=jnp.float32
    ).reshape(D, 3, att_local)
    back_second = head_scatter(
        jnp.einsum("tc,dc->td", back_projected, qkv_weight, preferred_element_type=jnp.float32)
    )
    back_hidden_norm, back_total_one, grad_second_gain = second_pull(back_second)
    back_hidden_one = (
        cotangent.astype(jnp.float32)
        + back_hidden_norm
        + 2.0 * hidden_one * head_totals(back_total_one)[:, None]
    )
    back_branch = head_gather(back_hidden_one.astype(jnp.bfloat16))
    grad_proj_out = jnp.einsum(
        "ti,td->id", gated_low, back_branch, preferred_element_type=jnp.float32
    )
    back_gated = jnp.einsum("td,id->ti", back_branch, proj_out, preferred_element_type=jnp.float32)
    back_mixed, back_total_gate, grad_gated_gain = gated_pull(back_gated)
    back_mixed = back_mixed + 2.0 * mixed * head_totals(back_total_gate)[:, None]
    back_ssd, back_gate_z = gate_pull(back_mixed)
    back_bc_carry, back_step_carry, back_bias_carry, back_decay_carry, back_entering = carry_pull(
        back_ssd
    )
    back_end = prefix((through, back_entering), "seq", combine, identity)[1]
    back_through = jnp.sum(back_end * entering, axis=(1, 2))
    (
        back_inner_u,
        back_bc_local,
        back_step_local,
        back_bias_local,
        back_decay_local,
        grad_skip_scale,
    ) = ssd_pull((back_ssd, back_end, back_through))
    back_conv_out = jnp.concatenate([back_inner_u, back_bc_local + back_bc_carry], axis=1)
    back_conv_in, back_edge, back_conv_weight, back_conv_bias = conv_pull(back_conv_out)
    edge_back = from_behind(back_edge, "seq", -1)
    back_conv_in = jnp.concatenate(
        [back_conv_in[:edge_start], back_conv_in[edge_start:] + edge_back], axis=0
    )
    back_zx = jnp.concatenate([back_gate_z, back_conv_in[:, :inner_local]], axis=1).astype(
        jnp.bfloat16
    )
    back_bc = back_conv_in[:, inner_local:].astype(jnp.bfloat16)
    back_step = (back_step_local + back_step_carry).astype(jnp.bfloat16)
    grad_proj_zx = jnp.einsum(
        "td,tc->dc", first_full, back_zx, preferred_element_type=jnp.float32
    ).reshape(D, 2, inner_local)
    grad_bc_part = jnp.einsum("td,tc->dc", first_full, back_bc, preferred_element_type=jnp.float32)
    grad_proj_step = jnp.einsum(
        "td,tc->dc", first_full, back_step, preferred_element_type=jnp.float32
    )
    back_first_part = (
        jnp.einsum("tc,dc->td", back_zx, zx_weight, preferred_element_type=jnp.float32)
        + jnp.einsum("tc,dc->td", back_bc, proj_bc, preferred_element_type=jnp.float32)
        + jnp.einsum("tc,dc->td", back_step, proj_step, preferred_element_type=jnp.float32)
    )
    back_first = head_scatter(back_first_part)
    back_hidden_first, back_total_zero, grad_first_gain = first_pull(back_first)
    grad_tokens = (
        back_hidden_one
        + back_hidden_first
        + 2.0 * hidden_zero * head_totals(back_total_zero)[:, None]
    ).astype(jnp.bfloat16)
    wide_sums = (
        lax.psum_scatter(
            grad_proj_zx.astype(jnp.bfloat16), "seq", scatter_dimension=0, tiled=True
        ).astype(jnp.float32),
        lax.psum_scatter(
            grad_proj_step.astype(jnp.bfloat16), "seq", scatter_dimension=0, tiled=True
        ).astype(jnp.float32),
        lax.psum_scatter(
            grad_proj_out.astype(jnp.bfloat16), "seq", scatter_dimension=1, tiled=True
        ).astype(jnp.float32),
        lax.psum_scatter(
            grad_proj_qkv.astype(jnp.bfloat16), "seq", scatter_dimension=0, tiled=True
        ).astype(jnp.float32),
        lax.psum_scatter(
            grad_attention_out.astype(jnp.bfloat16), "seq", scatter_dimension=1, tiled=True
        ).astype(jnp.float32),
    )
    shared_sums = (
        lax.psum_scatter(grad_bc_part, ("seq", "head"), scatter_dimension=1, tiled=True),
        lax.psum_scatter(
            back_conv_weight[:, inner_local:], ("seq", "head"), scatter_dimension=1, tiled=True
        ),
        lax.psum_scatter(
            back_conv_bias[inner_local:], ("seq", "head"), scatter_dimension=0, tiled=True
        ),
    )
    small_sums = lax.psum(
        (
            grad_first_gain,
            back_conv_weight[:, :inner_local],
            back_conv_bias[:inner_local],
            back_bias_local + back_bias_carry,
            back_decay_local + back_decay_carry,
            grad_skip_scale,
            grad_gated_gain,
            grad_second_gain,
        ),
        "seq",
    )
    return (
        output.astype(jnp.bfloat16),
        grad_tokens,
        small_sums[0],
        wide_sums[0],
        shared_sums[0],
        wide_sums[1],
        small_sums[1],
        small_sums[2],
        shared_sums[1],
        shared_sums[2],
        small_sums[3],
        small_sums[4],
        small_sums[5],
        small_sums[6],
        wide_sums[2],
        small_sums[7],
        wide_sums[3],
        wide_sums[4],
    )


def solution(mesh):
    placed = (
        P("seq", "head"),
        P(),
        P("head"),
        P(None, None, "head"),
        P(),
        P(None, "head"),
        P(None, "head"),
        P("head"),
        P(),
        P(),
        P("head"),
        P("head"),
        P("head"),
        P("head"),
        P("head", None),
        P("head"),
        P(None, None, "head"),
        P("head", None),
        P("seq", "head"),
    )
    return jax.shard_map(
        per_device,
        mesh=mesh,
        in_specs=placed,
        out_specs=(
            P("seq", "head"),
            P("seq", "head"),
            P("head"),
            P("seq", None, "head"),
            P(None, ("seq", "head")),
            P("seq", "head"),
            P(None, "head"),
            P("head"),
            P(None, ("seq", "head")),
            P(("seq", "head")),
            P("head"),
            P("head"),
            P("head"),
            P("head"),
            P("head", "seq"),
            P("head"),
            P("seq", None, "head"),
            P("head", "seq"),
        ),
        check_vma=False,
    )
```

profile of v0, /device:TPU:0, one launch (start us, length us, event | category | flops | bytes accessed | tf_op | source)
XLA Modules:
  0.0 2029.9 jit_solution(6232779370404908400)
XLA Ops:
  30.0 19.0 all-gather.10.cloned.1.call-done
  96.0 236.7 %while.152 = (s32[]{:T(128)}, f32[12,64,128]{2,1,0:T(8,128)S(1)}, f32[4,256,12,64]{1,0,3,2:T(4,128)}, pred[4,256,256,12]{2,1,3,0:T(32,128)(4,1)}, f32[4,256,256,...) while((s32[]{:T(128)}, f32[12,64,128]{2,1,0:T(8,128)S(1)}, ...), condition=%wide.region_5.7_spmd.clone.clone, body=%wide.region_2.6_spmd.clone.clone.sunk | while | flops 1318768640 | bytes 28506800 | solution.py:155
  120.1 17.9 dynamic_update_slice.291
  179.2 17.9 dynamic_update_slice.291
  238.3 17.9 dynamic_update_slice.291
  297.5 17.9 dynamic_update_slice.291
  344.3 21.2 %all-reduce.14 = bf16[96]{0:T(256)(128)(2,1)S(1)} all-reduce(bf16[96]{0:T(256)(128)(2,1)S(1)} %dynamic-update-slice), channel_id=3, replica_groups=mesh['seq'=8,'head'=4] {'seq'}, use_global_device_ids=true, to_apply=%add.14 | all-reduce | flops 96 | bytes 384
  407.1 64.3 %reduce-scatter.13.cloned.1.call-done = f32[1024,384]{1,0:T(8,128)} async-done(((f32[1024,1536]{1,0:T(8,128)}), f32[1024,384]{1,0:T(8,128)}) %reduce-scatter.13.cloned.1.call-update) | async-done | bytes 1572880 | tf_op jit(solution)/shard_map/reduce_scatter | solution.py:82
  489.2 22.5 %all-gather.12.cloned.1.call-done = bf16[1024,1536]{1,0:T(8,128)(2,1)} async-done(((bf16[1024,384]{1,0:T(8,128)(2,1)}), bf16[1024,1536]{1,0:T(8,128)(2,1)}) %all-gather.12.cloned.1.call-update) | async-done | bytes 3145744 | tf_op jit(solution)/shard_map/all_gather | solution.py:78
  529.7 17.6 gather_fusion
  574.3 76.4 %while.149 = (s32[]{:T(128)}, f32[6,1024]{1,0:T(8,128)S(1)}, f32[6,1024]{1,0:T(8,128)S(1)}, s32[1024]{0:T(1024)S(1)}, s32[3,1024]{1,0:T(4,128)}, /*index=5*/s32[...) while((s32[]{:T(128)}, f32[6,1024]{1,0:T(8,128)S(1)}, ...), condition=%wide.region_19.21_spmd.clone, body=%wide.region_16.20_spmd.clone.sunk | while | flops 858815488 | bytes 60125348 | solution.py:315
  577.5 10.5 fusion.350
  588.1 11.6 select_reduce_fusion.2
  603.0 10.5 fusion.350
  613.5 11.6 select_reduce_fusion.2
  628.5 10.5 fusion.350
  639.0 11.6 select_reduce_fusion.2
  650.7 49.4 %while.150 = (s32[]{:T(128)}, f32[1024,6,64]{0,2,1:T(8,128)}, bf16[3,2,1024,384]{2,3,1,0:T(8,128)(2,1)}, s32[1024]{0:T(1024)S(1)}, s32[3,1024]{1,0:T(4,128)}, /*...) while((s32[]{:T(128)}, f32[1024,6,64]{0,2,1:T(8,128)}, ...), condition=%wide.region_21.23_spmd.clone, body=%wide.region_20.22_spmd.clone.sunk | while | flops 1646003200 | bytes 13979847 | solution.py:332
  656.4 10.7 bitcast_add_fusion.8
  672.4 11.2 bitcast_add_fusion.8
  689.0 11.2 bitcast_add_fusion.8
  702.0 196.8 %while.151 = (s32[]{:T(128)}, f32[1024,6,64]{0,2,1:T(8,128)}, f32[3,2,1024,384]{2,3,1,0:T(8,128)}, bf16[3,2,1024,384]{2,3,1,0:T(8,128)(2,1)}, s32[1024]{0:T(1024...) while((s32[]{:T(128)}, f32[1024,6,64]{0,2,1:T(8,128)}, ...), condition=%wide.region_24.26_spmd.clone, body=%wide.region_23.25_spmd.clone.sunk | while | flops 4082369536 | bytes 146125072 | solution.py:379
  706.9 11.9 bitcast_select_fusion.4
  718.7 15.4 fusion.366
  742.6 11.4 fusion.367
  771.9 11.9 bitcast_select_fusion.4
  783.8 15.4 fusion.366
  808.0 11.4 fusion.367
  837.4 11.9 bitcast_select_fusion.4
  849.3 15.4 fusion.366
  873.5 11.4 fusion.367
  906.5 67.3 %collective-permute-done.4 = bf16[2,1024,384]{1,2,0:T(8,128)(2,1)S(1)} collective-permute-done((bf16[2,1024,384]{1,2,0:T(8,128)(2,1)S(1)}, bf16[2,1024,384]{1,2,0:T(8,128)(2,1)S(1)}, u32[]{:S(2)}, u32[]{:S(2)}) %collective-permute-start.4) | collective-permute-done | bytes 1572896 | tf_op jit(solution)/shard_map/ppermute | solution.py:25
  984.3 89.7 %reduce-scatter.17.cloned.1.call-done = f32[1024,384]{1,0:T(8,128)} async-done(((f32[1024,1536]{1,0:T(8,128)}), f32[1024,384]{1,0:T(8,128)}) %reduce-scatter.17.cloned.1.call-update) | async-done | bytes 1572880 | tf_op jit(solution)/shard_map/reduce_scatter | solution.py:82
  1086.6 29.2 %all-gather.16.cloned.1.call-done = bf16[1024,1536]{1,0:T(8,128)(2,1)} async-done(((bf16[1024,384]{1,0:T(8,128)(2,1)}), bf16[1024,1536]{1,0:T(8,128)(2,1)}) %all-gather.16.cloned.1.call-update) | async-done | bytes 3145744 | tf_op jit(solution)/shard_map/all_gather | solution.py:78
  1178.4 14.9 reduce-window.58
  1201.3 12.4 while.147
  1219.0 268.4 %while.148 = (s32[]{:T(128)}, f32[12,64,128]{2,1,0:T(8,128)S(1)}, f32[4,256,12,64]{1,0,3,2:T(4,128)}, f32[4,256,128]{2,1,0:T(8,128)}, f32[4,256,128]{2,1,0:T(8,1...) while((s32[]{:T(128)}, f32[12,64,128]{2,1,0:T(8,128)S(1)}, ...), condition=%wide.region_43.45_spmd, body=%wide.region_32.44_spmd.sunk | while | flops 2628286464 | bytes 35172296 | solution.py:155
  1238.4 17.9 dynamic_update_slice.273
  1305.5 17.9 dynamic_update_slice.273
  1372.6 17.9 dynamic_update_slice.273
  1439.5 17.9 dynamic_update_slice.273
  1548.1 12.5 copy.251
  1591.6 40.7 %all-reduce.18 = (f32[4,256]{1,0:T(4,128)S(1)}, f32[256]{0:T(256)S(1)}) all-reduce(f32[4,256]{1,0:T(4,128)S(1)} %pad_add_fusion.4, f32[256]{0:T(256)S(1)} %slice.237), channel_id=12, replica_groups=mesh['seq'=8,'head'=4] {'seq','head'}, use_global_device_ids=true, to_apply=%region_63.65.clone | all-reduce | flops 1280 | bytes 10240
  1637.0 162.8 %all-reduce.22.cloned.1.call-done = bf16[1536,2,768]{2,1,0:T(2,128)(2,1)} async-done(((bf16[1536,2,768]{2,1,0:T(2,128)(2,1)}), bf16[1536,2,768]{2,1,0:T(2,128)(2,1)}) %all-reduce.22.cloned.1.call-update) | async-done | bytes 4718608
  1802.3 56.8 %reduce-scatter.19.cloned.1.call-done = f32[1024,384]{1,0:T(8,128)} async-done(((f32[1024,1536]{1,0:T(8,128)}), f32[1024,384]{1,0:T(8,128)}) %reduce-scatter.19.cloned.1.call-update) | async-done | bytes 1572880 | tf_op jit(solution)/shard_map/reduce_scatter | solution.py:82
  1861.2 37.7 %all-reduce.19 = (f32[384]{0:T(512)}, f32[4,768]{1,0:T(4,128)}, f32[768]{0:T(1024)}, f32[12]{0:T(128)}, f32[12]{0:T(128)}, /*index=5*/f32[12]{0:T(128)}, f32[768]{0:T(1024)}, f32[384]{0:T(512)}) all-reduce(f32[384]{0:T(512)S(1)} %get-tuple-element.2099, f32[4,768]{1,0:T(4,128)S(1)} %slice.287, ...), channel_id=1, replica_groups=mesh['seq'=8,'head'=4] {'seq'}, use_global_device_ids=true, to_apply=%region_52.54 | all-reduce | flops 5412 | bytes 43296 | tf_op jit(solution)/shard_map/psum | solution.py:479
  1905.4 14.2 reduce-scatter.15.cloned.1.call-done
  1924.0 99.2 %reduce-scatter.21.cloned.1.call-done = f32[1536,8]{0,1:T(8,128)} async-done(((f32[1536,256]{0,1:T(8,128)}), f32[1536,8]{0,1:T(8,128)}) %reduce-scatter.21.cloned.1.call-update) | async-done | bytes 49168 | tf_op jit(solution)/shard_map/reduce_scatter | solution.py:471
  (912 shorter events, 875.4 us)
Async XLA Ops:
  7.2 393.2 %copy-start = (bf16[768,1536]{1,0:T(8,128)(2,1)S(1)}, bf16[768,1536]{1,0:T(8,128)(2,1)}, u32[]{:S(2)}) copy-start(bf16[768,1536]{1,0:T(8,128)(2,1)} %param.48) | copy-start | bytes 7077892
  7.2 41.8 %all-gather.10.cloned.1.call-start = ((), (), s32[]{:S(2)}) async-start(), calls=%async_computation.9 | async-start | bytes 3932160 | tf_op jit(solution)/shard_map/all_gather | solution.py:78
  20.0 357.4 %all-gather.18.cloned.1.call-start = ((), (), s32[]{:S(2)}) async-start(), calls=%async_computation.21 | async-start | bytes 1769472 | tf_op jit(solution)/shard_map/all_gather | solution.py:31
  29.9 41.9 %copy-start.67 = (f32[1024]{0:T(1024)}, f32[1024]{0:T(1024)S(1)}, u32[]{:S(2)}) copy-start(f32[1024]{0:T(1024)S(1)} %get-tuple-element.2420) | copy-start | bytes 12292
  29.9 41.9 %copy-start.69 = (f32[1024]{0:T(1024)}, f32[1024]{0:T(1024)S(1)}, u32[]{:S(2)}) copy-start(f32[1024]{0:T(1024)S(1)} %get-tuple-element.2421) | copy-start | bytes 12292
  29.9 41.9 %copy-start.71 = (f32[1024]{0:T(1024)}, f32[1024]{0:T(1024)S(1)}, u32[]{:S(2)}) copy-start(f32[1024]{0:T(1024)S(1)} %get-tuple-element.2422) | copy-start | bytes 12292
  29.9 41.9 %copy-start.73 = (f32[1,1024]{1,0:T(1,128)}, f32[1,1024]{1,0:T(1,128)S(1)}, u32[]{:S(2)}) copy-start(f32[1,1024]{1,0:T(1,128)S(1)} %get-tuple-element.2416) | copy-start | bytes 12292
  29.9 41.9 %copy-start.75 = (f32[1,1024]{1,0:T(1,128)}, f32[1,1024]{1,0:T(1,128)S(1)}, u32[]{:S(2)}) copy-start(f32[1,1024]{1,0:T(1,128)S(1)} %get-tuple-element.2417) | copy-start | bytes 12292
  29.9 41.9 %copy-start.77 = (f32[1,1024]{1,0:T(1,128)}, f32[1,1024]{1,0:T(1,128)S(1)}, u32[]{:S(2)}) copy-start(f32[1,1024]{1,0:T(1,128)S(1)} %get-tuple-element.2418) | copy-start | bytes 12292
  30.0 41.9 %copy-start.79 = (f32[1,1024]{1,0:T(1,128)}, f32[1,1024]{1,0:T(1,128)S(1)}, u32[]{:S(2)}) copy-start(f32[1,1024]{1,0:T(1,128)S(1)} %get-tuple-element.2419) | copy-start | bytes 12292
  62.9 5.8 collective-permute-start
  333.4 138.0 %reduce-scatter.13.cloned.1.call-start = ((), (), s32[]{:S(2)}) async-start(), calls=%async_computation.10 | async-start | bytes 7864320 | tf_op jit(solution)/shard_map/reduce_scatter | solution.py:82
  336.1 50.8 %copy-start.90 = (f32[768]{0:T(1024)}, f32[768]{0:T(1024)S(1)}, u32[]{:S(2)}) copy-start(f32[768]{0:T(1024)S(1)} %mul.1122) | copy-start | bytes 9220
  407.0 64.4 %copy-start.21 = (bf16[1024,384]{1,0:T(8,128)(2,1)S(1)}, bf16[1024,384]{1,0:T(8,128)(2,1)}, u32[]{:S(2)}) copy-start(bf16[1024,384]{1,0:T(8,128)(2,1)} %param.34) | copy-start | bytes 2359300
  407.0 72.9 %copy-start.92 = (f32[384]{0:T(512)S(1)}, f32[384]{0:T(512)}, u32[]{:S(2)}) copy-start(f32[384]{0:T(512)} %param.49) | copy-start | bytes 4612
  407.0 104.6 %all-gather.12.cloned.1.call-start = ((), (), s32[]{:S(2)}) async-start(), calls=%async_computation.11 | async-start | bytes 3932160 | tf_op jit(solution)/shard_map/all_gather | solution.py:78
  482.4 65.6 %all-gather.14.cloned.1.call-start = ((), (), s32[]{:S(2)}) async-start(), calls=%async_computation.13 | async-start | bytes 3932160 | tf_op jit(solution)/shard_map/all_gather | solution.py:78
  483.0 591.0 %reduce-scatter.17.cloned.1.call-start = ((), (), s32[]{:S(2)}) async-start(), calls=%async_computation.14 | async-start | bytes 7864320 | tf_op jit(solution)/shard_map/reduce_scatter | solution.py:82
  520.5 37.7 %collective-permute-start.2 = (bf16[1,2,1024,384]{3,2,1,0:T(8,128)(2,1)}, bf16[1,2,1024,384]{3,2,1,0:T(8,128)(2,1)}, u32[]{:S(2)}, u32[]{:S(2)}) collective-permute-start(bf16[1,2,1024,384]{3,2,1,0:T(8,128)(2,1)} %maximum_bitcast_fusion.1), channel_id=1, source_target_pairs={{0,8},{4,12},{8,16},{12,20},{16,24},{20,28},{1,9},{5,13},{9,17},{1... | collective-permute-start | bytes 4718600 | tf_op jit(solution)/shard_map/ppermute | solution.py:25
  525.0 37.4 %collective-permute-start.1 = (bf16[1,2,1024,384]{3,2,1,0:T(8,128)(2,1)}, bf16[1,2,1024,384]{3,2,1,0:T(8,128)(2,1)}, u32[]{:S(2)}, u32[]{:S(2)}) collective-permute-start(bf16[1,2,1024,384]{3,2,1,0:T(8,128)(2,1)} %maximum_bitcast_fusion.1), channel_id=1, source_target_pairs={{0,4},{4,8},{8,12},{12,16},{16,20},{20,24},{24,28},{1,5},{5,9},{9,... | collective-permute-start | bytes 4718600 | tf_op jit(solution)/shard_map/ppermute | solution.py:25
  903.6 70.1 %collective-permute-start.4 = (bf16[2,1024,384]{1,2,0:T(8,128)(2,1)S(1)}, bf16[2,1024,384]{1,2,0:T(8,128)(2,1)S(1)}, u32[]{:S(2)}, u32[]{:S(2)}) collective-permute-start(bf16[2,1024,384]{1,2,0:T(8,128)(2,1)S(1)} %get-tuple-element.2397), channel_id=1, source_target_pairs={{8,0},{12,4},{16,8},{20,12},{24,16},{28,20},{9,1},{13,5},{17,9},{2... | collective-permute-start | bytes 4718600 | tf_op jit(solution)/shard_map/ppermute | solution.py:25
  905.1 68.7 %collective-permute-start.3 = (bf16[2,1024,384]{1,2,0:T(8,128)(2,1)S(1)}, bf16[2,1024,384]{1,2,0:T(8,128)(2,1)S(1)}, u32[]{:S(2)}, u32[]{:S(2)}) collective-permute-start(bf16[2,1024,384]{1,2,0:T(8,128)(2,1)S(1)} %get-tuple-element.2396), channel_id=1, source_target_pairs={{4,0},{8,4},{12,8},{16,12},{20,16},{24,20},{28,24},{5,1},{9,5},{13... | collective-permute-start | bytes 4718600 | tf_op jit(solution)/shard_map/ppermute | solution.py:25
  906.5 70.3 %copy-start.50 = (bf16[1024,6,64]{0,2,1:T(8,128)(2,1)}, bf16[1024,6,64]{0,2,1:T(8,128)(2,1)S(1)}, u32[]{:S(2)}) copy-start(bf16[1024,6,64]{0,2,1:T(8,128)(2,1)S(1)} %convert.30) | copy-start | bytes 2359300
  984.2 89.8 %copy-start.63 = (f32[1024]{0:T(1024)S(1)}, f32[1024]{0:T(1024)}, u32[]{:S(2)}) copy-start(f32[1024]{0:T(1024)} %copy-done.62) | copy-start | bytes 12292
  984.2 89.8 %copy-start.93 = (f32[384]{0:T(512)S(1)}, f32[384]{0:T(512)}, u32[]{:S(2)}) copy-start(f32[384]{0:T(512)} %param.49) | copy-start | bytes 4612
  984.2 92.7 %copy-start.87 = (f32[1024]{0:T(1024)S(1)}, f32[1024]{0:T(1024)}, u32[]{:S(2)}) copy-start(f32[1024]{0:T(1024)} %copy-done.86) | copy-start | bytes 12292
  984.3 99.1 %copy-start.30 = (bf16[1024,384]{1,0:T(8,128)(2,1)S(1)}, bf16[1024,384]{1,0:T(8,128)(2,1)}, u32[]{:S(2)}) copy-start(bf16[1024,384]{1,0:T(8,128)(2,1)} %param.52) | copy-start | bytes 2359300
  984.3 131.6 %all-gather.16.cloned.1.call-start = ((), (), s32[]{:S(2)}) async-start(), calls=%async_computation.15 | async-start | bytes 3932160 | tf_op jit(solution)/shard_map/all_gather | solution.py:78
  1086.6 114.7 %all-gather.20.cloned.1.call-start = ((), (), s32[]{:S(2)}) async-start(), calls=%async_computation.22 | async-start | bytes 1769472 | tf_op jit(solution)/shard_map/all_gather | solution.py:53
  1147.5 440.1 %reduce-scatter.27.cloned.1.call-start = ((), (), s32[]{:S(2)}) async-start(), calls=%async_computation.20 | async-start | bytes 1327104 | tf_op jit(solution)/shard_map/reduce_scatter | solution.py:466
  1155.2 434.1 %reduce-scatter.25.cloned.1.call-start = ((), (), s32[]{:S(2)}) async-start(), calls=%async_computation.19 | async-start | bytes 3981312 | tf_op jit(solution)/shard_map/reduce_scatter | solution.py:463
  1169.5 464.1 %reduce-scatter.29.cloned.1.call-start = ((), (), s32[]{:S(2)}) async-start(), calls=%async_computation.23 | async-start | bytes 442368
  1495.7 139.4 %reduce-scatter.23.cloned.1.call-start = ((), (), s32[]{:S(2)}) async-start(), calls=%async_computation.18 | async-start | bytes 2654208 | tf_op jit(solution)/shard_map/reduce_scatter | solution.py:460
  1502.7 297.1 %all-reduce.22.cloned.1.call-start = ((), (), s32[]{:S(2)}) async-start(), calls=%async_computation.24 | async-start | bytes 9437184
  1527.2 8.0 collective-permute-start.5
  1560.6 298.5 %reduce-scatter.19.cloned.1.call-start = ((), (), s32[]{:S(2)}) async-start(), calls=%async_computation.16 | async-start | bytes 7864320 | tf_op jit(solution)/shard_map/reduce_scatter | solution.py:82
  1574.9 344.6 %reduce-scatter.15.cloned.1.call-start = ((), (), s32[]{:S(2)}) async-start(), calls=%async_computation.12 | async-start | bytes 7864320 | tf_op jit(solution)/shard_map/reduce_scatter | solution.py:82
  1581.8 441.3 %reduce-scatter.21.cloned.1.call-start = ((), (), s32[]{:S(2)}) async-start(), calls=%async_computation.17 | async-start | bytes 1622016 | tf_op jit(solution)/shard_map/reduce_scatter | solution.py:471
  1586.9 46.7 %copy-start.111 = (f32[12]{0:T(128)S(1)}, f32[12]{0:T(128)}, u32[]{:S(2)}) copy-start(f32[12]{0:T(128)} %param.45) | copy-start | bytes 148
  1586.9 272.2 %copy-start.22 = (bf16[1024,384]{1,0:T(8,128)(2,1)S(1)}, bf16[1024,384]{1,0:T(8,128)(2,1)}, u32[]{:S(2)}) copy-start(bf16[1024,384]{1,0:T(8,128)(2,1)} %param.34) | copy-start | bytes 2359300
  1586.9 272.2 %copy-start.66 = (f32[1024]{0:T(1024)S(1)}, f32[1024]{0:T(1024)}, u32[]{:S(2)}) copy-start(f32[1024]{0:T(1024)} %copy-done.65) | copy-start | bytes 12292
  1586.9 272.2 %copy-start.95 = (f32[384]{0:T(512)S(1)}, f32[384]{0:T(512)}, u32[]{:S(2)}) copy-start(f32[384]{0:T(512)} %param.36) | copy-start | bytes 4612
  1589.3 271.8 %copy-start.100 = (f32[384]{0:T(512)S(1)}, f32[384]{0:T(512)}, u32[]{:S(2)}) copy-start(f32[384]{0:T(512)} %get-tuple-element.2097) | copy-start | bytes 4612
  1589.3 271.8 %copy-start.104 = (f32[768]{0:T(1024)S(1)}, f32[768]{0:T(1024)}, u32[]{:S(2)}) copy-start(f32[768]{0:T(1024)} %get-tuple-element.2093) | copy-start | bytes 9220
  1589.3 309.5 %copy-start.83 = (f32[1024]{0:T(1024)S(1)}, f32[1024]{0:T(1024)}, u32[]{:S(2)}) copy-start(f32[1024]{0:T(1024)} %copy-done.82) | copy-start | bytes 12292
  1589.3 330.2 %copy-start.64 = (f32[1024]{0:T(1024)S(1)}, f32[1024]{0:T(1024)}, u32[]{:S(2)}) copy-start(f32[1024]{0:T(1024)} %copy-done.62) | copy-start | bytes 12292
  1589.3 330.2 %copy-start.89 = (f32[1024]{0:T(1024)S(1)}, f32[1024]{0:T(1024)}, u32[]{:S(2)}) copy-start(f32[1024]{0:T(1024)} %copy-done.88) | copy-start | bytes 12292
  1589.3 330.2 %copy-start.94 = (f32[384]{0:T(512)S(1)}, f32[384]{0:T(512)}, u32[]{:S(2)}) copy-start(f32[384]{0:T(512)} %param.49) | copy-start | bytes 4612
  (116 other events, 841.1 us)
Sparse Core Ops, SparseCore 0:
  20.2 28.7 all-gather.9
  333.5 43.9 all-gather.17
  407.1 64.2 reduce-scatter.12
  482.5 29.0 all-gather.11
  513.1 28.4 all-gather.13
  984.4 89.5 reduce-scatter.16
  1086.7 29.1 all-gather.15
  1147.7 45.2 all-gather.19
  1196.9 63.2 reduce-scatter.26
  1263.6 78.4 reduce-scatter.24
  1495.8 59.4 reduce-scatter.28
  1558.7 68.8 reduce-scatter.22
  1631.1 168.6 all-reduce.21
  1802.2 56.8 reduce-scatter.18
  1861.5 58.0 reduce-scatter.14
  1925.2 97.8 reduce-scatter.20
where the time goes:
time: 2050 us; the launch traced here: 2030 us
  waiting for transfers between devices  638 us (31%)
  matrix products  501 us (24%)
  local copies, waits for them, and re-layouts  411 us (20%)
  other arithmetic  299 us (15%)
  blocking collectives  137 us (7%)
    reduce_scatter x4, waiting for transfers between devices, head_scatter(): return lax.psum_scatter(values, 'head', scatter_dimension=1, tiled=True)  225 us
    dynamic_update_slice x56, local copies, waits for them, and re-layouts, local_ssd(): end_state, outputs = lax.scan(ssd_span, start_state, inputs)  198 us
    unnamed x18, waiting for transfers between devices  164 us
    reduce_scatter x1, waiting for transfers between devices, per_device(): lax.psum_scatter(grad_bc_part, ('seq', 'head'), scatter_dimension=1, tile...  99.2 us
    ppermute x6, waiting for transfers between devices, from_behind(): return lax.ppermute(value, axis, pairs)  76.1 us
    all_gather x4, waiting for transfers between devices, head_gather(): return lax.all_gather(values, 'head', axis=1, tiled=True)  70.7 us
    dot_general x12, matrix products, ssd_span(): within = jnp.einsum('tsh,shp->thp', mixing, values, precision=highest)  67.9 us
    dot_general x6, matrix products, scores_of(): jnp.einsum('qhd,khd->hqk', queries, key_heads, preferred_element_type=jnp...  67.2 us
  transfers between devices with their start and end apart: 22, of which 13 were waited for; matrix products, arithmetic and copies ran while one was open for 25% of the time, Pallas kernels for 0%

commit v1 on v0

v1 whole, which is shorter than its diff:
```python
from functools import partial
import math

import jax
import jax.numpy as jnp
from jax import lax
from jax.experimental import pallas as pl
from jax.experimental.pallas import tpu as pltpu
from jax.sharding import PartitionSpec as P

D = 1536
ATT_DIM = 64
SSM_DIM = 64
SPAN = 256
CONV = 4
DOC_MAX = 2000
INNER = 3072
LANES = 128

epsilon = 1e-05
highest = lax.Precision.HIGHEST
f32 = jnp.float32
bf16 = jnp.bfloat16
masked_score = -1e30
VMEM_LIMIT = 60 * 1024 * 1024


def dot_nn(a, b, precision=None):
    return lax.dot_general(a, b, (((1,), (0,)), ((), ())), precision=precision, preferred_element_type=f32)


def dot_nt(a, b, precision=None):
    return lax.dot_general(a, b, (((1,), (1,)), ((), ())), precision=precision, preferred_element_type=f32)


def dot_tn(a, b, precision=None):
    return lax.dot_general(a, b, (((0,), (0,)), ((), ())), precision=precision, preferred_element_type=f32)


def softplus(x):
    return jnp.maximum(x, 0.0) + jnp.log1p(jnp.exp(-jnp.abs(x)))


def sigmoid(x):
    return 1.0 / (1.0 + jnp.exp(-x))


def lane_low(rows):
    return lax.broadcasted_iota(jnp.int32, (rows, LANES), 1) < SSM_DIM


def conv_rows(buf, weight, bias, kept, rows):
    summed = bias + weight[3:4, :] * buf[8 : 8 + rows, :]
    for tap in range(3):
        summed = summed + weight[tap : tap + 1, :] * (buf[5 + tap : 5 + tap + rows, :] * kept[:, tap : tap + 1])
    return summed


def fill_conv(buf, chunk, x_ref, xprev_ref, bcs_ref, bprev_ref, edge_ref, inner, rows):
    buf[8 : 8 + rows, :inner] = x_ref[...]
    buf[8 : 8 + rows, inner:] = bcs_ref[:, : buf.shape[1] - inner]

    @pl.when(chunk == 0)
    def _():
        buf[0:8, :] = edge_ref[...]

    @pl.when(chunk > 0)
    def _():
        buf[0:8, :inner] = xprev_ref[...]
        buf[0:8, inner:] = bprev_ref[:, : buf.shape[1] - inner]


def span_terms(bcs_ref, bc_width, bias_ref, rate_ref, segc_ref, segr_ref, prev, last, rows):
    raw = bcs_ref[:, bc_width:] + bias_ref[...]
    step = softplus(raw)
    decay = rate_ref[...] * step
    row = lax.broadcasted_iota(jnp.int32, (rows, rows), 0)
    col = lax.broadcasted_iota(jnp.int32, (rows, rows), 1)
    causal = row >= col
    tri = causal.astype(f32)
    cum = dot_nn(tri, decay, highest)
    segc = segc_ref[...]
    allowed = (segc == segr_ref[...]) & causal
    opened = (segc == prev).astype(f32)
    closing = (segc == last).astype(f32)
    last_cum = cum[rows - 1 : rows, :]
    enter = jnp.exp(cum) * opened
    tail = jnp.exp(last_cum - cum) * closing
    through = jnp.exp(last_cum) * (last == prev).astype(f32)
    return raw, step, decay, cum, tri, allowed, enter, tail, last_cum, through


def ssd_forward_kernel(
    prev_ref, last_ref, x_ref, xprev_ref, bcs_ref, bprev_ref, edge_ref, kept_ref, segc_ref, segr_ref,
    weight_ref, cbias_ref, bias_ref, rate_ref, skip_ref, wide_ref, tall_ref,
    y_ref, c_ref, open_ref, states_ref, end_ref, through_ref,
    state, base, buf,
):
    chunk = pl.program_id(0)
    rows = x_ref.shape[0]
    inner = x_ref.shape[1]
    width = c_ref.shape[1]
    heads = inner // SSM_DIM

    @pl.when(chunk == 0)
    def _():
        state[...] = jnp.zeros_like(state)
        base[...] = jnp.zeros_like(base)

    fill_conv(buf, chunk, x_ref, xprev_ref, bcs_ref, bprev_ref, edge_ref, inner, rows)
    pre = conv_rows(buf, weight_ref[...], cbias_ref[...], kept_ref[...], rows)
    conv = pre * sigmoid(pre)
    values = conv[:, :inner]
    b_low = conv[:, inner : inner + width].astype(bf16)
    c_low = conv[:, inner + width :].astype(bf16)
    prev, last, prev_dev = prev_ref[chunk], last_ref[chunk], prev_ref[0]
    raw, step, decay, cum, tri, allowed, enter, tail, last_cum, through = span_terms(
        bcs_ref, 2 * width, bias_ref, rate_ref, segc_ref, segr_ref, prev, last, rows
    )
    cum_t = cum.T
    inter = jnp.where(allowed, dot_nt(c_low, b_low), 0.0)
    wide = wide_ref[...]
    scaled = values * dot_nn(step, wide, highest)
    scaled_low = scaled.astype(bf16)
    old = state[...]
    old_low = old.astype(bf16)
    states_ref[...] = old_low
    c_ref[...] = c_low
    carried = dot_nt(c_low, old_low) * dot_nn(enter, wide, highest) + skip_ref[...] * values
    low = lane_low(rows)
    for pair in range(heads // 2):
        cols = slice(pair * LANES, (pair + 1) * LANES)
        both = []
        for head in (2 * pair, 2 * pair + 1):
            spread = jnp.exp(jnp.minimum(cum[:, head : head + 1] - cum_t[head : head + 1, :], 0.0))
            both.append(dot_nn((inter * spread).astype(bf16), scaled_low[:, cols]))
        y_ref[:, cols] = jnp.where(low, both[0], both[1]) + carried[:, cols]
    fresh = dot_tn((scaled * dot_nn(tail, wide, highest)).astype(bf16), b_low)
    through_rows = jnp.broadcast_to(through, (8, LANES))
    column = dot_nt(tall_ref[...], through_rows, highest)[:, 0:1]
    new = old * column + fresh
    state[...] = new
    end_ref[...] = new
    total = base[0:1, :]
    open_ref[...] = jnp.exp(total + cum) * (segc_ref[...] == prev_dev).astype(f32)
    base[...] = jnp.broadcast_to(total + last_cum, base.shape)
    through_ref[...] = jnp.broadcast_to(
        jnp.exp(total + last_cum) * (last == prev_dev).astype(f32), through_ref.shape
    )


def gate_forward_kernel(y_ref, c_ref, open_ref, enter_ref, z_ref, gain_ref, wide_ref, ssd_ref, out_ref, sum_ref):
    ssd = y_ref[...] + dot_nt(c_ref[...], enter_ref[...]) * dot_nn(open_ref[...], wide_ref[...], highest)
    z = z_ref[...]
    mixed = ssd * (z * sigmoid(z))
    ssd_ref[...] = ssd
    out_ref[...] = (mixed * gain_ref[...]).astype(bf16)
    sum_ref[...] = dot_nt(jnp.ones((8, mixed.shape[1]), f32), mixed * mixed, highest)


def gate_backward_kernel(
    bg_ref, ssd_ref, z_ref, rc_ref, gain_ref, c_ref, open_ref, wide_ref,
    dy_ref, gz_ref, gated_ref, ggain_ref, enter_ref,
):
    @pl.when(pl.program_id(0) == 0)
    def _():
        ggain_ref[...] = jnp.zeros_like(ggain_ref)
        enter_ref[...] = jnp.zeros_like(enter_ref)

    ssd = ssd_ref[...]
    z = z_ref[...]
    sig = sigmoid(z)
    gate = z * sig
    mixed = ssd * gate
    rms = rc_ref[:, 0:1]
    back = bg_ref[...].astype(f32)
    normed = mixed * rms
    gained = back * gain_ref[...]
    g_mixed = gained * rms - mixed * rc_ref[:, 1:2]
    gated_ref[...] = (normed * gain_ref[...]).astype(bf16)
    ggain_ref[...] += jnp.sum(normed * back, axis=0, keepdims=True)
    dy = (g_mixed * gate).astype(bf16)
    dy_ref[...] = dy
    gz_ref[...] = (g_mixed * ssd * (sig + gate * (1.0 - sig))).astype(bf16)
    opened = (dy.astype(f32) * dot_nn(open_ref[...], wide_ref[...], highest)).astype(bf16)
    enter_ref[...] += dot_tn(opened, c_ref[...])


def ssd_backward_kernel(
    prev_ref, last_ref, x_ref, xprev_ref, bcs_ref, bprev_ref, edge_ref, kept_ref, segc_ref, segr_ref,
    dy_ref, states_ref, openprev_ref, enter_ref, back_ref,
    weight_ref, cbias_ref, bias_ref, rate_ref, skip_ref, wide_ref, tall_ref,
    dx_ref, dbc_ref, dstep_ref, tail_ref, dedge_ref, dconv_ref, dhead_ref,
    dstate, follow, buf, grad,
):
    rows = x_ref.shape[0]
    inner = x_ref.shape[1]
    width = states_ref.shape[1]
    heads = inner // SSM_DIM
    first = pl.program_id(0) == 0
    chunk = pl.num_programs(0) - 1 - pl.program_id(0)

    @pl.when(first)
    def _():
        dstate[...] = back_ref[...]
        follow[...] = jnp.zeros_like(follow)
        dconv_ref[...] = jnp.zeros_like(dconv_ref)
        dhead_ref[...] = jnp.zeros_like(dhead_ref)

    fill_conv(buf, chunk, x_ref, xprev_ref, bcs_ref, bprev_ref, edge_ref, inner, rows)
    weight = weight_ref[...]
    kept = kept_ref[...]
    pre = conv_rows(buf, weight, cbias_ref[...], kept, rows)
    sig = sigmoid(pre)
    conv = pre * sig
    slope = sig + conv * (1.0 - sig)
    values = conv[:, :inner]
    b_low = conv[:, inner : inner + width].astype(bf16)
    c_low = conv[:, inner + width :].astype(bf16)
    prev, last = prev_ref[chunk], last_ref[chunk]
    raw, step, decay, cum, tri, allowed, enter, tail, last_cum, through = span_terms(
        bcs_ref, 2 * width, bias_ref, rate_ref, segc_ref, segr_ref, prev, last, rows
    )
    cum_t = cum.T
    inter = jnp.where(allowed, dot_nt(c_low, b_low), 0.0)
    wide = wide_ref[...]
    tall = tall_ref[...]
    step_wide = dot_nn(step, wide, highest)
    enter_wide = dot_nn(enter, wide, highest)
    tail_wide = dot_nn(tail, wide, highest)
    scaled_low = (values * step_wide).astype(bf16)
    scaled = scaled_low.astype(f32)
    dy_low = dy_ref[...]
    dy = dy_low.astype(f32)
    reach = jnp.where(chunk == 0, jnp.ones((8, LANES), f32), jnp.broadcast_to(openprev_ref[7:8, :], (8, LANES)))
    old = states_ref[...].astype(f32) + dot_nt(tall, reach, highest)[:, 0:1] * enter_ref[...].astype(f32)
    old_low = old.astype(bf16)
    dnew = dstate[...]
    dnew_low = dnew.astype(bf16)
    dy_enter = (dy * enter_wide).astype(bf16)
    from_state = dot_nt(c_low, old_low) * enter_wide
    to_state = dot_nt(b_low, dnew_low) * tail_wide
    dc = dot_nn(dy_enter, old_low)
    db = dot_nn((scaled * tail_wide).astype(bf16), dnew_low)
    through_column = dot_nt(tall, jnp.broadcast_to(through, (8, LANES)), highest)[:, 0:1]
    state_dots = jnp.sum(dnew * old, axis=1, keepdims=True) * through_column
    through_sum = jnp.sum(tall * state_dots, axis=0, keepdims=True)
    dstate[...] = dnew * through_column + dot_tn(dy_enter, c_low)
    low = lane_low(rows)
    mixed_grad = jnp.zeros((rows, rows), f32)
    within_parts = []
    dscaled_parts = []
    for pair in range(heads // 2):
        cols = slice(pair * LANES, (pair + 1) * LANES)
        scaled_pair = scaled_low[:, cols]
        dy_pair = dy_low[:, cols]
        ahead = []
        behind = []
        for index in range(2):
            head = 2 * pair + index
            spread = jnp.exp(jnp.minimum(cum[:, head : head + 1] - cum_t[head : head + 1, :], 0.0))
            mixing = (inter * spread).astype(bf16)
            dy_one = jnp.where(low if index == 0 else jnp.logical_not(low), dy_pair, jnp.zeros_like(dy_pair))
            mixed_grad = mixed_grad + dot_nt(dy_one, scaled_pair) * spread
            ahead.append(dot_nn(mixing, scaled_pair))
            behind.append(dot_tn(mixing, dy_pair))
        within_parts.append(jnp.where(low, ahead[0], ahead[1]))
        dscaled_parts.append(jnp.where(low, behind[0], behind[1]))
    within = jnp.concatenate(within_parts, axis=1)
    dscaled = jnp.concatenate(dscaled_parts, axis=1)
    mixed_low = jnp.where(allowed, mixed_grad, 0.0).astype(bf16)
    dc = dc + dot_nn(mixed_low, b_low)
    db = db + dot_tn(mixed_low, c_low)
    fresh_dots = dot_nn(scaled * to_state, tall, highest)
    dcum = dot_nn(dy * (within + from_state) - scaled * dscaled, tall, highest) - fresh_dots
    tail_sum = jnp.sum(fresh_dots, axis=0, keepdims=True) + through_sum
    ddecay = dot_tn(tri, dcum, highest) + tail_sum
    dscaled = dscaled + to_state
    dvalues = step_wide * dscaled + skip_ref[...] * dy
    dstep = dot_nn(dscaled * values, tall, highest) + ddecay * rate_ref[...]
    draw = dstep * sigmoid(raw)
    dskip = jnp.sum(dot_nn(dy * values, tall, highest), axis=0, keepdims=True)
    dhead_ref[0:1, :] += jnp.sum(draw, axis=0, keepdims=True)
    dhead_ref[1:2, :] += jnp.sum(ddecay * decay, axis=0, keepdims=True)
    dhead_ref[2:3, :] += dskip
    dstep_ref[...] = draw.astype(bf16)
    dpre = jnp.concatenate([dvalues, db, dc], axis=1) * slope
    din = weight[3:4, :] * dpre
    dconv_ref[3:4, :] += jnp.sum(dpre * buf[8 : 8 + rows, :], axis=0, keepdims=True)
    dconv_ref[4:5, :] += jnp.sum(dpre, axis=0, keepdims=True)
    dedge = jnp.zeros((8, dpre.shape[1]), f32)
    for tap in range(3):
        masked = dpre * kept[:, tap : tap + 1]
        dconv_ref[tap : tap + 1, :] += jnp.sum(masked * buf[5 + tap : 5 + tap + rows, :], axis=0, keepdims=True)
        grad[0:8, :] = jnp.zeros((8, dpre.shape[1]), f32)
        grad[8 : 8 + rows, :] = masked
        grad[8 + rows :, :] = follow[tap]
        din = din + weight[tap : tap + 1, :] * grad[11 - tap : 11 - tap + rows, :]
        dedge = dedge + weight[tap : tap + 1, :] * grad[3 - tap : 11 - tap, :]
        follow[tap] = masked[0:8, :]
    dedge_ref[...] = dedge
    dx_ref[...] = din[:, :inner].astype(bf16)
    dbc_ref[...] = din[:, inner:].astype(bf16)

    @pl.when(first)
    def _():
        tail_ref[...] = din[rows - 8 :, :]


def attention_kernel(
    low_ref, q_ref, do_ref, k0_ref, v0_ref, k1_ref, v1_ref, k2_ref, v2_ref, segc_ref, segr_ref,
    out_ref, dq_ref, dk0_ref, dv0_ref, dk1_ref, dv1_ref, dk2_ref, dv2_ref,
    dk_acc, dv_acc, acc, stats, dqt,
    *, scale,
):
    rows = q_ref.shape[0]
    blocks = rows // SPAN
    piece_refs = ((k2_ref, v2_ref), (k1_ref, v1_ref), (k0_ref, v0_ref))
    pieces = len(piece_refs)
    low = lane_low(SPAN)
    high = jnp.logical_not(low)
    zero = jnp.zeros((SPAN, LANES), bf16)
    top_rows = lax.broadcasted_iota(jnp.int32, (LANES, SPAN), 0) < ATT_DIM
    row = lax.broadcasted_iota(jnp.int32, (SPAN, SPAN), 0)
    col = lax.broadcasted_iota(jnp.int32, (SPAN, SPAN), 1)
    pick = (
        (lax.broadcasted_iota(jnp.int32, (8, LANES), 1) >= ATT_DIM)
        == (lax.broadcasted_iota(jnp.int32, (8, LANES), 0) == 1)
    ).astype(f32)
    dk_acc[...] = jnp.zeros_like(dk_acc)
    dv_acc[...] = jnp.zeros_like(dv_acc)

    def halves(value):
        return jnp.where(low, value, zero), jnp.where(high, value, zero)

    def allowed_at(piece, start, segr, block):
        same = segc_ref[pl.ds(piece * rows + start, SPAN), :] == segr
        if piece == pieces - 1:
            return same & (row + start <= col + block * SPAN)
        return same

    for block in range(blocks):
        q_rows = slice(block * SPAN, (block + 1) * SPAN)
        q_both = halves(q_ref[q_rows, :] * jnp.asarray(scale, bf16))
        do_full = do_ref[q_rows, :]
        do_both = halves(do_full)
        segr = segr_ref[:, q_rows]
        acc[...] = jnp.zeros_like(acc)
        stats[0:2, :] = jnp.full((2, SPAN), masked_score, f32)
        stats[2:4, :] = jnp.zeros((2, SPAN), f32)
        for piece in range(pieces):
            k_ref, v_ref = piece_refs[piece]
            stop = block + 1 if piece == pieces - 1 else blocks

            def forward_step(index, unused):
                start = pl.multiple_of(index * SPAN, SPAN)
                key = k_ref[pl.ds(start, SPAN), :]
                value_both = halves(v_ref[pl.ds(start, SPAN), :])
                allowed = allowed_at(piece, start, segr, block)
                added = jnp.zeros((LANES, SPAN), f32)
                shrink = []
                for head in range(2):
                    scores = jnp.where(allowed, dot_nt(key, q_both[head]), masked_score)
                    old_top = stats[head : head + 1, :]
                    new_top = jnp.maximum(old_top, jnp.max(scores, axis=0, keepdims=True))
                    weights = jnp.where(allowed, jnp.exp(scores - new_top), 0.0)
                    factor = jnp.exp(old_top - new_top)
                    stats[head : head + 1, :] = new_top
                    stats[2 + head : 3 + head, :] = stats[2 + head : 3 + head, :] * factor + jnp.sum(
                        weights, axis=0, keepdims=True
                    )
                    shrink.append(factor)
                    added = added + dot_tn(value_both[head], weights.astype(bf16))
                acc[...] = acc[...] * jnp.where(top_rows, shrink[0], shrink[1]) + added
                return unused

            lax.fori_loop(low_ref[block * pieces + piece], stop, forward_step, 0)
        inverse = [1.0 / stats[2 + head : 3 + head, :] for head in range(2)]
        attended = (acc[...] * jnp.where(top_rows, inverse[0], inverse[1])).T
        out_ref[q_rows, :] = attended.astype(bf16)
        delta = dot_nt(pick, do_full.astype(f32) * attended, highest)
        mass = [stats[head : head + 1, :] + jnp.log(stats[2 + head : 3 + head, :]) for head in range(2)]
        dqt[...] = jnp.zeros_like(dqt)
        for piece in range(pieces):
            k_ref, v_ref = piece_refs[piece]
            stop = block + 1 if piece == pieces - 1 else blocks

            def backward_step(index, unused):
                start = pl.multiple_of(index * SPAN, SPAN)
                key = k_ref[pl.ds(start, SPAN), :]
                value = v_ref[pl.ds(start, SPAN), :]
                key_both = halves(key)
                allowed = allowed_at(piece, start, segr, block)
                dk = jnp.zeros((SPAN, LANES), f32)
                dv = jnp.zeros((SPAN, LANES), f32)
                dq = jnp.zeros((LANES, SPAN), f32)
                for head in range(2):
                    scores = dot_nt(key, q_both[head])
                    weights = jnp.where(allowed, jnp.exp(scores - mass[head]), 0.0)
                    dweights = dot_nt(value, do_both[head])
                    dscores = (weights * (dweights - delta[head : head + 1, :])).astype(bf16)
                    dv = dv + dot_nn(weights.astype(bf16), do_both[head])
                    dk = dk + dot_nn(dscores, q_both[head])
                    dq = dq + dot_tn(key_both[head], dscores)
                where = pl.ds(piece * rows + start, SPAN)
                dk_acc[where, :] += dk
                dv_acc[where, :] += dv
                dqt[...] += dq
                return unused

            lax.fori_loop(low_ref[block * pieces + piece], stop, backward_step, 0)
        dq_ref[q_rows, :] = (dqt[...] * scale).T.astype(dq_ref.dtype)
    for piece, (dk_ref, dv_ref) in enumerate(((dk2_ref, dv2_ref), (dk1_ref, dv1_ref), (dk0_ref, dv0_ref))):
        dk_ref[...] = dk_acc[piece * rows : (piece + 1) * rows, :].astype(dk_ref.dtype)
        dv_ref[...] = dv_acc[piece * rows : (piece + 1) * rows, :].astype(dv_ref.dtype)


def from_behind(value, axis, by):
    count = lax.axis_size(axis)
    pairs = [(i, i + by) for i in range(count) if 0 <= i + by < count]
    return lax.ppermute(value, axis, pairs)


def params(**extra):
    return pltpu.CompilerParams(vmem_limit_bytes=VMEM_LIMIT, **extra)


def cost(flops, moved, transcendentals=0):
    return pl.CostEstimate(flops=int(flops), bytes_accessed=int(moved), transcendentals=int(transcendentals))


def fixed(shape):
    return pl.BlockSpec(shape, lambda *unused: (0,) * len(shape))


def ssd_specs(order, inner, bc_width, state_width):
    per = SPAN // 8
    channels = inner + bc_width

    def before(i):
        return jnp.maximum(order(i) * per - 1, 0)

    return [
        pl.BlockSpec((SPAN, inner), lambda i, *unused: (order(i), 1)),
        pl.BlockSpec((8, inner), lambda i, *unused: (before(i), 1)),
        pl.BlockSpec((SPAN, bc_width + LANES), lambda i, *unused: (order(i), 0)),
        pl.BlockSpec((8, bc_width + LANES), lambda i, *unused: (before(i), 0)),
        fixed((8, channels)),
        pl.BlockSpec((SPAN, 8), lambda i, *unused: (order(i), 0)),
        pl.BlockSpec((SPAN, 1), lambda i, *unused: (order(i), 0)),
        pl.BlockSpec((1, SPAN), lambda i, *unused: (0, order(i))),
    ]


def ssd_constant_specs(inner, channels):
    return [
        fixed((CONV, channels)),
        fixed((1, channels)),
        fixed((1, LANES)),
        fixed((1, LANES)),
        fixed((1, inner)),
        fixed((LANES, inner)),
        fixed((inner, LANES)),
    ]


def ssd_forward(prev, last, zx, bcs, edge, kept, segc, segr, constants, inner, width):
    rows = zx.shape[0]
    blocks = rows // SPAN
    channels = inner + 2 * width
    heads = inner // SSM_DIM
    order = lambda i: i
    return pl.pallas_call(
        ssd_forward_kernel,
        grid_spec=pltpu.PrefetchScalarGridSpec(
            num_scalar_prefetch=2,
            grid=(blocks,),
            in_specs=ssd_specs(order, inner, 2 * width, width) + ssd_constant_specs(inner, channels),
            out_specs=[
                pl.BlockSpec((SPAN, inner), lambda i, *unused: (i, 0)),
                pl.BlockSpec((SPAN, width), lambda i, *unused: (i, 0)),
                pl.BlockSpec((SPAN, LANES), lambda i, *unused: (i, 0)),
                pl.BlockSpec((inner, width), lambda i, *unused: (i, 0)),
                fixed((inner, width)),
                fixed((8, LANES)),
            ],
            scratch_shapes=[
                pltpu.VMEM((inner, width), f32),
                pltpu.VMEM((8, LANES), f32),
                pltpu.VMEM((SPAN + 8, channels), f32),
            ],
        ),
        out_shape=[
            jax.ShapeDtypeStruct((rows, inner), f32),
            jax.ShapeDtypeStruct((rows, width), bf16),
            jax.ShapeDtypeStruct((rows, LANES), f32),
            jax.ShapeDtypeStruct((blocks * inner, width), bf16),
            jax.ShapeDtypeStruct((inner, width), f32),
            jax.ShapeDtypeStruct((8, LANES), f32),
        ],
        compiler_params=params(),
        cost_estimate=cost(rows * SPAN * inner * 6, rows * inner * 12, rows * SPAN * heads),
        name="ssd_forward",
    )(prev, last, zx, zx, bcs, bcs, edge, kept, segc, segr, *constants)


def ssd_backward(prev, last, zx, bcs, edge, kept, segc, segr, dy, states, opened, entering, back_end, constants, inner, width):
    rows = zx.shape[0]
    blocks = rows // SPAN
    channels = inner + 2 * width
    heads = inner // SSM_DIM
    order = lambda i: blocks - 1 - i
    return pl.pallas_call(
        ssd_backward_kernel,
        grid_spec=pltpu.PrefetchScalarGridSpec(
            num_scalar_prefetch=2,
            grid=(blocks,),
            in_specs=ssd_specs(order, inner, 2 * width, width)
            + [
                pl.BlockSpec((SPAN, inner), lambda i, *unused: (order(i), 0)),
                pl.BlockSpec((inner, width), lambda i, *unused: (order(i), 0)),
                pl.BlockSpec((8, LANES), lambda i, *unused: (jnp.maximum(order(i) * (SPAN // 8) - 1, 0), 0)),
                fixed((inner, width)),
                fixed((inner, width)),
            ]
            + ssd_constant_specs(inner, channels),
            out_specs=[
                pl.BlockSpec((SPAN, inner), lambda i, *unused: (order(i), 0)),
                pl.BlockSpec((SPAN, 2 * width), lambda i, *unused: (order(i), 0)),
                pl.BlockSpec((SPAN, LANES), lambda i, *unused: (order(i), 0)),
                fixed((8, channels)),
                fixed((8, channels)),
                fixed((8, channels)),
                fixed((8, LANES)),
            ],
            scratch_shapes=[
                pltpu.VMEM((inner, width), f32),
                pltpu.VMEM((3, 8, channels), f32),
                pltpu.VMEM((SPAN + 8, channels), f32),
                pltpu.VMEM((SPAN + 16, channels), f32),
            ],
        ),
        out_shape=[
            jax.ShapeDtypeStruct((rows, inner), bf16),
            jax.ShapeDtypeStruct((rows, 2 * width), bf16),
            jax.ShapeDtypeStruct((rows, LANES), bf16),
            jax.ShapeDtypeStruct((8, channels), f32),
            jax.ShapeDtypeStruct((8, channels), f32),
            jax.ShapeDtypeStruct((8, channels), f32),
            jax.ShapeDtypeStruct((8, LANES), f32),
        ],
        compiler_params=params(),
        cost_estimate=cost(rows * SPAN * inner * 14, rows * inner * 16, rows * SPAN * heads),
        name="ssd_backward",
    )(prev, last, zx, zx, bcs, bcs, edge, kept, segc, segr, dy, states, opened, entering, back_end, *constants)


def gate_forward(y_zero, state_c, opened, entering, zx, gain, wide):
    rows, inner = y_zero.shape
    width = state_c.shape[1]
    return pl.pallas_call(
        gate_forward_kernel,
        grid=(rows // SPAN,),
        in_specs=[
            pl.BlockSpec((SPAN, inner), lambda i: (i, 0)),
            pl.BlockSpec((SPAN, width), lambda i: (i, 0)),
            pl.BlockSpec((SPAN, LANES), lambda i: (i, 0)),
            fixed((inner, width)),
            pl.BlockSpec((SPAN, inner), lambda i: (i, 0)),
            fixed((1, inner)),
            fixed((LANES, inner)),
        ],
        out_specs=[
            pl.BlockSpec((SPAN, inner), lambda i: (i, 0)),
            pl.BlockSpec((SPAN, inner), lambda i: (i, 0)),
            pl.BlockSpec((8, SPAN), lambda i: (0, i)),
        ],
        out_shape=[
            jax.ShapeDtypeStruct((rows, inner), f32),
            jax.ShapeDtypeStruct((rows, inner), bf16),
            jax.ShapeDtypeStruct((8, rows), f32),
        ],
        compiler_params=params(),
        cost_estimate=cost(rows * inner * width * 4, rows * inner * 14, rows * inner),
        name="gate_forward",
    )(y_zero, state_c, opened, entering, zx, gain, wide)


def gate_backward(back_gated, ssd_out, zx, coefficients, gain, state_c, opened, wide):
    rows, inner = ssd_out.shape
    width = state_c.shape[1]
    return pl.pallas_call(
        gate_backward_kernel,
        grid=(rows // SPAN,),
        in_specs=[
            pl.BlockSpec((SPAN, inner), lambda i: (i, 0)),
            pl.BlockSpec((SPAN, inner), lambda i: (i, 0)),
            pl.BlockSpec((SPAN, inner), lambda i: (i, 0)),
            pl.BlockSpec((SPAN, 8), lambda i: (i, 0)),
            fixed((1, inner)),
            pl.BlockSpec((SPAN, width), lambda i: (i, 0)),
            pl.BlockSpec((SPAN, LANES), lambda i: (i, 0)),
            fixed((LANES, inner)),
        ],
        out_specs=[
            pl.BlockSpec((SPAN, inner), lambda i: (i, 0)),
            pl.BlockSpec((SPAN, inner), lambda i: (i, 0)),
            pl.BlockSpec((SPAN, inner), lambda i: (i, 0)),
            fixed((1, inner)),
            fixed((inner, width)),
        ],
        out_shape=[
            jax.ShapeDtypeStruct((rows, inner), bf16),
            jax.ShapeDtypeStruct((rows, inner), bf16),
            jax.ShapeDtypeStruct((rows, inner), bf16),
            jax.ShapeDtypeStruct((1, inner), f32),
            jax.ShapeDtypeStruct((inner, width), f32),
        ],
        compiler_params=params(),
        cost_estimate=cost(rows * inner * width * 4, rows * inner * 18, rows * inner),
        name="gate_backward",
    )(back_gated, ssd_out, zx, coefficients, gain, state_c, opened, wide)


def attention(low_blocks, query_array, back_attended, pieces, segc, segr, att_pad, rows):
    pairs = att_pad // LANES
    scale = 1.0 / math.sqrt(ATT_DIM)
    count = len(pieces)

    def lane(offset):
        return pl.BlockSpec((rows, LANES), lambda p, *unused: (0, p + offset))

    in_specs = [lane(0), lane(0)]
    operands = [query_array, back_attended]
    for array, offset in pieces:
        in_specs += [lane(offset), lane(offset + pairs)]
        operands += [array, array]
    in_specs += [fixed((count * rows, 1)), fixed((1, rows))]
    shapes = [bf16, f32] + [f32, f32] + [bf16, bf16] * (count - 1)
    return pl.pallas_call(
        partial(attention_kernel, scale=scale),
        grid_spec=pltpu.PrefetchScalarGridSpec(
            num_scalar_prefetch=1,
            grid=(pairs,),
            in_specs=in_specs,
            out_specs=[lane(0)] * len(shapes),
            scratch_shapes=[
                pltpu.VMEM((count * rows, LANES), f32),
                pltpu.VMEM((count * rows, LANES), f32),
                pltpu.VMEM((LANES, SPAN), f32),
                pltpu.VMEM((8, SPAN), f32),
                pltpu.VMEM((LANES, SPAN), f32),
            ],
        ),
        out_shape=[jax.ShapeDtypeStruct((rows, att_pad), kind) for kind in shapes],
        compiler_params=params(),
        cost_estimate=cost(rows * rows * att_pad * 28, rows * att_pad * 30, rows * rows * pairs * 4),
        name="attention",
    )(low_blocks, *operands, segc, segr)


def fit(value, size, axis):
    if value.shape[axis] == size:
        return value
    widths = [(0, 0)] * value.ndim
    widths[axis] = (0, size - value.shape[axis])
    return jnp.pad(value, widths)


def head_gather(values):
    return lax.all_gather(values, "head", axis=1, tiled=True)


def head_scatter(values):
    return lax.psum_scatter(values, "head", scatter_dimension=1, tiled=True)


def seq_scatter(values):
    return lax.psum_scatter(values.astype(bf16), "seq", scatter_dimension=0, tiled=True).astype(f32)


def matmul(a, b, kind=f32):
    return jnp.dot(a, b, preferred_element_type=f32).astype(kind)


def matmul_nt(a, b, kind=f32):
    return lax.dot_general(a, b, (((1,), (1,)), ((), ())), preferred_element_type=f32).astype(kind)


def matmul_tn(a, b, kind=f32):
    return lax.dot_general(a, b, (((0,), (0,)), ((), ())), preferred_element_type=f32).astype(kind)


def per_device(
    tokens, segment_ids, first_gain, proj_zx, proj_bc, proj_step, conv_inner, conv_inner_bias,
    conv_state, conv_state_bias, step_bias, decay_log, skip_scale, gated_gain, proj_out,
    second_gain, proj_qkv, attention_out, cotangent,
):
    rows = tokens.shape[0]
    inner = proj_zx.shape[2]
    bc_width = proj_bc.shape[1]
    width = bc_width // 2
    channels = inner + bc_width
    heads = step_bias.shape[0]
    att = proj_qkv.shape[2]
    att_pad = -(-att // LANES) * LANES
    pairs = att_pad // LANES
    blocks = rows // SPAN
    reach = (DOC_MAX - 2) // rows + 1
    row_start = lax.axis_index("seq") * rows

    padded_seg = jnp.concatenate([jnp.full((reach * rows,), -1, jnp.int32), segment_ids])
    window = lax.dynamic_slice_in_dim(padded_seg, row_start, (reach + 1) * rows)
    local_seg = window[reach * rows :]
    shifted = window[reach * rows - (CONV - 1) :]
    kept = jnp.stack([(shifted[tap : tap + rows] == local_seg).astype(f32) for tap in range(CONV - 1)], axis=1)
    kept = fit(kept, 8, 1)
    span_prev = shifted[CONV - 2 :: SPAN][:blocks]
    span_last = local_seg[SPAN - 1 :: SPAN]
    segc_window = window[:, None]
    segc = local_seg[:, None]
    segr = local_seg[None, :]
    key_last = window[SPAN - 1 :: SPAN].reshape(reach + 1, blocks)
    query_first = local_seg[::SPAN]
    low_blocks = jnp.sum((key_last[None] < query_first[:, None, None]).astype(jnp.int32), axis=2).reshape(-1)

    owner = jnp.arange(inner, dtype=jnp.int32)[None, :] // SSM_DIM
    wide = (owner == jnp.arange(LANES, dtype=jnp.int32)[:, None]).astype(f32)
    tall = wide.T
    constants = (
        jnp.concatenate([conv_inner, conv_state], axis=1),
        jnp.concatenate([conv_inner_bias, conv_state_bias])[None],
        fit(step_bias[None], LANES, 1),
        fit(-jnp.exp(decay_log)[None], LANES, 1),
        jnp.repeat(skip_scale, SSM_DIM)[None],
        wide,
        tall,
    )
    zx_weight = proj_zx.reshape(D, 2 * inner)
    bcs_weight = jnp.concatenate([proj_bc, fit(proj_step, LANES, 1)], axis=1)
    qkv_weight = fit(proj_qkv, att_pad, 2).reshape(D, 3 * att_pad)
    att_weight = fit(attention_out, att_pad, 0)

    gains = lax.all_gather(jnp.stack([first_gain, second_gain]), "head", axis=1, tiled=True)
    token_full = head_gather(tokens).astype(f32)
    first_rms = lax.rsqrt(jnp.sum(token_full * token_full, axis=1) / D + epsilon)
    first_full = (token_full * first_rms[:, None] * gains[0]).astype(bf16)
    cot_full = head_gather(cotangent)
    zx = matmul(first_full, zx_weight)
    bcs = matmul(first_full, bcs_weight)
    edge_rows = jnp.concatenate([zx[rows - 8 :, inner:], bcs[rows - 8 :, :bc_width]], axis=1)
    edge = from_behind(edge_rows, "seq", 1)

    ssd_shared = (span_prev, span_last, zx, bcs, edge, kept, segc, segr)
    y_zero, state_c, opened, states, end_state, through = ssd_forward(*ssd_shared, constants, inner, width)
    through_rows = jnp.broadcast_to(jnp.repeat(through[0, :heads], SSM_DIM)[:, None], (inner, width))

    sent = end_state.astype(bf16)
    near = from_behind(sent, "seq", 1).astype(f32)
    packed = jnp.concatenate([sent, jnp.broadcast_to(through[0:1], (8, LANES)).astype(bf16)], axis=0)
    near_pack = from_behind(packed, "seq", 1).astype(f32)
    near = near_pack[:inner]
    near_through = jnp.repeat(near_pack[inner, :heads], SSM_DIM)[:, None]
    far = from_behind(sent, "seq", 2).astype(f32)
    entering = (near + near_through * far).astype(bf16)

    ssd_out, gated_raw, gate_sums = gate_forward(y_zero, state_c, opened, entering, zx, gated_gain[None], wide)
    gate_total = lax.psum(gate_sums[0], "head")
    gate_rms = lax.rsqrt(gate_total / INNER + epsilon)
    branch_part = matmul(gated_raw, proj_out, bf16)
    branch = head_scatter(branch_part).astype(f32) * gate_rms[:, None]
    hidden_zero = tokens.astype(f32)
    hidden_one = hidden_zero + branch
    second_total = lax.psum(jnp.sum(hidden_one * hidden_one, axis=1), "head")
    second_rms = lax.rsqrt(second_total / D + epsilon)
    second_full = head_gather((hidden_one * second_gain).astype(bf16))
    projected = (matmul(second_full, qkv_weight) * second_rms[:, None]).astype(bf16)
    key_value = projected[:, att_pad:]
    moved = [from_behind(key_value, "seq", back) for back in range(1, reach + 1)]

    back_attended = matmul_nt(cot_full, att_weight, bf16)
    pieces = [(projected, pairs)] + [(array, 0) for array in moved]
    attended, back_query, back_key, back_value, *back_moved = attention(
        low_blocks, projected, back_attended, pieces, segc_window, segr, att_pad, rows
    )
    output = (hidden_one + head_scatter(matmul(attended, att_weight, bf16)).astype(f32)).astype(bf16)
    grad_attention_out = matmul_tn(cot_full, attended[:, :att], bf16)

    for back in range(1, reach + 1):
        pair = jnp.concatenate(back_moved[2 * back - 2 : 2 * back], axis=1)
        pair = from_behind(pair, "seq", -back).astype(f32)
        back_key = back_key + pair[:, :att_pad]
        back_value = back_value + pair[:, att_pad:]
    back_projected = jnp.concatenate([back_query, back_key, back_value], axis=1).astype(bf16)
    back_second = head_scatter(matmul_nt(back_projected, qkv_weight, bf16)).astype(f32)
    second_dots = lax.psum(jnp.sum(back_projected.astype(f32) * projected.astype(f32), axis=1), "head")
    grad_qkv = matmul_tn(
        second_full, (back_projected.astype(f32) * second_rms[:, None]).astype(bf16), bf16
    )
    if att != att_pad:
        grad_qkv = grad_qkv.reshape(D, 3, att_pad)[:, :, :att].reshape(D, 3 * att)
    normed_one = hidden_one * second_rms[:, None]
    grad_second_gain = jnp.sum(normed_one * back_second, axis=0)
    back_hidden_one = (
        cotangent.astype(f32)
        + second_rms[:, None] * second_gain * back_second
        - hidden_one * (second_rms * second_rms / D * second_dots)[:, None]
    )
    back_low = back_hidden_one.astype(bf16)
    back_branch = head_gather(back_low)
    back_gated = matmul_nt(back_branch, proj_out, bf16)
    gate_dots = lax.psum(jnp.sum(back_low.astype(f32) * branch, axis=1), "head")
    coefficients = fit(jnp.stack([gate_rms, gate_rms * gate_rms / INNER * gate_dots], axis=1), 8, 1)
    dy, back_z, gated, grad_gated_gain, back_entering = gate_backward(
        back_gated, ssd_out, zx, coefficients, gated_gain[None], state_c, opened, wide
    )
    grad_out = matmul_tn(back_branch, gated, bf16)

    back_sent = back_entering.astype(bf16)
    back_pack = jnp.concatenate([back_sent, jnp.broadcast_to(through[0:1], (8, LANES)).astype(bf16)], axis=0)
    back_near_pack = from_behind(back_pack, "seq", -1).astype(f32)
    back_far = from_behind(back_sent, "seq", -2).astype(f32)
    back_near_through = jnp.repeat(back_near_pack[inner, :heads], SSM_DIM)[:, None]
    back_end = back_near_pack[:inner] + back_near_through * back_far

    back_x, back_bc, back_step, tail_rows, back_edge, grad_conv, grad_heads = ssd_backward(
        *ssd_shared, dy, states, opened, entering, back_end, constants, inner, width
    )
    tail_rows = (tail_rows + from_behind(back_edge, "seq", -1)).astype(bf16)
    back_x = lax.dynamic_update_slice(back_x, tail_rows[:, :inner], (rows - 8, 0))
    back_bc = lax.dynamic_update_slice(back_bc, tail_rows[:, inner:], (rows - 8, 0))

    first_part = (
        matmul_nt(back_z, zx_weight[:, :inner])
        + matmul_nt(back_x, zx_weight[:, inner:])
        + matmul_nt(back_bc, proj_bc)
        + matmul_nt(back_step, bcs_weight[:, bc_width:])
    ).astype(bf16)
    back_first = head_scatter(first_part).astype(f32)
    first_dots = lax.psum(
        jnp.sum(back_z.astype(f32) * zx[:, :inner], axis=1)
        + jnp.sum(back_x.astype(f32) * zx[:, inner:], axis=1)
        + jnp.sum(back_bc.astype(f32) * bcs[:, :bc_width], axis=1)
        + jnp.sum(back_step.astype(f32) * bcs[:, bc_width:], axis=1),
        "head",
    )
    grad_zx_gate = matmul_tn(first_full, back_z, bf16)
    grad_zx_inner = matmul_tn(first_full, back_x, bf16)
    grad_bc = matmul_tn(first_full, back_bc, bf16)
    grad_step = matmul_tn(first_full, back_step)[:, :heads].astype(bf16)
    grad_first_gain = jnp.sum(hidden_zero * first_rms[:, None] * back_first, axis=0)
    grad_tokens = (
        back_hidden_one
        + first_rms[:, None] * first_gain * back_first
        - hidden_zero * (first_rms * first_rms / D * first_dots)[:, None]
    ).astype(bf16)

    wide_qkv = seq_scatter(grad_qkv).reshape(-1, 3, att)
    wide_att = seq_scatter(grad_attention_out).T
    wide_out = seq_scatter(grad_out).T
    wide_zx = jnp.stack([seq_scatter(grad_zx_gate), seq_scatter(grad_zx_inner)], axis=1)
    wide_step = seq_scatter(grad_step)
    both = ("seq", "head")
    shared_bc = lax.psum_scatter(grad_bc, both, scatter_dimension=1, tiled=True).astype(f32)
    shared_conv = lax.psum_scatter(grad_conv[:5, inner:], both, scatter_dimension=1, tiled=True)
    small = lax.psum(
        (
            grad_first_gain,
            grad_conv[:5, :inner],
            grad_heads[:3, :heads],
            grad_gated_gain[0],
            grad_second_gain,
        ),
        "seq",
    )
    return (
        output,
        grad_tokens,
        small[0],
        wide_zx,
        shared_bc,
        wide_step,
        small[1][:4],
        small[1][4],
        shared_conv[:4],
        shared_conv[4],
        small[2][0],
        small[2][1],
        small[2][2],
        small[3],
        wide_out,
        small[4],
        wide_qkv,
        wide_att,
    )


def solution(mesh):
    placed = (
        P("seq", "head"),
        P(),
        P("head"),
        P(None, None, "head"),
        P(),
        P(None, "head"),
        P(None, "head"),
        P("head"),
        P(),
        P(),
        P("head"),
        P("head"),
        P("head"),
        P("head"),
        P("head", None),
        P("head"),
        P(None, None, "head"),
        P("head", None),
        P("seq", "head"),
    )
    return jax.shard_map(
        per_device,
        mesh=mesh,
        in_specs=placed,
        out_specs=(
            P("seq", "head"),
            P("seq", "head"),
            P("head"),
            P("seq", None, "head"),
            P(None, ("seq", "head")),
            P("seq", "head"),
            P(None, "head"),
            P("head"),
            P(None, ("seq", "head")),
            P(("seq", "head")),
            P("head"),
            P("head"),
            P("head"),
            P("head"),
            P("head", "seq"),
            P("head"),
            P("seq", None, "head"),
            P("head", "seq"),
        ),
        check_vma=False,
    )
```

time: 2050 us -> 1190 us (0.58); the launches traced: 2030 us -> 1190 us
  matrix products: 501 us -> 96.1 us
  local copies, waits for them, and re-layouts: 411 us -> 78.2 us
  other arithmetic: 299 us -> 45.3 us
  Pallas kernels: 0 us -> 138 us
  waiting for transfers between devices: 638 us -> 681 us
  blocking collectives: 137 us -> 114 us
    dot_general x90 -> x19, matrix products: 501 us -> 96.1 us  [the longest x7 40.2 us: matmul_tn(): lax.dot_general(a, b, (((0,), (0,)), ((), ())), preferred_element_type=f32)]
    dynamic_update_slice x56 -> x2, local copies, waits for them, and re-layouts: 198 us -> 1.2 us  [the longest x1 0.6 us: per_device(): lax.dynamic_update_slice(back_x, tail_rows[:, :inner], (rows - 8, 0))]
    pallas_call x0 -> x5, Pallas kernels: none -> 138 us  [the longest x1 52.9 us: ssd_backward(): pl.pallas_call(ssd_backward_kernel, grid_spec=pltpu.PrefetchScalarGridSpe...]
    ppermute x6 -> x10, waiting for transfers between devices: 76.1 us -> 184 us  [from_behind(): return lax.ppermute(value, axis, pairs)]
    dynamic_update_slice x35 -> x0, other arithmetic: 65.3 us -> none  [the longest x32 53.2 us: local_ssd(): end_state, outputs = lax.scan(ssd_span, start_state, inputs)]
    reduce_sum x26 -> x9, other arithmetic: 88.2 us -> 23.3 us  [the longest x1 4.01 us: per_device(): jnp.sum(back_x.astype(f32) * zx[:, inner:], axis=1)]
    unnamed x18 -> x21, waiting for transfers between devices: 164 us -> 105 us
    another operation x53 -> x7, other arithmetic: 43.2 us -> 2.55 us
  transfers between devices with their start and end apart: 22 -> 25, of which waited for: 13 -> 20; matrix products, arithmetic and copies ran while one was open for 25% -> 13% of each run, Pallas kernels for 0% -> 5%
where the time goes in v1:
time: 1190 us
  waiting for transfers between devices  681 us (57%)
  Pallas kernels  138 us (12%)
  blocking collectives  114 us (10%)
  matrix products  96.1 us (8%)
  local copies, waits for them, and re-layouts  78.2 us (7%)
  other arithmetic  45.3 us (4%)
  starting transfers between devices  26.7 us (2%)
  between operations  15 us (1%)
    reduce_scatter x4, waiting for transfers between devices, seq_scatter(): lax.psum_scatter(values.astype(bf16), 'seq', scatter_dimension=0, tiled=T...  255 us
    ppermute x10, waiting for transfers between devices, from_behind(): return lax.ppermute(value, axis, pairs)  184 us
    unnamed x21, waiting for transfers between devices  105 us
    reduce_scatter x1, waiting for transfers between devices, per_device(): lax.psum_scatter(grad_bc, both, scatter_dimension=1, tiled=True).astype(f32)  99.6 us
    unnamed x121, local copies, waits for them, and re-layouts  55.5 us
    pallas_call x1, Pallas kernels, ssd_backward(): pl.pallas_call(ssd_backward_kernel, grid_spec=pltpu.PrefetchScalarGridSpe...  52.9 us
    pallas_call x1, Pallas kernels, attention(): pl.pallas_call(partial(attention_kernel, scale=scale), grid_spec=pltpu.Pr...  46 us
    unnamed x1, blocking collectives  40.3 us
  transfers between devices with their start and end apart: 25, of which 20 were waited for; matrix products, arithmetic and copies ran while one was open for 13% of the time, Pallas kernels for 5%

profile of v1, /device:TPU:0, one launch (start us, length us, event | category | flops | bytes accessed | tf_op | source)
XLA Modules:
  0.0 1194.2 jit_solution(10316139136185892445)
XLA Ops:
  11.4 5.6 copy.90
  18.1 6.2 all_gather.16
  27.1 13.8 %all-gather.5.cloned.1.call-done = bf16[1024,1536]{1,0:T(8,128)(2,1)} async-done(((bf16[1024,384]{1,0:T(8,128)(2,1)}), bf16[1024,1536]{1,0:T(8,128)(2,1)}) %all-gather.5.cloned.1.call-update) | async-done | bytes 3145744 | tf_op jit(solution)/shard_map/all_gather | solution.py:671
  44.2 7.1 fusion.52.x_ref.xprev_ref.z_ref
  63.7 19.5 %ssd_forward.1 = (f32[1024,768]{1,0:T(8,128)}, bf16[1024,128]{1,0:T(8,128)(2,1)}, f32[1024,128]{1,0:T(8,128)}, bf16[3072,128]{1,0:T(8,128)(2,1)}, f32[768,128]{1,0:T(8,128)}, /*index=5*/f32[8,128]{1,0:T(8,128)}) custom-call(s32[4]{0:T(128)} %bitcast.106, s32[4]{0:T(128)} %slice.139.last_ref, f32[1024,1536]{1,0:T(8,128)} %copy-done.1, ...), custom_call_target="tpu_custom_call" | custom-call | flops 1207959552 | bytes 9437184 | tf_op jit(solution)/shard_map/ssd_forward/pallas_call | solution.py:473
  97.2 10.5 gate_forward.1
  107.6 5.4 convolution_convert_fusion.2
  113.1 4.7 copy.75
  118.6 5.9 psum.70
  124.6 32.8 %reduce-scatter.35.cloned.1.call-done = bf16[384,1024]{1,0:T(8,128)(2,1)} async-done(((bf16[1536,1024]{1,0:T(8,128)(2,1)}), bf16[384,1024]{1,0:T(8,128)(2,1)}) %reduce-scatter.35.cloned.1.call-update) | async-done | bytes 786448
  162.8 6.1 copy.68
  168.9 6.2 psum.71
  175.1 15.8 %all-gather.7.cloned.1.call-done = bf16[1024,1536]{1,0:T(8,128)(2,1)} async-done(((bf16[1024,384]{1,0:T(8,128)(2,1)}), bf16[1024,1536]{1,0:T(8,128)(2,1)}) %all-gather.7.cloned.1.call-update) | async-done | bytes 3145744 | tf_op jit(solution)/shard_map/all_gather | solution.py:671
  190.9 7.2 fusion.5.q_ref.k0_ref.v0_ref
  212.4 8.5 all-gather.9.cloned.1.call-done
  220.8 4.9 convolution_convert_fusion.10.do_ref
  225.7 12.8 %collective-permute-done.3.k1_ref.v1_ref = bf16[1024,768]{1,0:T(8,128)(2,1)} collective-permute-done((bf16[1024,768]{1,0:T(8,128)(2,1)}, bf16[1024,768]{1,0:T(8,128)(2,1)}, u32[]{:S(2)}, u32[]{:S(2)}) %collective-permute-start.3) | collective-permute-done | bytes 1572896 | tf_op jit(solution)/shard_map/ppermute | solution.py:421
  241.7 46.0 %attention.1 = (bf16[1024,384]{1,0:T(8,128)(2,1)}, f32[1024,384]{1,0:T(8,128)}, f32[1024,384]{1,0:T(8,128)}, f32[1024,384]{1,0:T(8,128)}, bf16[1024,384]{1,0:T(8...) custom-call(s32[12]{0:T(128)} %reshape.106.low_ref, ...), custom_call_target="tpu_custom_call" | custom-call | flops 11274289152 | bytes 11796480 | tf_op jit(solution)/shard_map/attention/pallas_call | solution.py:640
  292.6 118.4 %collective-permute-done.5 = bf16[1024,768]{1,0:T(8,128)(2,1)S(1)} collective-permute-done((bf16[1024,768]{1,0:T(8,128)(2,1)S(1)}, bf16[1024,768]{1,0:T(8,128)(2,1)S(1)}, u32[]{:S(2)}, u32[]{:S(2)}) %collective-permute-start.5) | collective-permute-done | bytes 1572896 | tf_op jit(solution)/shard_map/ppermute | solution.py:421
  411.2 34.6 %collective-permute-done.6 = bf16[1024,768]{1,0:T(8,128)(2,1)S(1)} collective-permute-done((bf16[1024,768]{1,0:T(8,128)(2,1)S(1)}, bf16[1024,768]{1,0:T(8,128)(2,1)S(1)}, u32[]{:S(2)}, u32[]{:S(2)}) %collective-permute-start.6) | collective-permute-done | bytes 1572896 | tf_op jit(solution)/shard_map/ppermute | solution.py:421
  448.6 5.6 convolution_convert_fusion.3
  454.3 4.6 copy.79
  462.5 5.8 psum.72
  468.3 25.0 %reduce-scatter.39.cloned.1.call-done = bf16[384,1024]{1,0:T(8,128)(2,1)} async-done(((bf16[1536,1024]{1,0:T(8,128)(2,1)}), bf16[384,1024]{1,0:T(8,128)(2,1)}) %reduce-scatter.39.cloned.1.call-update) | async-done | bytes 786448
  506.4 5.2 convolution_convert_fusion.1
  511.6 4.7 copy.77
  516.3 8.8 convolution_convert_fusion
  525.2 5.9 psum.73
  534.0 5.7 convolution_convert_fusion.9.bg_ref
  539.7 8.8 gate_backward.1
  553.8 6.3 collective-permute-done.7
  562.2 4.8 collective-permute-done.8
  568.8 52.9 %ssd_backward.1 = (bf16[1024,768]{1,0:T(8,128)(2,1)}, bf16[1024,256]{1,0:T(8,128)(2,1)}, bf16[1024,128]{1,0:T(8,128)(2,1)}, f32[8,1024]{1,0:T(8,128)}, f32[8,102...) custom-call(s32[4]{0:T(128)} %bitcast.107, s32[4]{0:T(128)} %slice.139.last_ref, f32[1024,1536]{1,0:T(8,128)} %copy-done.1, ...), custom_call_target="tpu_custom_call" | custom-call | flops 2818572288 | bytes 12582912 | tf_op jit(solution)/shard_map/ssd_backward/pallas_call | solution.py:513
  632.4 6.4 convolution_convert_fusion.4
  638.9 6.7 convolution_convert_fusion.6
  646.3 6.7 convolution_convert_fusion.5
  653.3 4.9 fusion.12
  666.7 4.7 copy.81
  677.4 41.6 %reduce-scatter.33.cloned.1.call-done = bf16[192,1152]{1,0:T(8,128)(2,1)} async-done(((bf16[1536,1152]{1,0:T(8,128)(2,1)}), bf16[192,1152]{1,0:T(8,128)(2,1)}) %reduce-scatter.33.cloned.1.call-update) | async-done | bytes 442384 | tf_op jit(solution)/shard_map/reduce_scatter | solution.py:679
  721.1 40.3 %all-reduce.6 = f32[5,256]{1,0:T(8,128)S(1)} all-reduce(f32[5,256]{1,0:T(8,128)S(1)} %slice.171), channel_id=10, replica_groups=mesh['seq'=8,'head'=4] {'seq','head'}, use_global_device_ids=true, to_apply=%region_25.26.clone | all-reduce | flops 1280 | bytes 10240
  769.4 5.8 psum.74
  775.3 9.3 reduce-scatter.43.cloned.1.call-done
  786.0 99.6 %reduce-scatter.29.cloned.1.call-done = bf16[1536,8]{0,1:T(8,128)(2,1)} async-done(((bf16[1536,256]{0,1:T(8,128)(2,1)}), bf16[1536,8]{0,1:T(8,128)(2,1)}) %reduce-scatter.29.cloned.1.call-update) | async-done | bytes 24592 | tf_op jit(solution)/shard_map/reduce_scatter | solution.py:864
  886.9 70.7 %reduce-scatter.31.cloned.1.call-done = bf16[192,768]{1,0:T(8,128)(2,1)} async-done(((bf16[1536,768]{1,0:T(8,128)(2,1)}), bf16[192,768]{1,0:T(8,128)(2,1)}) %reduce-scatter.31.cloned.1.call-update) | async-done | bytes 294928 | tf_op jit(solution)/shard_map/reduce_scatter | solution.py:679
  959.5 70.5 %reduce-scatter.25.cloned.1.call-done = bf16[192,768]{1,0:T(8,128)(2,1)} async-done(((bf16[1536,768]{1,0:T(8,128)(2,1)}), bf16[192,768]{1,0:T(8,128)(2,1)}) %reduce-scatter.25.cloned.1.call-update) | async-done | bytes 294928 | tf_op jit(solution)/shard_map/reduce_scatter | solution.py:679
  1030.0 72.1 %reduce-scatter.27.cloned.1.call-done = bf16[192,768]{1,0:T(8,128)(2,1)} async-done(((bf16[1536,768]{1,0:T(8,128)(2,1)}), bf16[192,768]{1,0:T(8,128)(2,1)}) %reduce-scatter.27.cloned.1.call-update) | async-done | bytes 294928 | tf_op jit(solution)/shard_map/reduce_scatter | solution.py:679
  1105.2 36.5 %reduce-scatter.41.cloned.1.call-done = bf16[384,1024]{1,0:T(8,128)(2,1)} async-done(((bf16[1536,1024]{1,0:T(8,128)(2,1)}), bf16[384,1024]{1,0:T(8,128)(2,1)}) %reduce-scatter.41.cloned.1.call-update) | async-done | bytes 786448
  1147.8 38.0 %all-reduce.7 = (f32[384]{0:T(512)}, f32[5,768]{1,0:T(8,128)S(1)}, f32[3,12]{1,0:T(4,128)S(1)}, f32[768]{0:T(1024)}, f32[384]{0:T(512)}) all-reduce(f32[384]{0:T(512)S(1)} %get-tuple-element.162, f32[5,768]{1,0:T(8,128)S(1)} %slice.168, f32[3,12]{1,0:T(4,128)S(1)} %slice.174, ...), channel_id=1, replica_groups=mesh['seq'=8,'head'=4] {'seq'}, use_global_device_ids=true, to_apply=%region_19.20 | all-reduce | flops 5412 | bytes 43296 | tf_op jit(solution)/shard_map/psum | solution.py:866
  (272 shorter events, 149.4 us)
Async XLA Ops:
  7.2 100.5 %copy-start = (bf16[768,1536]{1,0:T(8,128)(2,1)S(1)}, bf16[768,1536]{1,0:T(8,128)(2,1)}, u32[]{:S(2)}) copy-start(bf16[768,1536]{1,0:T(8,128)(2,1)} %param.33) | copy-start | bytes 7077892
  7.2 33.7 %all-gather.5.cloned.1.call-start = ((), (), s32[]{:S(2)}) async-start(), calls=%async_computation.11 | async-start | bytes 3932160 | tf_op jit(solution)/shard_map/all_gather | solution.py:671
  7.9 149.4 %reduce-scatter.35.cloned.1.call-start = ((), (), s32[]{:S(2)}) async-start(), calls=%async_computation.20 | async-start | bytes 3932160
  8.8 50.9 %copy-start.28 = (s32[1024]{0:T(1024)}, s32[1024]{0:T(1024)S(1)}, u32[]{:S(2)}) copy-start(s32[1024]{0:T(1024)S(1)} %get-tuple-element.159) | copy-start | bytes 12292
  11.4 12.9 %copy-start.37 = (f32[4,768]{1,0:T(4,128)S(1)}, f32[4,768]{1,0:T(4,128)}, u32[]{:S(2)}) copy-start(f32[4,768]{1,0:T(4,128)} %param.25) | copy-start | bytes 36868
  11.4 12.9 %copy-start.43 = (f32[4,256]{1,0:T(4,128)S(1)}, f32[4,256]{1,0:T(4,128)}, u32[]{:S(2)}) copy-start(f32[4,256]{1,0:T(4,128)} %param.27) | copy-start | bytes 12292
  11.4 12.9 %copy-start.22 = (s32[8192]{0:T(1024)S(1)}, s32[8192]{0:T(1024)}, u32[]{:S(2)}) copy-start(s32[8192]{0:T(1024)} %param.20) | copy-start | bytes 98308
  11.4 13.9 %copy-start.49 = (f32[12]{0:T(128)S(1)}, f32[12]{0:T(128)}, u32[]{:S(2)}) copy-start(f32[12]{0:T(128)} %param.30) | copy-start | bytes 148
  24.4 26.9 %copy-start.27 = (f32[4,1024]{1,0:T(4,128)}, f32[4,1024]{1,0:T(4,128)S(1)}, u32[]{:S(2)}) copy-start(f32[4,1024]{1,0:T(4,128)S(1)} %constant_dynamic-update-slice_fusion.weight_ref) | copy-start | bytes 49156
  24.5 26.9 %copy-start.40 = (f32[1536]{0:T(1024)}, f32[1536]{0:T(1024)S(1)}, u32[]{:S(2)}) copy-start(f32[1536]{0:T(1024)S(1)} %slice_reduce_fusion) | copy-start | bytes 18436
  51.4 11.2 copy-start.50
  55.1 8.0 collective-permute-start
  63.7 24.7 %copy-start.42 = (f32[768]{0:T(1024)S(1)}, f32[768]{0:T(1024)}, u32[]{:S(2)}) copy-start(f32[768]{0:T(1024)} %param.32) | copy-start | bytes 9220
  85.0 7.8 collective-permute-start.1
  89.0 7.4 collective-permute-start.2
  117.7 41.9 %copy-start.3 = (bf16[1024,384]{1,0:T(8,128)(2,1)S(1)}, bf16[1024,384]{1,0:T(8,128)(2,1)}, u32[]{:S(2)}) copy-start(bf16[1024,384]{1,0:T(8,128)(2,1)} %param.19) | copy-start | bytes 2359300
  117.7 41.9 %copy-start.33 = (f32[384]{0:T(512)S(1)}, f32[384]{0:T(512)}, u32[]{:S(2)}) copy-start(f32[384]{0:T(512)} %param.34) | copy-start | bytes 4612
  117.8 73.1 %all-gather.7.cloned.1.call-start = ((), (), s32[]{:S(2)}) async-start(), calls=%async_computation.12 | async-start | bytes 3932160 | tf_op jit(solution)/shard_map/all_gather | solution.py:671
  162.1 58.7 %all-gather.9.cloned.1.call-start = ((), (), s32[]{:S(2)}) async-start(), calls=%async_computation.13 | async-start | bytes 3932160 | tf_op jit(solution)/shard_map/all_gather | solution.py:671
  162.7 330.6 %reduce-scatter.39.cloned.1.call-start = ((), (), s32[]{:S(2)}) async-start(), calls=%async_computation.22 | async-start | bytes 3932160
  200.8 37.7 %collective-permute-start.3 = (bf16[1024,768]{1,0:T(8,128)(2,1)}, bf16[1024,768]{1,0:T(8,128)(2,1)}, u32[]{:S(2)}, u32[]{:S(2)}) collective-permute-start(bf16[1024,768]{1,0:T(8,128)(2,1)} %slice.183), channel_id=1, source_target_pairs={{0,4},{4,8},{8,12},{12,16},{16,20},{20,24},{24,28},{1,5},{5,9},{9,... | collective-permute-start | bytes 4718600 | tf_op jit(solution)/shard_map/ppermute | solution.py:421
  205.3 36.3 %collective-permute-start.4 = (bf16[1024,768]{1,0:T(8,128)(2,1)}, bf16[1024,768]{1,0:T(8,128)(2,1)}, u32[]{:S(2)}, u32[]{:S(2)}) collective-permute-start(bf16[1024,768]{1,0:T(8,128)(2,1)} %slice.183), channel_id=1, source_target_pairs={{0,8},{4,12},{8,16},{12,20},{16,24},{20,28},{1,9},{5,13},{9,17},{1... | collective-permute-start | bytes 4718600 | tf_op jit(solution)/shard_map/ppermute | solution.py:421
  289.3 121.6 %collective-permute-start.5 = (bf16[1024,768]{1,0:T(8,128)(2,1)S(1)}, bf16[1024,768]{1,0:T(8,128)(2,1)S(1)}, u32[]{:S(2)}, u32[]{:S(2)}) collective-permute-start(bf16[1024,768]{1,0:T(8,128)(2,1)S(1)} %pad_maximum_fusion.1), channel_id=1, source_target_pairs={{4,0},{8,4},{12,8},{16,12},{20,16},{24,20},{28,24},{5,1},{9,5},{13... | collective-permute-start | bytes 4718600 | tf_op jit(solution)/shard_map/ppermute | solution.py:421
  291.1 154.7 %collective-permute-start.6 = (bf16[1024,768]{1,0:T(8,128)(2,1)S(1)}, bf16[1024,768]{1,0:T(8,128)(2,1)S(1)}, u32[]{:S(2)}, u32[]{:S(2)}) collective-permute-start(bf16[1024,768]{1,0:T(8,128)(2,1)S(1)} %pad_maximum_fusion.2), channel_id=1, source_target_pairs={{8,0},{12,4},{16,8},{20,12},{24,16},{28,20},{9,1},{13,5},{17,9},{2... | collective-permute-start | bytes 4718600 | tf_op jit(solution)/shard_map/ppermute | solution.py:421
  292.6 154.1 %copy-start.8 = (bf16[1024,384]{1,0:T(8,128)(2,1)}, bf16[1024,384]{1,0:T(8,128)(2,1)S(1)}, u32[]{:S(2)}) copy-start(bf16[1024,384]{1,0:T(8,128)(2,1)S(1)} %convert.28) | copy-start | bytes 2359300
  411.2 34.9 %copy-start.14 = (f32[1024,384]{1,0:T(8,128)S(1)}, f32[1024,384]{1,0:T(8,128)}, u32[]{:S(2)}) copy-start(f32[1024,384]{1,0:T(8,128)} %get-tuple-element.56) | copy-start | bytes 4718596
  411.2 34.9 %copy-start.15 = (f32[1024,384]{1,0:T(8,128)S(1)}, f32[1024,384]{1,0:T(8,128)}, u32[]{:S(2)}) copy-start(f32[1024,384]{1,0:T(8,128)} %get-tuple-element.61) | copy-start | bytes 4718596
  459.0 75.1 %all-gather.11.cloned.1.call-start = ((), (), s32[]{:S(2)}) async-start(), calls=%async_computation.14 | async-start | bytes 3932160 | tf_op jit(solution)/shard_map/all_gather | solution.py:671
  499.4 172.1 %reduce-scatter.45.cloned.1.call-start = ((), (), s32[]{:S(2)}) async-start(), calls=%async_computation.25 | async-start | bytes 1327104
  506.4 168.7 %reduce-scatter.37.cloned.1.call-start = ((), (), s32[]{:S(2)}) async-start(), calls=%async_computation.21 | async-start | bytes 3932160
  516.3 202.7 %reduce-scatter.33.cloned.1.call-start = ((), (), s32[]{:S(2)}) async-start(), calls=%async_computation.19 | async-start | bytes 3981312 | tf_op jit(solution)/shard_map/reduce_scatter | solution.py:679
  525.1 259.4 %reduce-scatter.43.cloned.1.call-start = ((), (), s32[]{:S(2)}) async-start(), calls=%async_computation.24 | async-start | bytes 442368
  551.2 8.9 collective-permute-start.7
  552.5 14.5 %collective-permute-start.8 = (bf16[768,128]{1,0:T(8,128)(2,1)}, bf16[768,128]{1,0:T(8,128)(2,1)}, u32[]{:S(2)}, u32[]{:S(2)}) collective-permute-start(bf16[768,128]{1,0:T(8,128)(2,1)} %convert_element_type.209), channel_id=1, source_target_pairs={{8,0},{12,4},{16,8},{20,12},{24,16},{28,20},{9,1},{13,5},{17,9},{2... | collective-permute-start | bytes 589832 | tf_op jit(solution)/shard_map/ppermute | solution.py:421
  568.8 54.6 %copy-start.36 = (f32[1024]{0:T(1024)S(1)}, f32[1024]{0:T(1024)}, u32[]{:S(2)}) copy-start(f32[1024]{0:T(1024)} %copy-done.35) | copy-start | bytes 12292
  568.8 54.7 %copy-start.41 = (f32[1536]{0:T(1024)S(1)}, f32[1536]{0:T(1024)}, u32[]{:S(2)}) copy-start(f32[1536]{0:T(1024)} %copy-done.40) | copy-start | bytes 18436
  621.7 6.0 collective-permute-start.9
  627.5 258.1 %reduce-scatter.29.cloned.1.call-start = ((), (), s32[]{:S(2)}) async-start(), calls=%async_computation.17 | async-start | bytes 811008 | tf_op jit(solution)/shard_map/reduce_scatter | solution.py:864
  632.4 325.3 %reduce-scatter.31.cloned.1.call-start = ((), (), s32[]{:S(2)}) async-start(), calls=%async_computation.18 | async-start | bytes 2654208 | tf_op jit(solution)/shard_map/reduce_scatter | solution.py:679
  638.9 391.1 %reduce-scatter.25.cloned.1.call-start = ((), (), s32[]{:S(2)}) async-start(), calls=%async_computation.15 | async-start | bytes 2654208 | tf_op jit(solution)/shard_map/reduce_scatter | solution.py:679
  645.7 456.5 %reduce-scatter.27.cloned.1.call-start = ((), (), s32[]{:S(2)}) async-start(), calls=%async_computation.16 | async-start | bytes 2654208 | tf_op jit(solution)/shard_map/reduce_scatter | solution.py:679
  653.1 488.6 %reduce-scatter.41.cloned.1.call-start = ((), (), s32[]{:S(2)}) async-start(), calls=%async_computation.23 | async-start | bytes 3932160
  675.0 46.0 %copy-start.45 = (f32[1,768]{1,0:T(1,128)S(1)}, f32[1,768]{1,0:T(1,128)}, u32[]{:S(2)}) copy-start(f32[1,768]{1,0:T(1,128)} %get-tuple-element.74) | copy-start | bytes 9220
  675.0 46.0 %copy-start.31 = (f32[8,1024]{1,0:T(8,128)S(1)}, f32[8,1024]{1,0:T(8,128)}, u32[]{:S(2)}) copy-start(f32[8,1024]{1,0:T(8,128)} %get-tuple-element.72) | copy-start | bytes 98308
  675.0 46.1 %copy-start.47 = (f32[8,128]{1,0:T(8,128)S(1)}, f32[8,128]{1,0:T(8,128)}, u32[]{:S(2)}) copy-start(f32[8,128]{1,0:T(8,128)} %get-tuple-element.73) | copy-start | bytes 12292
  675.0 87.0 %copy-start.17 = (bf16[1024,128]{1,0:T(8,128)(2,1)S(1)}, bf16[1024,128]{1,0:T(8,128)(2,1)}, u32[]{:S(2)}) copy-start(bf16[1024,128]{1,0:T(8,128)(2,1)} %get-tuple-element.71) | copy-start | bytes 786436
  886.9 257.0 %copy-start.34 = (f32[384]{0:T(512)S(1)}, f32[384]{0:T(512)}, u32[]{:S(2)}) copy-start(f32[384]{0:T(512)} %param.34) | copy-start | bytes 4612
  886.9 257.0 %copy-start.39 = (f32[384]{0:T(512)S(1)}, f32[384]{0:T(512)}, u32[]{:S(2)}) copy-start(f32[384]{0:T(512)} %param.21) | copy-start | bytes 4612
  (28 other events, 119.9 us)
Sparse Core Ops, SparseCore 0:
  9.6 31.2 all-gather.4
  117.9 39.4 reduce-scatter.34
  162.3 28.5 all-gather.6
  192.3 28.4 all-gather.8
  459.1 34.1 reduce-scatter.38
  499.5 28.4 all-gather.10
  531.4 64.9 reduce-scatter.44
  598.9 36.8 reduce-scatter.36
  639.5 79.4 reduce-scatter.32
  722.7 61.8 reduce-scatter.42
  790.2 95.3 reduce-scatter.28
  888.9 68.6 reduce-scatter.30
  961.1 68.8 reduce-scatter.24
  1033.3 68.7 reduce-scatter.26
  1104.5 37.0 reduce-scatter.40

commit v2 on v1

--- a/solution.py
+++ b/solution.py
@@ -441,8 +441,8 @@
         return jnp.maximum(order(i) * per - 1, 0)
 
     return [
-        pl.BlockSpec((SPAN, inner), lambda i, *unused: (order(i), 1)),
-        pl.BlockSpec((8, inner), lambda i, *unused: (before(i), 1)),
+        pl.BlockSpec((SPAN, inner), lambda i, *unused: (order(i), 0)),
+        pl.BlockSpec((8, inner), lambda i, *unused: (before(i), 0)),
         pl.BlockSpec((SPAN, bc_width + LANES), lambda i, *unused: (order(i), 0)),
         pl.BlockSpec((8, bc_width + LANES), lambda i, *unused: (before(i), 0)),
         fixed((8, channels)),
@@ -691,6 +691,467 @@
     return lax.dot_general(a, b, (((0,), (0,)), ((), ())), preferred_element_type=f32).astype(kind)
 
 
+MESH = pl.DeviceIdType.MESH
+
+
+class HeadPlace:
+    def __init__(self, count):
+        self.count = count
+        self.chips = count // 2
+        self.me = lax.axis_index("head")
+        self.core = lax.rem(self.me, 2)
+        self.chip = self.me // 2
+        self.partner = self.chip * 2 + (1 - self.core)
+
+    def ahead(self, step):
+        return lax.rem(self.chip + step, self.chips) * 2 + self.core
+
+    def behind(self, step):
+        return lax.rem(self.chip + self.chips - step, self.chips) * 2 + self.core
+
+    def meet(self):
+        barrier = pltpu.get_barrier_semaphore()
+        others = [self.partner] + [self.ahead(step) for step in range(1, self.chips)]
+        for other in others:
+            pl.semaphore_signal(barrier, inc=1, device_id={"head": other}, device_id_type=MESH)
+        pl.semaphore_wait(barrier, len(others))
+
+
+def remote(source, target, send, receive, device):
+    return pltpu.make_async_remote_copy(
+        src_ref=source, dst_ref=target, send_sem=send, recv_sem=receive,
+        device_id={"head": device}, device_id_type=MESH,
+    )
+
+
+class TwoLevelGather:
+    def __init__(self, place, own_at, full_at, send, receive, parts):
+        self.place, self.own_at, self.full_at = place, own_at, full_at
+        self.send, self.receive, self.parts = send, receive, parts
+
+    def copy(self, kind, part):
+        place = self.place
+        slot = kind * self.parts + part
+        send, receive = self.send.at[slot], self.receive.at[slot]
+        if kind == 0:
+            return remote(self.own_at(part), self.full_at(place.me, part), send, receive, place.partner)
+        if kind < place.chips:
+            return remote(self.own_at(part), self.full_at(place.me, part), send, receive, place.ahead(kind))
+        origin = place.behind(kind - place.chips + 1)
+        return remote(self.full_at(origin, part), self.full_at(origin, part), send, receive, place.partner)
+
+    def kinds(self):
+        return 2 * self.place.chips - 1
+
+    def start(self, part):
+        for kind in list(range(1, self.place.chips)) + [0]:
+            self.copy(kind, part).start()
+
+    def arrive(self, part):
+        for step in range(1, self.place.chips):
+            self.copy(step, part).wait_recv()
+            self.copy(self.place.chips + step - 1, part).start()
+        self.copy(0, part).wait_recv()
+        for step in range(1, self.place.chips):
+            self.copy(self.place.chips + step - 1, part).wait_recv()
+
+    def finish(self, part):
+        for kind in range(self.kinds()):
+            self.copy(kind, part).wait_send()
+
+
+class ScalarSum:
+    def __init__(self, place, own, near, pair, far, send, receive):
+        self.place, self.own, self.near, self.pair, self.far = place, own, near, pair, far
+        self.send, self.receive = send, receive
+
+    def first(self):
+        return remote(self.own, self.near, self.send.at[0], self.receive.at[0], self.place.partner)
+
+    def second(self, step):
+        return remote(
+            self.pair, self.far.at[step - 1], self.send.at[step], self.receive.at[step], self.place.ahead(step)
+        )
+
+    def start(self):
+        self.first().start()
+
+    def middle(self):
+        self.first().wait_recv()
+        self.pair[...] = self.own[...] + self.near[...]
+        for step in range(1, self.place.chips):
+            self.second(step).start()
+
+    def total(self):
+        total = self.pair[...]
+        for step in range(1, self.place.chips):
+            self.second(step).wait_recv()
+            total = total + self.far[step - 1]
+        return total
+
+    def finish(self):
+        self.first().wait_send()
+        for step in range(1, self.place.chips):
+            self.second(step).wait_send()
+
+
+def column_of(line):
+    rows = line.shape[1]
+    pick = (lax.broadcasted_iota(jnp.int32, (8, LANES), 0) == 0).astype(f32)
+    return dot_tn(jnp.broadcast_to(line, (8, rows)), pick, highest)
+
+
+def gather_sems(chips, parts):
+    slots = (2 * chips - 1) * parts
+    return [pltpu.SemaphoreType.DMA((slots,)), pltpu.SemaphoreType.DMA((slots,))]
+
+
+def scalar_scratch(chips, dense):
+    return [
+        pltpu.VMEM((dense, LANES), f32),
+        pltpu.VMEM((dense, LANES), f32),
+        pltpu.VMEM((max(chips - 1, 1), dense, LANES), f32),
+        pltpu.SemaphoreType.DMA((chips,)),
+        pltpu.SemaphoreType.DMA((chips,)),
+    ]
+
+
+def comm_params(ident):
+    return pltpu.CompilerParams(vmem_limit_bytes=VMEM_LIMIT, collective_id=ident, has_side_effects=True)
+
+
+VMEM = pl.BlockSpec(memory_space=pltpu.VMEM)
+CHUNK = 256
+
+
+def first_gather_kernel(
+    count, products, tokens_ref, gain_ref, *refs
+):
+    weights, (full_ref, rms_ref), outs = refs[:products], refs[products : products + 2], refs[products + 2 : 2 * products + 2]
+    raw, gains, send, receive, gsend, greceive = refs[2 * products + 2 :]
+    rows, features = tokens_ref.shape
+    place = HeadPlace(count)
+    parts = rows // CHUNK
+
+    def rows_of(part):
+        return pl.ds(pl.multiple_of(part * CHUNK, CHUNK), CHUNK)
+
+    data = TwoLevelGather(
+        place, lambda part: tokens_ref.at[rows_of(part)], lambda who, part: raw.at[who, rows_of(part)],
+        send, receive, parts,
+    )
+    gain = TwoLevelGather(place, lambda part: gain_ref, lambda who, part: gains.at[who], gsend, greceive, 1)
+    place.meet()
+    gain.start(0)
+    lax.fori_loop(0, parts, lambda part, unused: (data.start(part), unused)[1], 0)
+    gains[place.me] = gain_ref[...]
+    raw[place.me] = tokens_ref[...]
+    gain.arrive(0)
+
+    def step(part, unused):
+        data.arrive(part)
+        where = rows_of(part)
+        values = [raw[who, where, :].astype(f32) for who in range(count)]
+        total = sum(jnp.sum(value * value, axis=1, keepdims=True) for value in values)
+        scale = lax.rsqrt(total / (count * features) + epsilon)
+        rms_ref[where, :] = jnp.broadcast_to(scale, (CHUNK, 8))
+        sums = [jnp.zeros((CHUNK, out.shape[1]), f32) for out in outs]
+        for who in range(count):
+            normed = (values[who] * scale * gains[who, 0:1, :]).astype(bf16)
+            full_ref[who, where, :] = normed
+            inner_rows = slice(who * features, (who + 1) * features)
+            sums = [value + dot_nn(normed, weight[inner_rows, :]) for value, weight in zip(sums, weights)]
+        for out, value in zip(outs, sums):
+            out[where, :] = value
+        return unused
+
+    lax.fori_loop(0, parts, step, 0)
+    gain.finish(0)
+    lax.fori_loop(0, parts, lambda part, unused: (data.finish(part), unused)[1], 0)
+
+
+def first_gather(tokens, gain, weights, ident):
+    rows, features = tokens.shape
+    count = D // features
+    chips = count // 2
+    return pl.pallas_call(
+        partial(first_gather_kernel, count, len(weights)),
+        in_specs=[VMEM] * (2 + len(weights)),
+        out_specs=[VMEM] * (2 + len(weights)),
+        out_shape=[
+            jax.ShapeDtypeStruct((count, rows, features), bf16),
+            jax.ShapeDtypeStruct((rows, 8), f32),
+        ]
+        + [jax.ShapeDtypeStruct((rows, weight.shape[1]), f32) for weight in weights],
+        scratch_shapes=[
+            pltpu.VMEM((count, rows, features), bf16),
+            pltpu.VMEM((count, 8, features), f32),
+        ]
+        + gather_sems(chips, rows // CHUNK)
+        + gather_sems(chips, 1),
+        compiler_params=comm_params(ident),
+        cost_estimate=cost(2 * rows * D * sum(weight.shape[1] for weight in weights), 30e6),
+        name="first_gather",
+    )(tokens, fit(gain[None], 8, 0), *weights)
+
+
+def gather_kernel(
+    count, transposed, scaled, own_ref, dense_ref, weight_ref,
+    full_ref, total_ref, out_ref,
+    send, receive, near, pair, far, ssend, sreceive,
+):
+    rows, features = own_ref.shape
+    place = HeadPlace(count)
+    parts = rows // CHUNK
+
+    def rows_of(part):
+        return pl.ds(pl.multiple_of(part * CHUNK, CHUNK), CHUNK)
+
+    data = TwoLevelGather(
+        place, lambda part: own_ref.at[rows_of(part)], lambda who, part: full_ref.at[who, rows_of(part)],
+        send, receive, parts,
+    )
+    scalars = ScalarSum(place, dense_ref, near, pair, far, ssend, sreceive)
+    place.meet()
+    scalars.start()
+    lax.fori_loop(0, parts, lambda part, unused: (data.start(part), unused)[1], 0)
+    scalars.middle()
+    full_ref[place.me] = own_ref[...]
+    total = scalars.total()
+    total_ref[...] = total
+    if scaled:
+        near[...] = lax.rsqrt(total / (count * features) + epsilon)
+
+    def step(part, unused):
+        data.arrive(part)
+        where = rows_of(part)
+        out = jnp.zeros((CHUNK, out_ref.shape[1]), f32)
+        for who in range(count):
+            piece = full_ref[who, where, :]
+            if transposed:
+                out = out + dot_nt(piece, weight_ref[:, who * features : (who + 1) * features])
+            else:
+                out = out + dot_nn(piece, weight_ref[who * features : (who + 1) * features, :])
+        if scaled:
+            per = CHUNK // LANES
+            line = jnp.concatenate([near[pl.ds(part * per + i, 1), :] for i in range(per)], axis=1)
+            out = out * column_of(line)[:, 0:1]
+        out_ref[where, :] = out.astype(out_ref.dtype)
+        return unused
+
+    lax.fori_loop(0, parts, step, 0)
+    scalars.finish()
+    lax.fori_loop(0, parts, lambda part, unused: (data.finish(part), unused)[1], 0)
+
+
+def gather_matmul(own, sums, weight, transposed, scaled, ident, name):
+    rows, features = own.shape
+    count = D // features
+    chips = count // 2
+    columns = weight.shape[0 if transposed else 1]
+    dense = rows // LANES
+    return pl.pallas_call(
+        partial(gather_kernel, count, transposed, scaled),
+        in_specs=[VMEM] * 3,
+        out_specs=[VMEM] * 3,
+        out_shape=[
+            jax.ShapeDtypeStruct((count, rows, features), bf16),
+            jax.ShapeDtypeStruct((dense, LANES), f32),
+            jax.ShapeDtypeStruct((rows, columns), bf16),
+        ],
+        scratch_shapes=gather_sems(chips, rows // CHUNK) + scalar_scratch(chips, dense),
+        compiler_params=comm_params(ident),
+        cost_estimate=cost(2 * rows * D * columns, 20e6),
+        name=name,
+    )(own, sums.reshape(dense, LANES), weight)
+
+
+def scatter_kernel(count, operands, transposed, *refs):
+    lefts, rights = refs[:operands], refs[operands : 2 * operands]
+    dense_ref, out_ref, total_ref = refs[2 * operands : 2 * operands + 3]
+    (own, near_data, sent, far_data, psend, preceive, xsend, xreceive,
+     near, pair, far, ssend, sreceive) = refs[2 * operands + 3 :]
+    rows, features = out_ref.shape
+    place = HeadPlace(count)
+    chips = place.chips
+    parts = rows // CHUNK
+
+    def rows_of(part):
+        return pl.ds(pl.multiple_of(part * CHUNK, CHUNK), CHUNK)
+
+    def to_partner(chip, part):
+        slot = chip * parts + part
+        return remote(
+            own.at[chip * 2 + 1 - place.core, rows_of(part)], near_data.at[chip, rows_of(part)],
+            psend.at[slot], preceive.at[slot], place.partner,
+        )
+
+    def across(step, part):
+        slot = (step - 1) * parts + part
+        return remote(
+            sent.at[step - 1, rows_of(part)], far_data.at[step - 1, rows_of(part)],
+            xsend.at[slot], xreceive.at[slot], place.ahead(step),
+        )
+
+    scalars = ScalarSum(place, dense_ref, near, pair, far, ssend, sreceive)
+    place.meet()
+    scalars.start()
+
+    def compute(part):
+        where = rows_of(part)
+        for who in range(count):
+            inner = slice(who * features, (who + 1) * features)
+            value = jnp.zeros((CHUNK, features), f32)
+            for left, right in zip(lefts, rights):
+                if transposed:
+                    value = value + dot_nt(left[where, :], right[inner, :])
+                else:
+                    value = value + dot_nn(left[where, :], right[:, inner])
+            own[who, where, :] = value.astype(bf16)
+        for chip in range(chips):
+            to_partner(chip, part).start()
+
+    def combine(part):
+        where = rows_of(part)
+        for chip in range(chips):
+            to_partner(chip, part).wait_recv()
+        for step in range(1, chips):
+            chip = lax.rem(place.chip + step, chips)
+            mine = own[chip * 2 + place.core, where, :].astype(f32)
+            sent[step - 1, where, :] = (mine + near_data[chip, where, :].astype(f32)).astype(bf16)
+            across(step, part).start()
+
+    compute(0)
+    scalars.middle()
+
+    def forward(part, unused):
+        compute(part)
+        combine(part - 1)
+        return unused
+
+    lax.fori_loop(1, parts, forward, 0)
+    combine(parts - 1)
+    total_ref[...] = scalars.total()
+
+    def collect(part, unused):
+        where = rows_of(part)
+        value = own[place.me, where, :].astype(f32) + near_data[place.chip, where, :].astype(f32)
+        for step in range(1, chips):
+            across(step, part).wait_recv()
+            value = value + far_data[step - 1, where, :].astype(f32)
+        out_ref[where, :] = value
+        return unused
+
+    lax.fori_loop(0, parts, collect, 0)
+    scalars.finish()
+
+    def drain(part, unused):
+        for chip in range(chips):
+            to_partner(chip, part).wait_send()
+        for step in range(1, chips):
+            across(step, part).wait_send()
+        return unused
+
+    lax.fori_loop(0, parts, drain, 0)
+
+
+def matmul_scatter(lefts, rights, sums, transposed, count, ident, name):
+    rows = lefts[0].shape[0]
+    features = D // count
+    chips = count // 2
+    dense = rows // LANES
+    parts = rows // CHUNK
+    flops = sum(2 * rows * D * left.shape[1] for left in lefts)
+    return pl.pallas_call(
+        partial(scatter_kernel, count, len(lefts), transposed),
+        in_specs=[VMEM] * (2 * len(lefts) + 1),
+        out_specs=[VMEM] * 2,
+        out_shape=[
+            jax.ShapeDtypeStruct((rows, features), f32),
+            jax.ShapeDtypeStruct((dense, LANES), f32),
+        ],
+        scratch_shapes=[
+            pltpu.VMEM((count, rows, features), bf16),
+            pltpu.VMEM((chips, rows, features), bf16),
+            pltpu.VMEM((max(chips - 1, 1), rows, features), bf16),
+            pltpu.VMEM((max(chips - 1, 1), rows, features), bf16),
+            pltpu.SemaphoreType.DMA((chips * parts,)),
+            pltpu.SemaphoreType.DMA((chips * parts,)),
+            pltpu.SemaphoreType.DMA((max(chips - 1, 1) * parts,)),
+            pltpu.SemaphoreType.DMA((max(chips - 1, 1) * parts,)),
+        ]
+        + scalar_scratch(chips, dense),
+        compiler_params=comm_params(ident),
+        cost_estimate=cost(flops, 20e6),
+        name=name,
+    )(*lefts, *rights, sums.reshape(dense, LANES))
+
+
+def weight_grad_kernel(products, left_ref, *refs):
+    left = left_ref[...]
+    for right, out in zip(refs[:products], refs[products:]):
+        out[...] = dot_tn(left, right[...]).astype(out.dtype)
+
+
+def weight_grad(full, rights, name):
+    count, rows, features = full.shape
+    columns = [right.shape[1] for right in rights]
+    return pl.pallas_call(
+        partial(weight_grad_kernel, len(rights)),
+        grid=(count,),
+        in_specs=[pl.BlockSpec((None, rows, features), lambda i: (i, 0, 0))] + [fixed((rows, n)) for n in columns],
+        out_specs=[pl.BlockSpec((features, n), lambda i: (i, 0)) for n in columns],
+        out_shape=[jax.ShapeDtypeStruct((count * features, n), bf16) for n in columns],
+        compiler_params=params(),
+        cost_estimate=cost(2 * rows * D * sum(columns), 2 * (rows + D) * (D + sum(columns))),
+        name=name,
+    )(full, *rights)
+
+
+def gathered_product_kernel(full_ref, weight_ref, out_ref):
+    count, rows, features = full_ref.shape
+    value = jnp.zeros(out_ref.shape, f32)
+    for who in range(count):
+        value = value + dot_nt(full_ref[who], weight_ref[:, who * features : (who + 1) * features])
+    out_ref[...] = value.astype(out_ref.dtype)
+
+
+def gathered_product(full, weight, name):
+    count, rows, features = full.shape
+    columns = weight.shape[0]
+    return pl.pallas_call(
+        gathered_product_kernel,
+        grid=(rows // CHUNK,),
+        in_specs=[pl.BlockSpec((count, CHUNK, features), lambda i: (0, i, 0)), fixed(weight.shape)],
+        out_specs=pl.BlockSpec((CHUNK, columns), lambda i: (i, 0)),
+        out_shape=jax.ShapeDtypeStruct((rows, columns), bf16),
+        compiler_params=params(),
+        cost_estimate=cost(2 * rows * D * columns, 2 * (rows * D + D * columns + rows * columns)),
+        name=name,
+    )(full, weight)
+
+
+def spread_product_kernel(left_ref, weight_ref, out_ref):
+    features = out_ref.shape[2]
+    for who in range(out_ref.shape[0]):
+        out_ref[who] = dot_nn(left_ref[...], weight_ref[:, who * features : (who + 1) * features]).astype(out_ref.dtype)
+
+
+def spread_product(left, weight, count, name):
+    rows, depth = left.shape
+    features = weight.shape[1] // count
+    return pl.pallas_call(
+        spread_product_kernel,
+        grid=(rows // CHUNK,),
+        in_specs=[pl.BlockSpec((CHUNK, depth), lambda i: (i, 0)), fixed(weight.shape)],
+        out_specs=pl.BlockSpec((count, CHUNK, features), lambda i: (0, i, 0)),
+        out_shape=jax.ShapeDtypeStruct((count, rows, features), bf16),
+        compiler_params=params(),
+        cost_estimate=cost(2 * rows * D * depth, 2 * (rows * D + D * depth + rows * depth)),
+        name=name,
+    )(left, weight)
+
+
 def per_device(
     tokens, segment_ids, first_gain, proj_zx, proj_bc, proj_step, conv_inner, conv_inner_bias,
     conv_state, conv_state_bias, step_bias, decay_log, skip_scale, gated_gain, proj_out,
@@ -736,55 +1197,56 @@
         wide,
         tall,
     )
-    zx_weight = proj_zx.reshape(D, 2 * inner)
+    count = lax.axis_size("head")
+    gate_weight, inner_weight = proj_zx[:, 0, :], proj_zx[:, 1, :]
     bcs_weight = jnp.concatenate([proj_bc, fit(proj_step, LANES, 1)], axis=1)
     qkv_weight = fit(proj_qkv, att_pad, 2).reshape(D, 3 * att_pad)
     att_weight = fit(attention_out, att_pad, 0)
 
-    gains = lax.all_gather(jnp.stack([first_gain, second_gain]), "head", axis=1, tiled=True)
-    token_full = head_gather(tokens).astype(f32)
-    first_rms = lax.rsqrt(jnp.sum(token_full * token_full, axis=1) / D + epsilon)
-    first_full = (token_full * first_rms[:, None] * gains[0]).astype(bf16)
-    cot_full = head_gather(cotangent)
-    zx = matmul(first_full, zx_weight)
-    bcs = matmul(first_full, bcs_weight)
-    edge_rows = jnp.concatenate([zx[rows - 8 :, inner:], bcs[rows - 8 :, :bc_width]], axis=1)
+    first_full, first_rms, zed, inner_x, bcs = first_gather(
+        tokens, first_gain, (gate_weight, inner_weight, bcs_weight), 0
+    )
+    first_rms = first_rms[:, 0:1]
+    cot_full = lax.all_gather(cotangent, "head")
+    edge_rows = jnp.concatenate([inner_x[rows - 8 :], bcs[rows - 8 :, :bc_width]], axis=1)
     edge = from_behind(edge_rows, "seq", 1)
 
-    ssd_shared = (span_prev, span_last, zx, bcs, edge, kept, segc, segr)
+    ssd_shared = (span_prev, span_last, inner_x, bcs, edge, kept, segc, segr)
     y_zero, state_c, opened, states, end_state, through = ssd_forward(*ssd_shared, constants, inner, width)
-    through_rows = jnp.broadcast_to(jnp.repeat(through[0, :heads], SSM_DIM)[:, None], (inner, width))
 
     sent = end_state.astype(bf16)
-    near = from_behind(sent, "seq", 1).astype(f32)
     packed = jnp.concatenate([sent, jnp.broadcast_to(through[0:1], (8, LANES)).astype(bf16)], axis=0)
     near_pack = from_behind(packed, "seq", 1).astype(f32)
-    near = near_pack[:inner]
     near_through = jnp.repeat(near_pack[inner, :heads], SSM_DIM)[:, None]
     far = from_behind(sent, "seq", 2).astype(f32)
-    entering = (near + near_through * far).astype(bf16)
-
-    ssd_out, gated_raw, gate_sums = gate_forward(y_zero, state_c, opened, entering, zx, gated_gain[None], wide)
-    gate_total = lax.psum(gate_sums[0], "head")
-    gate_rms = lax.rsqrt(gate_total / INNER + epsilon)
-    branch_part = matmul(gated_raw, proj_out, bf16)
-    branch = head_scatter(branch_part).astype(f32) * gate_rms[:, None]
+    entering = (near_pack[:inner] + near_through * far).astype(bf16)
+
+    ssd_out, gated_raw, gate_sums = gate_forward(y_zero, state_c, opened, entering, zed, gated_gain[None], wide)
+    branch_raw, gate_total = matmul_scatter(
+        (gated_raw,), (proj_out,), gate_sums[0], False, count, 1, "branch_scatter"
+    )
+    gate_rms = lax.rsqrt(gate_total.reshape(rows, 1) / INNER + epsilon)
+    branch = branch_raw * gate_rms
     hidden_zero = tokens.astype(f32)
     hidden_one = hidden_zero + branch
-    second_total = lax.psum(jnp.sum(hidden_one * hidden_one, axis=1), "head")
-    second_rms = lax.rsqrt(second_total / D + epsilon)
-    second_full = head_gather((hidden_one * second_gain).astype(bf16))
-    projected = (matmul(second_full, qkv_weight) * second_rms[:, None]).astype(bf16)
+    second_full, second_total, projected = gather_matmul(
+        (hidden_one * second_gain).astype(bf16), jnp.sum(hidden_one * hidden_one, axis=1),
+        qkv_weight, False, True, 2, "second_gather",
+    )
+    second_rms = lax.rsqrt(second_total.reshape(rows, 1) / D + epsilon)
     key_value = projected[:, att_pad:]
     moved = [from_behind(key_value, "seq", back) for back in range(1, reach + 1)]
 
-    back_attended = matmul_nt(cot_full, att_weight, bf16)
+    back_attended = gathered_product(cot_full, att_weight, "back_attended")
     pieces = [(projected, pairs)] + [(array, 0) for array in moved]
     attended, back_query, back_key, back_value, *back_moved = attention(
         low_blocks, projected, back_attended, pieces, segc_window, segr, att_pad, rows
     )
-    output = (hidden_one + head_scatter(matmul(attended, att_weight, bf16)).astype(f32)).astype(bf16)
-    grad_attention_out = matmul_tn(cot_full, attended[:, :att], bf16)
+    out_part = spread_product(attended, att_weight, count, "output_product")
+    output = (
+        hidden_one + lax.psum_scatter(out_part, "head", scatter_dimension=0).astype(f32)
+    ).astype(bf16)
+    (grad_att,) = weight_grad(cot_full, (attended,), "grad_attention_out")
 
     for back in range(1, reach + 1):
         pair = jnp.concatenate(back_moved[2 * back - 2 : 2 * back], axis=1)
@@ -792,29 +1254,32 @@
         back_key = back_key + pair[:, :att_pad]
         back_value = back_value + pair[:, att_pad:]
     back_projected = jnp.concatenate([back_query, back_key, back_value], axis=1).astype(bf16)
-    back_second = head_scatter(matmul_nt(back_projected, qkv_weight, bf16)).astype(f32)
-    second_dots = lax.psum(jnp.sum(back_projected.astype(f32) * projected.astype(f32), axis=1), "head")
-    grad_qkv = matmul_tn(
-        second_full, (back_projected.astype(f32) * second_rms[:, None]).astype(bf16), bf16
+    second_sums = jnp.sum(back_projected.astype(f32) * projected.astype(f32), axis=1)
+    back_second, second_dots = matmul_scatter(
+        (back_projected,), (qkv_weight,), second_sums, True, count, 3, "second_scatter"
+    )
+    (grad_qkv,) = weight_grad(
+        second_full, ((back_projected.astype(f32) * second_rms).astype(bf16),), "grad_qkv"
     )
     if att != att_pad:
+        grad_att = grad_att[:, :att]
         grad_qkv = grad_qkv.reshape(D, 3, att_pad)[:, :, :att].reshape(D, 3 * att)
-    normed_one = hidden_one * second_rms[:, None]
-    grad_second_gain = jnp.sum(normed_one * back_second, axis=0)
+    grad_second_gain = jnp.sum(hidden_one * second_rms * back_second, axis=0)
     back_hidden_one = (
         cotangent.astype(f32)
-        + second_rms[:, None] * second_gain * back_second
-        - hidden_one * (second_rms * second_rms / D * second_dots)[:, None]
+        + second_rms * second_gain * back_second
+        - hidden_one * (second_rms * second_rms / D * second_dots.reshape(rows, 1))
     )
     back_low = back_hidden_one.astype(bf16)
-    back_branch = head_gather(back_low)
-    back_gated = matmul_nt(back_branch, proj_out, bf16)
-    gate_dots = lax.psum(jnp.sum(back_low.astype(f32) * branch, axis=1), "head")
-    coefficients = fit(jnp.stack([gate_rms, gate_rms * gate_rms / INNER * gate_dots], axis=1), 8, 1)
+    back_branch, gate_dots, back_gated = gather_matmul(
+        back_low, jnp.sum(back_low.astype(f32) * branch, axis=1), proj_out, True, False, 4, "branch_gather"
+    )
+    coefficients = fit(
+        jnp.concatenate([gate_rms, gate_rms * gate_rms / INNER * gate_dots.reshape(rows, 1)], axis=1), 8, 1
+    )
     dy, back_z, gated, grad_gated_gain, back_entering = gate_backward(
-        back_gated, ssd_out, zx, coefficients, gated_gain[None], state_c, opened, wide
-    )
-    grad_out = matmul_tn(back_branch, gated, bf16)
+        back_gated, ssd_out, zed, coefficients, gated_gain[None], state_c, opened, wide
+    )
 
     back_sent = back_entering.astype(bf16)
     back_pack = jnp.concatenate([back_sent, jnp.broadcast_to(through[0:1], (8, LANES)).astype(bf16)], axis=0)
@@ -822,6 +1287,8 @@
     back_far = from_behind(back_sent, "seq", -2).astype(f32)
     back_near_through = jnp.repeat(back_near_pack[inner, :heads], SSM_DIM)[:, None]
     back_end = back_near_pack[:inner] + back_near_through * back_far
+    (grad_out,) = weight_grad(back_branch, (gated,), "grad_out")
+    (grad_gate,) = weight_grad(first_full, (back_z,), "grad_gate")
 
     back_x, back_bc, back_step, tail_rows, back_edge, grad_conv, grad_heads = ssd_backward(
         *ssd_shared, dy, states, opened, entering, back_end, constants, inner, width
@@ -829,50 +1296,46 @@
     tail_rows = (tail_rows + from_behind(back_edge, "seq", -1)).astype(bf16)
     back_x = lax.dynamic_update_slice(back_x, tail_rows[:, :inner], (rows - 8, 0))
     back_bc = lax.dynamic_update_slice(back_bc, tail_rows[:, inner:], (rows - 8, 0))
-
-    first_part = (
-        matmul_nt(back_z, zx_weight[:, :inner])
-        + matmul_nt(back_x, zx_weight[:, inner:])
-        + matmul_nt(back_bc, proj_bc)
-        + matmul_nt(back_step, bcs_weight[:, bc_width:])
-    ).astype(bf16)
-    back_first = head_scatter(first_part).astype(f32)
-    first_dots = lax.psum(
-        jnp.sum(back_z.astype(f32) * zx[:, :inner], axis=1)
-        + jnp.sum(back_x.astype(f32) * zx[:, inner:], axis=1)
+    grad_inner, grad_bc, grad_step = weight_grad(first_full, (back_x, back_bc, back_step), "grad_inner")
+    first_sums = (
+        jnp.sum(back_z.astype(f32) * zed, axis=1)
+        + jnp.sum(back_x.astype(f32) * inner_x, axis=1)
         + jnp.sum(back_bc.astype(f32) * bcs[:, :bc_width], axis=1)
-        + jnp.sum(back_step.astype(f32) * bcs[:, bc_width:], axis=1),
-        "head",
-    )
-    grad_zx_gate = matmul_tn(first_full, back_z, bf16)
-    grad_zx_inner = matmul_tn(first_full, back_x, bf16)
-    grad_bc = matmul_tn(first_full, back_bc, bf16)
-    grad_step = matmul_tn(first_full, back_step)[:, :heads].astype(bf16)
-    grad_first_gain = jnp.sum(hidden_zero * first_rms[:, None] * back_first, axis=0)
+        + jnp.sum(back_step.astype(f32) * bcs[:, bc_width:], axis=1)
+    )
+    back_first, first_dots = matmul_scatter(
+        (back_z, back_x, back_bc, back_step),
+        (gate_weight, inner_weight, proj_bc, bcs_weight[:, bc_width:]),
+        first_sums, True, count, 5, "first_scatter",
+    )
+    grad_first_gain = jnp.sum(hidden_zero * first_rms * back_first, axis=0)
     grad_tokens = (
         back_hidden_one
-        + first_rms[:, None] * first_gain * back_first
-        - hidden_zero * (first_rms * first_rms / D * first_dots)[:, None]
+        + first_rms * first_gain * back_first
+        - hidden_zero * (first_rms * first_rms / D * first_dots.reshape(rows, 1))
     ).astype(bf16)
 
+    wide_att = seq_scatter(grad_att).T
     wide_qkv = seq_scatter(grad_qkv).reshape(-1, 3, att)
-    wide_att = seq_scatter(grad_attention_out).T
     wide_out = seq_scatter(grad_out).T
-    wide_zx = jnp.stack([seq_scatter(grad_zx_gate), seq_scatter(grad_zx_inner)], axis=1)
-    wide_step = seq_scatter(grad_step)
-    both = ("seq", "head")
-    shared_bc = lax.psum_scatter(grad_bc, both, scatter_dimension=1, tiled=True).astype(f32)
-    shared_conv = lax.psum_scatter(grad_conv[:5, inner:], both, scatter_dimension=1, tiled=True)
+    wide_gate = seq_scatter(grad_gate)
+    wide_tail = seq_scatter(jnp.concatenate([grad_inner, grad_step], axis=1))
+    wide_zx = jnp.stack([wide_gate, wide_tail[:, :inner]], axis=1)
+    wide_step = wide_tail[:, inner : inner + heads]
+    shared_bc = lax.psum_scatter(grad_bc, ("seq", "head"), scatter_dimension=1, tiled=True).astype(f32)
     small = lax.psum(
         (
             grad_first_gain,
-            grad_conv[:5, :inner],
+            grad_conv[:5],
             grad_heads[:3, :heads],
             grad_gated_gain[0],
             grad_second_gain,
         ),
         "seq",
     )
+    shared = bc_width // (lax.axis_size("seq") * count)
+    shared_at = (lax.axis_index("seq") * count + lax.axis_index("head")) * shared
+    shared_conv = lax.dynamic_slice_in_dim(lax.psum(small[1][:, inner:], "head"), shared_at, shared, 1)
     return (
         output,
         grad_tokens,
@@ -880,8 +1343,8 @@
         wide_zx,
         shared_bc,
         wide_step,
-        small[1][:4],
-        small[1][4],
+        small[1][:4, :inner],
+        small[1][4, :inner],
         shared_conv[:4],
         shared_conv[4],
         small[2][0],

time: 1190 us -> 1050 us (0.88)
  Pallas kernels: 138 us -> 366 us
  waiting for transfers between devices: 681 us -> 490 us
  matrix products: 96.1 us -> 0 us
  blocking collectives: 114 us -> 45.2 us
  local copies, waits for them, and re-layouts: 78.2 us -> 61.4 us
    pallas_call x0 -> x13, Pallas kernels: none -> 228 us  [the longest x3 82.7 us: matmul_scatter(): pl.pallas_call(partial(scatter_kernel, count, len(lefts), transposed), in...]
    dot_general x19 -> x0, matrix products: 96.1 us -> none  [the longest x7 40.2 us: matmul_tn(): lax.dot_general(a, b, (((0,), (0,)), ((), ())), preferred_element_type=f32)]
    unnamed x21 -> x9, waiting for transfers between devices: 105 us -> 41.7 us
    reduce_scatter x1, waiting for transfers between devices: 99.6 us -> 37.6 us  [per_device(): lax.psum_scatter(out_part, 'head', scatter_dimension=0).astype(f32)]
    unnamed x1 -> x0, blocking collectives: 40.3 us -> none
    unnamed x121 -> x98, local copies, waits for them, and re-layouts: 55.5 us -> 17.1 us
    all_gather x4 -> x1, waiting for transfers between devices: 38 us -> 0.01 us  [per_device(): cot_full = lax.all_gather(cotangent, 'head')]
    psum x6 -> x2, blocking collectives: 67.7 us -> 45.2 us  [the longest x1 39 us: per_device(): lax.psum((grad_first_gain, grad_conv[:5], grad_heads[:3, :heads], grad_ga...]
  transfers between devices with their start and end apart: 25 -> 18, of which waited for: 20 -> 14; matrix products, arithmetic and copies ran while one was open for 13% -> 8% of each run, Pallas kernels for 5% -> 27%
where the time goes in v2:
time: 1050 us; the launch traced here: 1060 us
  waiting for transfers between devices  490 us (47%)
  Pallas kernels  366 us (35%)
  local copies, waits for them, and re-layouts  61.4 us (6%)
  other arithmetic  52.4 us (5%)
  blocking collectives  45.2 us (4%)
  starting transfers between devices  27.5 us (3%)
  between operations  15.4 us (1%)
    reduce_scatter x5, waiting for transfers between devices, seq_scatter(): lax.psum_scatter(values.astype(bf16), 'seq', scatter_dimension=0, tiled=T...  243 us
    ppermute x10, waiting for transfers between devices, from_behind(): return lax.ppermute(value, axis, pairs)  167 us
    pallas_call x3, Pallas kernels, matmul_scatter(): pl.pallas_call(partial(scatter_kernel, count, len(lefts), transposed), in...  82.7 us
    pallas_call x2, Pallas kernels, gather_matmul(): pl.pallas_call(partial(gather_kernel, count, transposed, scaled), in_spec...  68.7 us
    pallas_call x1, Pallas kernels, ssd_backward(): pl.pallas_call(ssd_backward_kernel, grid_spec=pltpu.PrefetchScalarGridSpe...  52.8 us
    pallas_call x1, Pallas kernels, attention(): pl.pallas_call(partial(attention_kernel, scale=scale), grid_spec=pltpu.Pr...  46.2 us
    unnamed x9, waiting for transfers between devices  41.7 us
    psum x1, blocking collectives, per_device(): lax.psum((grad_first_gain, grad_conv[:5], grad_heads[:3, :heads], grad_ga...  39 us
  transfers between devices with their start and end apart: 18, of which 14 were waited for; matrix products, arithmetic and copies ran while one was open for 8% of the time, Pallas kernels for 27%

profile of v2, /device:TPU:0, one launch (start us, length us, event | category | flops | bytes accessed | tf_op | source)
XLA Modules:
  0.0 1057.4 jit_solution(7311631562530370574)
XLA Ops:
  7.3 10.7 %fusion.21 = (bf16[1536,1,768]{2,1,0:T(2,128)(2,1)}, bf16[1536,1,768]{2,1,0:T(2,128)(2,1)}) fusion(bf16[1536,2,768]{2,1,0:T(2,128)(2,1)} %param.22), kind=kLoop, calls=%fused_computation.96 | loop fusion | bytes 9437184 | tf_op jit(solution)/shard_map/slice | solution.py:1201
  18.3 6.8 copy_bitcast_fusion
  27.6 32.2 %first_gather.1 = (bf16[4,1024,384]{2,1,0:T(8,128)(2,1)}, f32[1024,8]{1,0:T(8,128)}, f32[1024,768]{1,0:T(8,128)}, f32[1024,768]{1,0:T(8,128)}, f32[1024,384]{1,0:T(8,128)}) custom-call(bf16[1024,384]{1,0:T(8,128)(2,1)} %tokens_ref.1, f32[8,384]{1,0:T(8,128)} %pad.26.gain_ref, bf16[1536,768]{1,0:T(8,128)(2,1)} %get-tuple-element.237.refs_0_.refs_4_, ...), custom_call_target="tpu_custom_call" | custom-call | flops 6039797760 | bytes 30000000 | tf_op jit(solution)/shard_map/first_gather/pallas_call | solution.py:877
  61.4 4.0 collective-permute-start
  74.0 19.5 %ssd_forward.1 = (f32[1024,768]{1,0:T(8,128)}, bf16[1024,128]{1,0:T(8,128)(2,1)}, f32[1024,128]{1,0:T(8,128)}, bf16[3072,128]{1,0:T(8,128)(2,1)}, f32[768,128]{1,0:T(8,128)}, /*index=5*/f32[8,128]{1,0:T(8,128)}) custom-call(s32[4]{0:T(128)} %bitcast.87, s32[4]{0:T(128)} %slice.135.last_ref, f32[1024,768]{1,0:T(8,128)} %get-tuple-element.67.x_ref.xprev_ref, ...), custom_call_target="tpu_custom_call" | custom-call | flops 1207959552 | bytes 9437184 | tf_op jit(solution)/shard_map/ssd_forward/pallas_call | solution.py:473
  95.9 4.1 collective-permute-start.1
  100.6 4.3 copy.106
  104.9 3.8 copy.107.weight_ref.refs_1_
  108.8 3.0 collective-permute-start.2
  112.9 2.9 collective-permute-done.2
  116.7 10.5 gate_forward.1
  128.5 26.0 %branch_scatter.1 = (f32[1024,384]{1,0:T(8,128)}, f32[8,128]{1,0:T(8,128)}) custom-call(bf16[1024,768]{1,0:T(8,128)(2,1)} %get-tuple-element.75.refs_0_, bf16[768,1536]{1,0:T(8,128)(2,1)} %weight_ref.5, f32[8,128]{1,0:T(8,128)} %bitcast.84), custom_call_target="tpu_custom_call" | custom-call | flops 2415919104 | bytes 20000000 | tf_op jit(solution)/shard_map/branch_scatter/pallas_call | solution.py:1065
  155.2 2.5 multiply_reduce_fusion.4
  158.8 36.2 %second_gather.1 = (bf16[4,1024,384]{2,1,0:T(8,128)(2,1)}, f32[8,128]{1,0:T(8,128)}, bf16[1024,1152]{1,0:T(8,128)(2,1)}) custom-call(bf16[1024,384]{1,0:T(8,128)(2,1)} %multiply_convert_fusion.own_ref, f32[8,128]{1,0:T(8,128)} %bitcast.86, bf16[1536,1152]{1,0:T(8,128)(2,1)} %copy.107.weight_ref.refs_1_), custom_call_target="tpu_custom_call" | custom-call | flops 3623878656 | bytes 20000000 | tf_op jit(solution)/shard_map/second_gather/pallas_call | solution.py:953
  196.5 4.6 collective-permute-start.3
  201.2 4.3 collective-permute-start.4
  209.0 5.4 back_attended.1.do_ref
  214.4 18.6 %collective-permute-done.3.k1_ref.v1_ref = bf16[1024,768]{1,0:T(8,128)(2,1)} collective-permute-done((bf16[1024,768]{1,0:T(8,128)(2,1)S(1)}, bf16[1024,768]{1,0:T(8,128)(2,1)}, u32[]{:S(2)}, u32[]{:S(2)}) %collective-permute-start.3) | collective-permute-done | bytes 1572896 | tf_op jit(solution)/shard_map/ppermute | solution.py:421
  233.0 4.0 collective-permute-done.4.k2_ref.v2_ref
  237.0 46.2 %attention.1 = (bf16[1024,384]{1,0:T(8,128)(2,1)}, f32[1024,384]{1,0:T(8,128)}, f32[1024,384]{1,0:T(8,128)}, f32[1024,384]{1,0:T(8,128)}, bf16[1024,384]{1,0:T(8...) custom-call(s32[12]{0:T(128)} %reshape.208.low_ref, ...), custom_call_target="tpu_custom_call" | custom-call | flops 11274289152 | bytes 11796480 | tf_op jit(solution)/shard_map/attention/pallas_call | solution.py:640
  283.2 2.8 pad_maximum_fusion.2
  290.2 5.2 grad_attention_out.1
  295.5 71.1 %collective-permute-done.5 = bf16[1024,768]{1,0:T(8,128)(2,1)} collective-permute-done((bf16[1024,768]{1,0:T(8,128)(2,1)}, bf16[1024,768]{1,0:T(8,128)(2,1)}, u32[]{:S(2)}, u32[]{:S(2)}) %collective-permute-start.5) | collective-permute-done | bytes 1572896 | tf_op jit(solution)/shard_map/ppermute | solution.py:421
  368.2 42.7 %collective-permute-done.6 = bf16[1024,768]{1,0:T(8,128)(2,1)} collective-permute-done((bf16[1024,768]{1,0:T(8,128)(2,1)}, bf16[1024,768]{1,0:T(8,128)(2,1)}, u32[]{:S(2)}, u32[]{:S(2)}) %collective-permute-start.6) | collective-permute-done | bytes 1572896 | tf_op jit(solution)/shard_map/ppermute | solution.py:421
  415.7 2.9 fusion.1
  418.7 27.4 %second_scatter.1 = (f32[1024,384]{1,0:T(8,128)}, f32[8,128]{1,0:T(8,128)}) custom-call(bf16[1024,1152]{1,0:T(8,128)(2,1)} %pad_maximum_fusion.1.refs_0_, bf16[1536,1152]{1,0:T(8,128)(2,1)} %copy.107.weight_ref.refs_1_, f32[8,128]{1,0:T(8,128)} %bitcast.81), custom_call_target="tpu_custom_call" | custom-call | flops 3623878656 | bytes 20000000 | tf_op jit(solution)/shard_map/second_scatter/pallas_call | solution.py:1065
  446.7 4.0 multiply_reduce_fusion.3
  450.7 32.5 %branch_gather.1 = (bf16[4,1024,384]{2,1,0:T(8,128)(2,1)}, f32[8,128]{1,0:T(8,128)}, bf16[1024,768]{1,0:T(8,128)(2,1)}) custom-call(bf16[1024,384]{1,0:T(8,128)(2,1)} %get-tuple-element.214.own_ref, f32[8,128]{1,0:T(8,128)} %bitcast.85, bf16[768,1536]{1,0:T(8,128)(2,1)} %weight_ref.5), custom_call_target="tpu_custom_call" | custom-call | flops 2415919104 | bytes 20000000 | tf_op jit(solution)/shard_map/branch_gather/pallas_call | solution.py:953
  484.9 8.8 gate_backward.1
  497.6 5.1 collective-permute-done.7
  502.8 18.4 %collective-permute-done.8 = bf16[768,128]{1,0:T(8,128)(2,1)S(1)} collective-permute-done((bf16[768,128]{1,0:T(8,128)(2,1)S(1)}, bf16[768,128]{1,0:T(8,128)(2,1)S(1)}, u32[]{:S(2)}, u32[]{:S(2)}) %collective-permute-start.8) | collective-permute-done | bytes 196640 | tf_op jit(solution)/shard_map/ppermute | solution.py:421
  522.2 52.8 %ssd_backward.1 = (bf16[1024,768]{1,0:T(8,128)(2,1)}, bf16[1024,256]{1,0:T(8,128)(2,1)}, bf16[1024,128]{1,0:T(8,128)(2,1)}, f32[8,1024]{1,0:T(8,128)}, f32[8,102...) custom-call(s32[4]{0:T(128)} %bitcast.88, s32[4]{0:T(128)} %slice.135.last_ref, ...), custom_call_target="tpu_custom_call" | custom-call | flops 2818572288 | bytes 12582912 | tf_op jit(solution)/shard_map/ssd_backward/pallas_call | solution.py:513
  576.5 4.5 collective-permute-done.9
  582.9 7.5 grad_inner.1
  592.8 5.4 output_product.1
  598.3 6.4 grad_out.1
  604.8 6.5 grad_gate.1
  614.7 8.1 grad_qkv.1
  629.5 29.3 %first_scatter.1 = (f32[1024,384]{1,0:T(8,128)}, f32[8,128]{1,0:T(8,128)}) custom-call(bf16[1024,768]{1,0:T(8,128)(2,1)} %get-tuple-element.95.refs_0_, bf16[1024,768]{1,0:T(8,128)(2,1)} %slice_dynamic-update-slice_fusion.refs_1_.refs_0_, bf16[1024,256]{1,0:T(8,128)(2,1)} %slice_dynamic-update-slice_fusion.1.refs_2_.refs_1_, ...), custom_call_target="tpu_custom_call" | custom-call | flops 6039797760 | bytes 20000000 | tf_op jit(solution)/shard_map/first_scatter/pallas_call | solution.py:1065
  664.5 41.5 %reduce-scatter.22.cloned.1.call-done = bf16[8,1536]{1,0:T(8,128)(2,1)} async-done(((bf16[256,1536]{1,0:T(8,128)(2,1)}), bf16[8,1536]{1,0:T(8,128)(2,1)}) %reduce-scatter.22.cloned.1.call-update) | async-done | bytes 24592
  707.7 37.6 %reduce-scatter.10.cloned.1.call-done = bf16[1,1024,384]{2,1,0:T(8,128)(2,1)} async-done(((bf16[4,1024,384]{2,1,0:T(8,128)(2,1)}), bf16[1,1024,384]{2,1,0:T(8,128)(2,1)}) %reduce-scatter.10.cloned.1.call-update) | async-done | bytes 786448 | tf_op jit(solution)/shard_map/reduce_scatter | solution.py:1247
  745.4 3.9 multiply_reduce_fusion.2
  749.4 39.0 %all-reduce.7 = (f32[384]{0:T(512)}, f32[5,1024]{1,0:T(8,128)S(1)}, f32[3,12]{1,0:T(4,128)S(1)}, f32[768]{0:T(1024)}, f32[384]{0:T(512)}) all-reduce(f32[384]{0:T(512)S(1)} %get-tuple-element.225, f32[5,1024]{1,0:T(8,128)S(1)} %bitcast.79, f32[3,12]{1,0:T(4,128)S(1)} %copy-done.35, ...), channel_id=1, replica_groups=mesh['seq'=8,'head'=4] {'seq'}, use_global_device_ids=true, to_apply=%region_10.11 | all-reduce | flops 6692 | bytes 53536 | tf_op jit(solution)/shard_map/psum | solution.py:1326
  789.0 6.1 psum.44
  797.5 21.5 %reduce-scatter.16.cloned.1.call-done = bf16[192,768]{1,0:T(8,128)(2,1)} async-done(((bf16[1536,768]{1,0:T(8,128)(2,1)}), bf16[192,768]{1,0:T(8,128)(2,1)}) %reduce-scatter.16.cloned.1.call-update) | async-done | bytes 294928 | tf_op jit(solution)/shard_map/reduce_scatter | solution.py:679
  820.8 70.3 %reduce-scatter.12.cloned.1.call-done = bf16[192,768]{1,0:T(8,128)(2,1)} async-done(((bf16[1536,768]{1,0:T(8,128)(2,1)}), bf16[192,768]{1,0:T(8,128)(2,1)}) %reduce-scatter.12.cloned.1.call-update) | async-done | bytes 294928 | tf_op jit(solution)/shard_map/reduce_scatter | solution.py:679
  892.0 73.8 %reduce-scatter.14.cloned.1.call-done = bf16[192,896]{1,0:T(8,128)(2,1)} async-done(((bf16[1536,896]{1,0:T(8,128)(2,1)}), bf16[192,896]{1,0:T(8,128)(2,1)}) %reduce-scatter.14.cloned.1.call-update) | async-done | bytes 344080 | tf_op jit(solution)/shard_map/reduce_scatter | solution.py:679
  970.4 77.7 %reduce-scatter.18.cloned.1.call-done = bf16[192,1152]{1,0:T(8,128)(2,1)} async-done(((bf16[1536,1152]{1,0:T(8,128)(2,1)}), bf16[192,1152]{1,0:T(8,128)(2,1)}) %reduce-scatter.18.cloned.1.call-update) | async-done | bytes 442384 | tf_op jit(solution)/shard_map/reduce_scatter | solution.py:679
  (222 shorter events, 79.7 us)
Async XLA Ops:
  7.2 10.8 %copy-start.28 = (bf16[1536,12]{0,1:T(8,128)(2,1)S(1)}, bf16[1536,12]{0,1:T(8,128)(2,1)}, u32[]{:S(2)}) copy-start(bf16[1536,12]{0,1:T(8,128)(2,1)} %param.24) | copy-start | bytes 110596
  7.2 11.0 %copy-start.34 = (f32[384]{0:T(512)S(1)}, f32[384]{0:T(512)}, u32[]{:S(2)}) copy-start(f32[384]{0:T(512)} %param.21) | copy-start | bytes 4612
  7.2 201.8 %all-gather.3.cloned.1.call-start = ((), (), s32[]{:S(2)}) async-start(), calls=%async_computation.13 | async-start | bytes 3932160 | tf_op jit(solution)/shard_map/all_gather | solution.py:1210
  18.3 7.6 copy-start.17
  27.6 37.9 %copy-start.21 = (s32[8192]{0:T(1024)S(1)}, s32[8192]{0:T(1024)}, u32[]{:S(2)}) copy-start(s32[8192]{0:T(1024)} %param.20) | copy-start | bytes 98308
  27.6 38.5 %copy-start.33 = (f32[4,768]{1,0:T(4,128)S(1)}, f32[4,768]{1,0:T(4,128)}, u32[]{:S(2)}) copy-start(f32[4,768]{1,0:T(4,128)} %param.25) | copy-start | bytes 36868
  27.6 38.5 %copy-start.43 = (f32[12]{0:T(128)S(1)}, f32[12]{0:T(128)}, u32[]{:S(2)}) copy-start(f32[12]{0:T(128)} %param.30) | copy-start | bytes 148
  27.6 38.5 %copy-start.37 = (f32[4,256]{1,0:T(4,128)S(1)}, f32[4,256]{1,0:T(4,128)}, u32[]{:S(2)}) copy-start(f32[4,256]{1,0:T(4,128)} %param.27) | copy-start | bytes 12292
  59.9 8.9 copy-start.38
  59.9 8.9 copy-start.40
  61.3 10.3 copy-start.42
  61.4 11.5 %copy-start.44 = (f32[12]{0:T(128)S(1)}, f32[12]{0:T(128)}, u32[]{:S(2)}) copy-start(f32[12]{0:T(128)} %param.29) | copy-start | bytes 148
  61.4 12.0 %collective-permute-start = (f32[8,1024]{1,0:T(8,128)S(1)}, f32[8,1024]{1,0:T(8,128)S(1)}, u32[]{:S(2)}, u32[]{:S(2)}) collective-permute-start(f32[8,1024]{1,0:T(8,128)S(1)} %pad_maximum_fusion.8), channel_id=1, source_target_pairs={{0,4},{4,8},{8,12},{12,16},{16,20},{20,24},{24,28},{1,5},{5,9},{9,... | collective-permute-start | bytes 98312 | tf_op jit(solution)/shard_map/ppermute | solution.py:421
  65.4 597.4 %reduce-scatter.20.cloned.1.call-start = ((), (), s32[]{:S(2)}) async-start(), calls=%async_computation.12 | async-start | bytes 1327104 | tf_op jit(solution)/shard_map/reduce_scatter | solution.py:679
  65.7 7.7 copy-start.27
  66.2 7.2 copy-start.26
  74.0 26.1 %copy-start.36 = (f32[768]{0:T(1024)S(1)}, f32[768]{0:T(1024)}, u32[]{:S(2)}) copy-start(f32[768]{0:T(1024)} %param.32) | copy-start | bytes 9220
  94.5 5.6 copy-start.16
  95.9 15.9 %collective-permute-start.1 = (bf16[776,128]{1,0:T(8,128)(2,1)}, bf16[776,128]{1,0:T(8,128)(2,1)}, u32[]{:S(2)}, u32[]{:S(2)}) collective-permute-start(bf16[776,128]{1,0:T(8,128)(2,1)} %pad_maximum_fusion.7), channel_id=1, source_target_pairs={{0,4},{4,8},{8,12},{12,16},{16,20},{20,24},{24,28},{1,5},{5,9},{9,... | collective-permute-start | bytes 595976 | tf_op jit(solution)/shard_map/ppermute | solution.py:421
  108.8 7.0 collective-permute-start.2
  128.5 26.7 %copy-start.8 = (bf16[1024,384]{1,0:T(8,128)(2,1)S(1)}, bf16[1024,384]{1,0:T(8,128)(2,1)}, u32[]{:S(2)}) copy-start(bf16[1024,384]{1,0:T(8,128)(2,1)} %tokens_ref.1) | copy-start | bytes 2359300
  157.6 289.1 %copy-start.3 = (f32[1024,384]{1,0:T(8,128)}, f32[1024,384]{1,0:T(8,128)S(1)}, u32[]{:S(2)}) copy-start(f32[1024,384]{1,0:T(8,128)S(1)} %get-tuple-element.216) | copy-start | bytes 4718596
  195.0 11.2 %copy-start.22 = (s32[8192]{0:T(1024)S(1)}, s32[8192]{0:T(1024)}, u32[]{:S(2)}) copy-start(s32[8192]{0:T(1024)} %param.20) | copy-start | bytes 98308
  196.5 36.5 %collective-permute-start.3 = (bf16[1024,768]{1,0:T(8,128)(2,1)S(1)}, bf16[1024,768]{1,0:T(8,128)(2,1)}, u32[]{:S(2)}, u32[]{:S(2)}) collective-permute-start(bf16[1024,768]{1,0:T(8,128)(2,1)S(1)} %slice.149), channel_id=1, source_target_pairs={{0,4},{4,8},{8,12},{12,16},{16,20},{20,24},{24,28},{1,5},{5,9},{9,... | collective-permute-start | bytes 4718600 | tf_op jit(solution)/shard_map/ppermute | solution.py:421
  201.2 35.9 %collective-permute-start.4 = (bf16[1024,768]{1,0:T(8,128)(2,1)S(1)}, bf16[1024,768]{1,0:T(8,128)(2,1)}, u32[]{:S(2)}, u32[]{:S(2)}) collective-permute-start(bf16[1024,768]{1,0:T(8,128)(2,1)S(1)} %slice.149), channel_id=1, source_target_pairs={{0,8},{4,12},{8,16},{12,20},{16,24},{20,28},{1,9},{5,13},{9,17},{1... | collective-permute-start | bytes 4718600 | tf_op jit(solution)/shard_map/ppermute | solution.py:421
  283.2 4.1 copy-start.18
  283.2 4.1 copy-start.19
  286.0 80.5 %collective-permute-start.5 = (bf16[1024,768]{1,0:T(8,128)(2,1)}, bf16[1024,768]{1,0:T(8,128)(2,1)}, u32[]{:S(2)}, u32[]{:S(2)}) collective-permute-start(bf16[1024,768]{1,0:T(8,128)(2,1)} %pad_maximum_fusion.2), channel_id=1, source_target_pairs={{4,0},{8,4},{12,8},{16,12},{20,16},{24,20},{28,24},{5,1},{9,5},{13... | collective-permute-start | bytes 4718600 | tf_op jit(solution)/shard_map/ppermute | solution.py:421
  288.6 122.3 %collective-permute-start.6 = (bf16[1024,768]{1,0:T(8,128)(2,1)}, bf16[1024,768]{1,0:T(8,128)(2,1)}, u32[]{:S(2)}, u32[]{:S(2)}) collective-permute-start(bf16[1024,768]{1,0:T(8,128)(2,1)} %pad_maximum_fusion.3), channel_id=1, source_target_pairs={{8,0},{12,4},{16,8},{20,12},{24,16},{28,20},{9,1},{13,5},{17,9},{2... | collective-permute-start | bytes 4718600 | tf_op jit(solution)/shard_map/ppermute | solution.py:421
  295.4 410.6 %reduce-scatter.22.cloned.1.call-start = ((), (), s32[]{:S(2)}) async-start(), calls=%async_computation.14 | async-start | bytes 811008
  368.2 44.4 %copy-start.14 = (f32[1024,384]{1,0:T(8,128)S(1)}, f32[1024,384]{1,0:T(8,128)}, u32[]{:S(2)}) copy-start(f32[1024,384]{1,0:T(8,128)} %get-tuple-element.83) | copy-start | bytes 4718596
  368.2 44.4 %copy-start.15 = (f32[1024,384]{1,0:T(8,128)S(1)}, f32[1024,384]{1,0:T(8,128)}, u32[]{:S(2)}) copy-start(f32[1024,384]{1,0:T(8,128)} %get-tuple-element.88) | copy-start | bytes 4718596
  418.6 28.1 %copy-start.5 = (bf16[1024,384]{1,0:T(8,128)(2,1)S(1)}, bf16[1024,384]{1,0:T(8,128)(2,1)}, u32[]{:S(2)}) copy-start(bf16[1024,384]{1,0:T(8,128)(2,1)} %param.37) | copy-start | bytes 2359300
  494.8 7.9 collective-permute-start.7
  496.1 25.2 %collective-permute-start.8 = (bf16[768,128]{1,0:T(8,128)(2,1)S(1)}, bf16[768,128]{1,0:T(8,128)(2,1)S(1)}, u32[]{:S(2)}, u32[]{:S(2)}) collective-permute-start(bf16[768,128]{1,0:T(8,128)(2,1)S(1)} %convert_element_type.146), channel_id=1, source_target_pairs={{8,0},{12,4},{16,8},{20,12},{24,16},{28,20},{9,1},{13,5},{17,9},{2... | collective-permute-start | bytes 589832 | tf_op jit(solution)/shard_map/ppermute | solution.py:421
  575.0 6.0 collective-permute-start.9
  592.7 152.7 %reduce-scatter.10.cloned.1.call-start = ((), (), s32[]{:S(2)}) async-start(), calls=%async_computation.7 | async-start | bytes 3932160 | tf_op jit(solution)/shard_map/reduce_scatter | solution.py:1247
  598.3 220.7 %reduce-scatter.16.cloned.1.call-start = ((), (), s32[]{:S(2)}) async-start(), calls=%async_computation.10 | async-start | bytes 2654208 | tf_op jit(solution)/shard_map/reduce_scatter | solution.py:679
  604.7 286.3 %reduce-scatter.12.cloned.1.call-start = ((), (), s32[]{:S(2)}) async-start(), calls=%async_computation.8 | async-start | bytes 2654208 | tf_op jit(solution)/shard_map/reduce_scatter | solution.py:679
  604.8 6.6 copy-start.23
  611.3 354.5 %reduce-scatter.14.cloned.1.call-start = ((), (), s32[]{:S(2)}) async-start(), calls=%async_computation.9 | async-start | bytes 3096576 | tf_op jit(solution)/shard_map/reduce_scatter | solution.py:679
  614.7 433.3 %reduce-scatter.18.cloned.1.call-start = ((), (), s32[]{:S(2)}) async-start(), calls=%async_computation.11 | async-start | bytes 3981312 | tf_op jit(solution)/shard_map/reduce_scatter | solution.py:679
  622.8 4.5 copy-start.24
  629.5 115.9 %copy-start.9 = (bf16[1024,384]{1,0:T(8,128)(2,1)S(1)}, bf16[1024,384]{1,0:T(8,128)(2,1)}, u32[]{:S(2)}) copy-start(bf16[1024,384]{1,0:T(8,128)(2,1)} %tokens_ref.1) | copy-start | bytes 2359300
  658.8 86.6 %copy-start.4 = (f32[1024,384]{1,0:T(8,128)S(1)}, f32[1024,384]{1,0:T(8,128)}, u32[]{:S(2)}) copy-start(f32[1024,384]{1,0:T(8,128)} %copy-done.3) | copy-start | bytes 4718596
  658.8 86.6 %copy-start.6 = (bf16[1024,384]{1,0:T(8,128)(2,1)S(1)}, bf16[1024,384]{1,0:T(8,128)(2,1)}, u32[]{:S(2)}) copy-start(bf16[1024,384]{1,0:T(8,128)(2,1)} %param.37) | copy-start | bytes 2359300
  745.4 4.0 copy-start.29
  745.4 4.0 copy-start.32
  (15 other events, 34.1 us)
Sparse Core Ops, SparseCore 0:
  65.5 28.7 all-gather.2
  295.6 142.8 reduce-scatter.19
  592.9 113.1 reduce-scatter.21
  708.4 36.9 reduce-scatter.9
  748.7 70.1 reduce-scatter.15
  822.3 68.6 reduce-scatter.11
  894.6 71.1 reduce-scatter.13
  969.4 78.5 reduce-scatter.17

commit v3 on v2

--- a/solution.py
+++ b/solution.py
@@ -308,111 +308,124 @@
 
 
 def attention_kernel(
-    low_ref, q_ref, do_ref, k0_ref, v0_ref, k1_ref, v1_ref, k2_ref, v2_ref, segc_ref, segr_ref,
-    out_ref, dq_ref, dk0_ref, dv0_ref, dk1_ref, dv1_ref, dk2_ref, dv2_ref,
-    dk_acc, dv_acc, acc, stats, dqt,
+    low_ref, projected_ref, do_ref, near_ref, far_ref, segc_ref, segr_ref,
+    out_ref, dq_ref, dkv_ref, dnear_ref, dfar_ref,
+    keys, dkeys, dvalues, q_both, do_both, acc, stats,
     *, scale,
 ):
-    rows = q_ref.shape[0]
+    rows = projected_ref.shape[0]
+    width = out_ref.shape[1]
+    pairs = width // LANES
     blocks = rows // SPAN
-    piece_refs = ((k2_ref, v2_ref), (k1_ref, v1_ref), (k0_ref, v0_ref))
-    pieces = len(piece_refs)
+    before = segc_ref.shape[0] // rows - 1
     low = lane_low(SPAN)
     high = jnp.logical_not(low)
     zero = jnp.zeros((SPAN, LANES), bf16)
     top_rows = lax.broadcasted_iota(jnp.int32, (LANES, SPAN), 0) < ATT_DIM
-    row = lax.broadcasted_iota(jnp.int32, (SPAN, SPAN), 0)
-    col = lax.broadcasted_iota(jnp.int32, (SPAN, SPAN), 1)
+    ahead = lax.broadcasted_iota(jnp.int32, (SPAN, SPAN), 1) - lax.broadcasted_iota(jnp.int32, (SPAN, SPAN), 0)
     pick = (
         (lax.broadcasted_iota(jnp.int32, (8, LANES), 1) >= ATT_DIM)
         == (lax.broadcasted_iota(jnp.int32, (8, LANES), 0) == 1)
     ).astype(f32)
-    dk_acc[...] = jnp.zeros_like(dk_acc)
-    dv_acc[...] = jnp.zeros_like(dv_acc)
+    keys[0:rows, :] = far_ref[...]
+    keys[rows : 2 * rows, :] = near_ref[...]
+    keys[2 * rows :, :] = projected_ref[:, width:]
+    dkeys[...] = jnp.zeros_like(dkeys)
+    dvalues[...] = jnp.zeros_like(dvalues)
 
     def halves(value):
         return jnp.where(low, value, zero), jnp.where(high, value, zero)
 
-    def allowed_at(piece, start, segr, block):
-        same = segc_ref[pl.ds(piece * rows + start, SPAN), :] == segr
-        if piece == pieces - 1:
-            return same & (row + start <= col + block * SPAN)
-        return same
-
-    for block in range(blocks):
-        q_rows = slice(block * SPAN, (block + 1) * SPAN)
-        q_both = halves(q_ref[q_rows, :] * jnp.asarray(scale, bf16))
-        do_full = do_ref[q_rows, :]
-        do_both = halves(do_full)
+    def block_step(block, unused):
+        q_start = pl.multiple_of(block * SPAN, SPAN)
+        q_rows = pl.ds(q_start, SPAN)
+        for pair in range(pairs):
+            cols = slice(pair * LANES, (pair + 1) * LANES)
+            for head, half in enumerate(halves(projected_ref[q_rows, cols] * jnp.asarray(scale, bf16))):
+                q_both[2 * pair + head] = half
+            for head, half in enumerate(halves(do_ref[q_rows, cols])):
+                do_both[2 * pair + head] = half
         segr = segr_ref[:, q_rows]
+        first, stop = low_ref[block], before * blocks + block + 1
         acc[...] = jnp.zeros_like(acc)
-        stats[0:2, :] = jnp.full((2, SPAN), masked_score, f32)
-        stats[2:4, :] = jnp.zeros((2, SPAN), f32)
-        for piece in range(pieces):
-            k_ref, v_ref = piece_refs[piece]
-            stop = block + 1 if piece == pieces - 1 else blocks
-
-            def forward_step(index, unused):
-                start = pl.multiple_of(index * SPAN, SPAN)
-                key = k_ref[pl.ds(start, SPAN), :]
-                value_both = halves(v_ref[pl.ds(start, SPAN), :])
-                allowed = allowed_at(piece, start, segr, block)
-                added = jnp.zeros((LANES, SPAN), f32)
+        stats[0, 0 : 2 * pairs, :] = jnp.full((2 * pairs, SPAN), 0.1 * masked_score, f32)
+        stats[1, 0 : 2 * pairs, :] = jnp.zeros((2 * pairs, SPAN), f32)
+
+        def allowed_at(start):
+            same = segc_ref[pl.ds(start, SPAN), :] == segr
+            return same & (ahead >= start - before * rows - q_start)
+
+        def forward_step(index, unused):
+            start = pl.multiple_of(index * SPAN, SPAN)
+            allowed = allowed_at(start)
+            for pair in range(pairs):
+                key = keys[pl.ds(start, SPAN), pair * LANES : (pair + 1) * LANES]
+                value = keys[pl.ds(start, SPAN), width + pair * LANES : width + (pair + 1) * LANES]
+                value_both = halves(value)
+                added = []
                 shrink = []
                 for head in range(2):
-                    scores = jnp.where(allowed, dot_nt(key, q_both[head]), masked_score)
-                    old_top = stats[head : head + 1, :]
+                    one = slice(2 * pair + head, 2 * pair + head + 1)
+                    scores = jnp.where(allowed, dot_nt(key, q_both[2 * pair + head]), masked_score)
+                    old_top = stats[0, one, :]
                     new_top = jnp.maximum(old_top, jnp.max(scores, axis=0, keepdims=True))
-                    weights = jnp.where(allowed, jnp.exp(scores - new_top), 0.0)
+                    weights = jnp.exp(scores - new_top)
                     factor = jnp.exp(old_top - new_top)
-                    stats[head : head + 1, :] = new_top
-                    stats[2 + head : 3 + head, :] = stats[2 + head : 3 + head, :] * factor + jnp.sum(
-                        weights, axis=0, keepdims=True
+                    stats[0, one, :] = new_top
+                    stats[1, one, :] = stats[1, one, :] * factor + jnp.sum(weights, axis=0, keepdims=True)
+                    shrink.append(factor)
+                    added.append(dot_tn(value_both[head], weights.astype(bf16)))
+                acc[pair] = acc[pair] * jnp.where(top_rows, shrink[0], shrink[1]) + (added[0] + added[1])
+            return unused
+
+        lax.fori_loop(first, stop, forward_step, 0)
+        inverse = 1.0 / stats[1, 0 : 2 * pairs, :]
+        mass = stats[0, 0 : 2 * pairs, :] + jnp.log(stats[1, 0 : 2 * pairs, :])
+        stats[0, 0 : 2 * pairs, :] = mass
+        for pair in range(pairs):
+            cols = slice(pair * LANES, (pair + 1) * LANES)
+            mine = jnp.where(top_rows, inverse[2 * pair : 2 * pair + 1, :], inverse[2 * pair + 1 : 2 * pair + 2, :])
+            attended = (acc[pair] * mine).T
+            out_ref[q_rows, cols] = attended.astype(bf16)
+            delta = dot_nt(pick, do_ref[q_rows, cols].astype(f32) * attended, highest)
+            stats[1, 2 * pair : 2 * pair + 2, :] = delta[0:2, :]
+        acc[...] = jnp.zeros_like(acc)
+
+        def backward_step(index, unused):
+            start = pl.multiple_of(index * SPAN, SPAN)
+            where = pl.ds(start, SPAN)
+            allowed = allowed_at(start)
+            for pair in range(pairs):
+                cols = slice(pair * LANES, (pair + 1) * LANES)
+                key = keys[where, cols]
+                value = keys[where, width + pair * LANES : width + (pair + 1) * LANES]
+                key_both = halves(key)
+                parts = []
+                for head in range(2):
+                    one = slice(2 * pair + head, 2 * pair + head + 1)
+                    q_one, do_one = q_both[2 * pair + head], do_both[2 * pair + head]
+                    scores = jnp.where(allowed, dot_nt(key, q_one), masked_score)
+                    weights = jnp.exp(scores - stats[0, one, :])
+                    dweights = dot_nt(value, do_one)
+                    dscores = (weights * (dweights - stats[1, one, :])).astype(bf16)
+                    parts.append(
+                        (dot_nn(weights.astype(bf16), do_one), dot_nn(dscores, q_one), dot_tn(key_both[head], dscores))
                     )
-                    shrink.append(factor)
-                    added = added + dot_tn(value_both[head], weights.astype(bf16))
-                acc[...] = acc[...] * jnp.where(top_rows, shrink[0], shrink[1]) + added
-                return unused
-
-            lax.fori_loop(low_ref[block * pieces + piece], stop, forward_step, 0)
-        inverse = [1.0 / stats[2 + head : 3 + head, :] for head in range(2)]
-        attended = (acc[...] * jnp.where(top_rows, inverse[0], inverse[1])).T
-        out_ref[q_rows, :] = attended.astype(bf16)
-        delta = dot_nt(pick, do_full.astype(f32) * attended, highest)
-        mass = [stats[head : head + 1, :] + jnp.log(stats[2 + head : 3 + head, :]) for head in range(2)]
-        dqt[...] = jnp.zeros_like(dqt)
-        for piece in range(pieces):
-            k_ref, v_ref = piece_refs[piece]
-            stop = block + 1 if piece == pieces - 1 else blocks
-
-            def backward_step(index, unused):
-                start = pl.multiple_of(index * SPAN, SPAN)
-                key = k_ref[pl.ds(start, SPAN), :]
-                value = v_ref[pl.ds(start, SPAN), :]
-                key_both = halves(key)
-                allowed = allowed_at(piece, start, segr, block)
-                dk = jnp.zeros((SPAN, LANES), f32)
-                dv = jnp.zeros((SPAN, LANES), f32)
-                dq = jnp.zeros((LANES, SPAN), f32)
-                for head in range(2):
-                    scores = dot_nt(key, q_both[head])
-                    weights = jnp.where(allowed, jnp.exp(scores - mass[head]), 0.0)
-                    dweights = dot_nt(value, do_both[head])
-                    dscores = (weights * (dweights - delta[head : head + 1, :])).astype(bf16)
-                    dv = dv + dot_nn(weights.astype(bf16), do_both[head])
-                    dk = dk + dot_nn(dscores, q_both[head])
-                    dq = dq + dot_tn(key_both[head], dscores)
-                where = pl.ds(piece * rows + start, SPAN)
-                dk_acc[where, :] += dk
-                dv_acc[where, :] += dv
-                dqt[...] += dq
-                return unused
-
-            lax.fori_loop(low_ref[block * pieces + piece], stop, backward_step, 0)
-        dq_ref[q_rows, :] = (dqt[...] * scale).T.astype(dq_ref.dtype)
-    for piece, (dk_ref, dv_ref) in enumerate(((dk2_ref, dv2_ref), (dk1_ref, dv1_ref), (dk0_ref, dv0_ref))):
-        dk_ref[...] = dk_acc[piece * rows : (piece + 1) * rows, :].astype(dk_ref.dtype)
-        dv_ref[...] = dv_acc[piece * rows : (piece + 1) * rows, :].astype(dv_ref.dtype)
+                dvalues[where, cols] += parts[0][0] + parts[1][0]
+                dkeys[where, cols] += parts[0][1] + parts[1][1]
+                acc[pair] += parts[0][2] + parts[1][2]
+            return unused
+
+        lax.fori_loop(first, stop, backward_step, 0)
+        for pair in range(pairs):
+            dq_ref[q_rows, pair * LANES : (pair + 1) * LANES] = (acc[pair] * scale).T
+        return unused
+
+    lax.fori_loop(0, blocks, block_step, 0)
+    for piece, ref in enumerate((dfar_ref, dnear_ref, dkv_ref)):
+        where = slice(piece * rows, (piece + 1) * rows)
+        ref[:, :width] = dkeys[where, :].astype(ref.dtype)
+        ref[:, width:] = dvalues[where, :].astype(ref.dtype)
 
 
 def from_behind(value, axis, by):
@@ -622,41 +635,35 @@
     )(back_gated, ssd_out, zx, coefficients, gain, state_c, opened, wide)
 
 
-def attention(low_blocks, query_array, back_attended, pieces, segc, segr, att_pad, rows):
+def attention(low_blocks, projected, back_attended, near, far, segc, segr, att_pad):
+    rows = projected.shape[0]
     pairs = att_pad // LANES
-    scale = 1.0 / math.sqrt(ATT_DIM)
-    count = len(pieces)
-
-    def lane(offset):
-        return pl.BlockSpec((rows, LANES), lambda p, *unused: (0, p + offset))
-
-    in_specs = [lane(0), lane(0)]
-    operands = [query_array, back_attended]
-    for array, offset in pieces:
-        in_specs += [lane(offset), lane(offset + pairs)]
-        operands += [array, array]
-    in_specs += [fixed((count * rows, 1)), fixed((1, rows))]
-    shapes = [bf16, f32] + [f32, f32] + [bf16, bf16] * (count - 1)
+    window = segc.shape[0]
+    vmem = pl.BlockSpec(memory_space=pltpu.VMEM)
     return pl.pallas_call(
-        partial(attention_kernel, scale=scale),
-        grid_spec=pltpu.PrefetchScalarGridSpec(
-            num_scalar_prefetch=1,
-            grid=(pairs,),
-            in_specs=in_specs,
-            out_specs=[lane(0)] * len(shapes),
-            scratch_shapes=[
-                pltpu.VMEM((count * rows, LANES), f32),
-                pltpu.VMEM((count * rows, LANES), f32),
-                pltpu.VMEM((LANES, SPAN), f32),
-                pltpu.VMEM((8, SPAN), f32),
-                pltpu.VMEM((LANES, SPAN), f32),
-            ],
-        ),
-        out_shape=[jax.ShapeDtypeStruct((rows, att_pad), kind) for kind in shapes],
+        partial(attention_kernel, scale=1.0 / math.sqrt(ATT_DIM)),
+        in_specs=[pl.BlockSpec(memory_space=pltpu.SMEM)] + [vmem] * 6,
+        out_specs=[vmem] * 5,
+        out_shape=[
+            jax.ShapeDtypeStruct((rows, att_pad), bf16),
+            jax.ShapeDtypeStruct((rows, att_pad), f32),
+            jax.ShapeDtypeStruct((rows, 2 * att_pad), f32),
+            jax.ShapeDtypeStruct((rows, 2 * att_pad), bf16),
+            jax.ShapeDtypeStruct((rows, 2 * att_pad), bf16),
+        ],
+        scratch_shapes=[
+            pltpu.VMEM((window, 2 * att_pad), bf16),
+            pltpu.VMEM((window, att_pad), f32),
+            pltpu.VMEM((window, att_pad), f32),
+            pltpu.VMEM((2 * pairs, SPAN, LANES), bf16),
+            pltpu.VMEM((2 * pairs, SPAN, LANES), bf16),
+            pltpu.VMEM((pairs, LANES, SPAN), f32),
+            pltpu.VMEM((2, -(-2 * pairs // 8) * 8, SPAN), f32),
+        ],
         compiler_params=params(),
         cost_estimate=cost(rows * rows * att_pad * 28, rows * att_pad * 30, rows * rows * pairs * 4),
         name="attention",
-    )(low_blocks, *operands, segc, segr)
+    )(low_blocks, projected, back_attended, near, far, segc, segr)
 
 
 def fit(value, size, axis):
@@ -667,28 +674,8 @@
     return jnp.pad(value, widths)
 
 
-def head_gather(values):
-    return lax.all_gather(values, "head", axis=1, tiled=True)
-
-
-def head_scatter(values):
-    return lax.psum_scatter(values, "head", scatter_dimension=1, tiled=True)
-
-
 def seq_scatter(values):
     return lax.psum_scatter(values.astype(bf16), "seq", scatter_dimension=0, tiled=True).astype(f32)
-
-
-def matmul(a, b, kind=f32):
-    return jnp.dot(a, b, preferred_element_type=f32).astype(kind)
-
-
-def matmul_nt(a, b, kind=f32):
-    return lax.dot_general(a, b, (((1,), (1,)), ((), ())), preferred_element_type=f32).astype(kind)
-
-
-def matmul_tn(a, b, kind=f32):
-    return lax.dot_general(a, b, (((0,), (0,)), ((), ())), preferred_element_type=f32).astype(kind)
 
 
 MESH = pl.DeviceIdType.MESH
@@ -747,10 +734,12 @@
         for kind in list(range(1, self.place.chips)) + [0]:
             self.copy(kind, part).start()
 
-    def arrive(self, part):
+    def pass_on(self, part):
         for step in range(1, self.place.chips):
             self.copy(step, part).wait_recv()
             self.copy(self.place.chips + step - 1, part).start()
+
+    def complete(self, part):
         self.copy(0, part).wait_recv()
         for step in range(1, self.place.chips):
             self.copy(self.place.chips + step - 1, part).wait_recv()
@@ -825,10 +814,9 @@
 
 
 def first_gather_kernel(
-    count, products, tokens_ref, gain_ref, *refs
+    count, tokens_ref, gain_ref, zx_ref, bcs_ref, full_ref, rms_ref, z_out, x_out, bcs_out,
+    raw, gains, send, receive, gsend, greceive,
 ):
-    weights, (full_ref, rms_ref), outs = refs[:products], refs[products : products + 2], refs[products + 2 : 2 * products + 2]
-    raw, gains, send, receive, gsend, greceive = refs[2 * products + 2 :]
     rows, features = tokens_ref.shape
     place = HeadPlace(count)
     parts = rows // CHUNK
@@ -846,23 +834,29 @@
     lax.fori_loop(0, parts, lambda part, unused: (data.start(part), unused)[1], 0)
     gains[place.me] = gain_ref[...]
     raw[place.me] = tokens_ref[...]
-    gain.arrive(0)
+    gain.pass_on(0)
+    gain.complete(0)
 
     def step(part, unused):
-        data.arrive(part)
+        data.pass_on(part)
+        data.complete(part)
         where = rows_of(part)
         values = [raw[who, where, :].astype(f32) for who in range(count)]
         total = sum(jnp.sum(value * value, axis=1, keepdims=True) for value in values)
         scale = lax.rsqrt(total / (count * features) + epsilon)
         rms_ref[where, :] = jnp.broadcast_to(scale, (CHUNK, 8))
-        sums = [jnp.zeros((CHUNK, out.shape[1]), f32) for out in outs]
+        zx = jnp.zeros((CHUNK, zx_ref.shape[1]), f32)
+        bcs = jnp.zeros((CHUNK, bcs_ref.shape[1]), f32)
         for who in range(count):
             normed = (values[who] * scale * gains[who, 0:1, :]).astype(bf16)
             full_ref[who, where, :] = normed
             inner_rows = slice(who * features, (who + 1) * features)
-            sums = [value + dot_nn(normed, weight[inner_rows, :]) for value, weight in zip(sums, weights)]
-        for out, value in zip(outs, sums):
-            out[where, :] = value
+            zx = zx + dot_nn(normed, zx_ref[inner_rows, :])
+            bcs = bcs + dot_nn(normed, bcs_ref[inner_rows, :])
+        inner = z_out.shape[1]
+        z_out[where, :] = zx[:, :inner]
+        x_out[where, :] = zx[:, inner:]
+        bcs_out[where, :] = bcs
         return unused
 
     lax.fori_loop(0, parts, step, 0)
@@ -870,19 +864,21 @@
     lax.fori_loop(0, parts, lambda part, unused: (data.finish(part), unused)[1], 0)
 
 
-def first_gather(tokens, gain, weights, ident):
+def first_gather(tokens, gain, zx_weight, bcs_weight, ident):
     rows, features = tokens.shape
     count = D // features
     chips = count // 2
     return pl.pallas_call(
-        partial(first_gather_kernel, count, len(weights)),
-        in_specs=[VMEM] * (2 + len(weights)),
-        out_specs=[VMEM] * (2 + len(weights)),
+        partial(first_gather_kernel, count),
+        in_specs=[VMEM] * 4,
+        out_specs=[VMEM] * 5,
         out_shape=[
             jax.ShapeDtypeStruct((count, rows, features), bf16),
             jax.ShapeDtypeStruct((rows, 8), f32),
-        ]
-        + [jax.ShapeDtypeStruct((rows, weight.shape[1]), f32) for weight in weights],
+            jax.ShapeDtypeStruct((rows, zx_weight.shape[1] // 2), f32),
+            jax.ShapeDtypeStruct((rows, zx_weight.shape[1] // 2), f32),
+            jax.ShapeDtypeStruct((rows, bcs_weight.shape[1]), f32),
+        ],
         scratch_shapes=[
             pltpu.VMEM((count, rows, features), bf16),
             pltpu.VMEM((count, 8, features), f32),
@@ -890,16 +886,17 @@
         + gather_sems(chips, rows // CHUNK)
         + gather_sems(chips, 1),
         compiler_params=comm_params(ident),
-        cost_estimate=cost(2 * rows * D * sum(weight.shape[1] for weight in weights), 30e6),
+        cost_estimate=cost(2 * rows * D * (zx_weight.shape[1] + bcs_weight.shape[1]), 30e6),
         name="first_gather",
-    )(tokens, fit(gain[None], 8, 0), *weights)
-
-
-def gather_kernel(
-    count, transposed, scaled, own_ref, dense_ref, weight_ref,
-    full_ref, total_ref, out_ref,
-    send, receive, near, pair, far, ssend, sreceive,
-):
+    )(tokens, fit(gain[None], 8, 0), zx_weight, bcs_weight)
+
+
+def gather_kernel(count, transposed, scaled, filled, own_ref, dense_ref, weight_ref, *refs):
+    fill_left, fill_right = refs[:2] if filled else (None, None)
+    refs = refs[2:] if filled else refs
+    full_ref, total_ref, out_ref = refs[:3]
+    fill_out = refs[3] if filled else None
+    send, receive, near, pair, far, ssend, sreceive = refs[-7:]
     rows, features = own_ref.shape
     place = HeadPlace(count)
     parts = rows // CHUNK
@@ -923,7 +920,13 @@
         near[...] = lax.rsqrt(total / (count * features) + epsilon)
 
     def step(part, unused):
-        data.arrive(part)
+        data.pass_on(part)
+        if filled:
+            for index in range(count // parts):
+                who = part * (count // parts) + index
+                where = pl.ds(pl.multiple_of(who * features, features), features)
+                fill_out[where, :] = dot_tn(fill_left[who], fill_right[...]).astype(bf16)
+        data.complete(part)
         where = rows_of(part)
         out = jnp.zeros((CHUNK, out_ref.shape[1]), f32)
         for who in range(count):
@@ -944,123 +947,414 @@
     lax.fori_loop(0, parts, lambda part, unused: (data.finish(part), unused)[1], 0)
 
 
-def gather_matmul(own, sums, weight, transposed, scaled, ident, name):
+def gather_matmul(own, sums, weight, transposed, scaled, ident, name, fill=()):
     rows, features = own.shape
     count = D // features
     chips = count // 2
     columns = weight.shape[0 if transposed else 1]
     dense = rows // LANES
+    shapes = [
+        jax.ShapeDtypeStruct((count, rows, features), bf16),
+        jax.ShapeDtypeStruct((dense, LANES), f32),
+        jax.ShapeDtypeStruct((rows, columns), bf16),
+    ]
+    if fill:
+        shapes.append(jax.ShapeDtypeStruct((D, fill[1].shape[1]), bf16))
     return pl.pallas_call(
-        partial(gather_kernel, count, transposed, scaled),
-        in_specs=[VMEM] * 3,
-        out_specs=[VMEM] * 3,
-        out_shape=[
-            jax.ShapeDtypeStruct((count, rows, features), bf16),
-            jax.ShapeDtypeStruct((dense, LANES), f32),
-            jax.ShapeDtypeStruct((rows, columns), bf16),
-        ],
+        partial(gather_kernel, count, transposed, scaled, bool(fill)),
+        in_specs=[VMEM] * (3 + len(fill)),
+        out_specs=[VMEM] * len(shapes),
+        out_shape=shapes,
         scratch_shapes=gather_sems(chips, rows // CHUNK) + scalar_scratch(chips, dense),
         compiler_params=comm_params(ident),
         cost_estimate=cost(2 * rows * D * columns, 20e6),
         name=name,
-    )(own, sums.reshape(dense, LANES), weight)
+    )(own, sums.reshape(dense, LANES), weight, *fill)
+
+
+def part_rows(part):
+    return pl.ds(pl.multiple_of(part * CHUNK, CHUNK), CHUNK)
+
+
+class TwoLevelScatter:
+    def __init__(self, place, lefts, rights, transposed, out, scratch):
+        self.place, self.lefts, self.rights, self.transposed, self.out = place, lefts, rights, transposed, out
+        (self.own, self.near, self.sent, self.far, self.psend, self.preceive, self.xsend, self.xreceive) = scratch
+        self.parts = out.shape[0] // CHUNK
+
+    def to_partner(self, chip, part):
+        slot = chip * self.parts + part
+        return remote(
+            self.own.at[chip * 2 + 1 - self.place.core, part_rows(part)], self.near.at[chip, part_rows(part)],
+            self.psend.at[slot], self.preceive.at[slot], self.place.partner,
+        )
+
+    def across(self, step, part):
+        slot = (step - 1) * self.parts + part
+        return remote(
+            self.sent.at[step - 1, part_rows(part)], self.far.at[step - 1, part_rows(part)],
+            self.xsend.at[slot], self.xreceive.at[slot], self.place.ahead(step),
+        )
+
+    def compute(self, part):
+        where = part_rows(part)
+        features = self.out.shape[1]
+        for who in range(self.place.count):
+            inner = slice(who * features, (who + 1) * features)
+            value = jnp.zeros((CHUNK, features), f32)
+            for left, right in zip(self.lefts, self.rights):
+                if self.transposed:
+                    right, columns = right if isinstance(right, tuple) else (right, slice(None))
+                    value = value + dot_nt(left[where, :], right[inner, columns])
+                else:
+                    value = value + dot_nn(left[where, :], right[:, inner])
+            self.own[who, where, :] = value.astype(bf16)
+        for chip in range(self.place.chips):
+            self.to_partner(chip, part).start()
+
+    def combine(self, part):
+        where = part_rows(part)
+        place = self.place
+        for chip in range(place.chips):
+            self.to_partner(chip, part).wait_recv()
+        for step in range(1, place.chips):
+            chip = lax.rem(place.chip + step, place.chips)
+            mine = self.own[chip * 2 + place.core, where, :].astype(f32)
+            self.sent[step - 1, where, :] = (mine + self.near[chip, where, :].astype(f32)).astype(bf16)
+            self.across(step, part).start()
+
+    def collect(self, part):
+        where = part_rows(part)
+        place = self.place
+        value = self.own[place.me, where, :].astype(f32) + self.near[place.chip, where, :].astype(f32)
+        for step in range(1, place.chips):
+            self.across(step, part).wait_recv()
+            value = value + self.far[step - 1, where, :].astype(f32)
+        self.out[where, :] = value
+
+    def drain(self, part):
+        for chip in range(self.place.chips):
+            self.to_partner(chip, part).wait_send()
+        for step in range(1, self.place.chips):
+            self.across(step, part).wait_send()
+
+
+def repeat(start, stop, step):
+    lax.fori_loop(start, stop, lambda i, unused: (step(i), unused)[1], 0)
+
+
+def scatter_scratch(count, rows, features):
+    chips = count // 2
+    parts = rows // CHUNK
+    others = max(chips - 1, 1)
+    return [
+        pltpu.VMEM((count, rows, features), bf16),
+        pltpu.VMEM((chips, rows, features), bf16),
+        pltpu.VMEM((others, rows, features), bf16),
+        pltpu.VMEM((others, rows, features), bf16),
+        pltpu.SemaphoreType.DMA((chips * parts,)),
+        pltpu.SemaphoreType.DMA((chips * parts,)),
+        pltpu.SemaphoreType.DMA((others * parts,)),
+        pltpu.SemaphoreType.DMA((others * parts,)),
+    ]
 
 
 def scatter_kernel(count, operands, transposed, *refs):
     lefts, rights = refs[:operands], refs[operands : 2 * operands]
     dense_ref, out_ref, total_ref = refs[2 * operands : 2 * operands + 3]
-    (own, near_data, sent, far_data, psend, preceive, xsend, xreceive,
-     near, pair, far, ssend, sreceive) = refs[2 * operands + 3 :]
-    rows, features = out_ref.shape
+    scratch = refs[2 * operands + 3 :]
     place = HeadPlace(count)
-    chips = place.chips
-    parts = rows // CHUNK
-
-    def rows_of(part):
-        return pl.ds(pl.multiple_of(part * CHUNK, CHUNK), CHUNK)
-
-    def to_partner(chip, part):
-        slot = chip * parts + part
-        return remote(
-            own.at[chip * 2 + 1 - place.core, rows_of(part)], near_data.at[chip, rows_of(part)],
-            psend.at[slot], preceive.at[slot], place.partner,
-        )
-
-    def across(step, part):
-        slot = (step - 1) * parts + part
-        return remote(
-            sent.at[step - 1, rows_of(part)], far_data.at[step - 1, rows_of(part)],
-            xsend.at[slot], xreceive.at[slot], place.ahead(step),
-        )
-
-    scalars = ScalarSum(place, dense_ref, near, pair, far, ssend, sreceive)
+    scatter = TwoLevelScatter(place, lefts, rights, transposed, out_ref, scratch[:8])
+    scalars = ScalarSum(place, dense_ref, *scratch[8:])
     place.meet()
     scalars.start()
-
-    def compute(part):
-        where = rows_of(part)
-        for who in range(count):
-            inner = slice(who * features, (who + 1) * features)
-            value = jnp.zeros((CHUNK, features), f32)
-            for left, right in zip(lefts, rights):
-                if transposed:
-                    value = value + dot_nt(left[where, :], right[inner, :])
-                else:
-                    value = value + dot_nn(left[where, :], right[:, inner])
-            own[who, where, :] = value.astype(bf16)
-        for chip in range(chips):
-            to_partner(chip, part).start()
-
-    def combine(part):
-        where = rows_of(part)
-        for chip in range(chips):
-            to_partner(chip, part).wait_recv()
-        for step in range(1, chips):
-            chip = lax.rem(place.chip + step, chips)
-            mine = own[chip * 2 + place.core, where, :].astype(f32)
-            sent[step - 1, where, :] = (mine + near_data[chip, where, :].astype(f32)).astype(bf16)
-            across(step, part).start()
-
-    compute(0)
+    scatter.compute(0)
     scalars.middle()
 
-    def forward(part, unused):
-        compute(part)
-        combine(part - 1)
-        return unused
-
-    lax.fori_loop(1, parts, forward, 0)
-    combine(parts - 1)
+    def forward(part):
+        scatter.compute(part)
+        scatter.combine(part - 1)
+
+    repeat(1, scatter.parts, forward)
+    scatter.combine(scatter.parts - 1)
     total_ref[...] = scalars.total()
-
-    def collect(part, unused):
-        where = rows_of(part)
-        value = own[place.me, where, :].astype(f32) + near_data[place.chip, where, :].astype(f32)
-        for step in range(1, chips):
-            across(step, part).wait_recv()
-            value = value + far_data[step - 1, where, :].astype(f32)
-        out_ref[where, :] = value
-        return unused
-
-    lax.fori_loop(0, parts, collect, 0)
+    repeat(0, scatter.parts, scatter.collect)
     scalars.finish()
-
-    def drain(part, unused):
-        for chip in range(chips):
-            to_partner(chip, part).wait_send()
-        for step in range(1, chips):
-            across(step, part).wait_send()
-        return unused
-
-    lax.fori_loop(0, parts, drain, 0)
+    repeat(0, scatter.parts, scatter.drain)
+
+
+class SeqRing:
+    def __init__(self, count):
+        self.count = count
+        self.me = lax.axis_index("seq")
+        self.columns = 2 if count == 8 else 1
+        self.place = self.position(self.me)
+        self.ahead = self.device(lax.rem(self.place + 1, count))
+        self.behind = self.device(lax.rem(self.place + count - 1, count))
+
+    def position(self, index):
+        if self.columns == 1:
+            return index
+        length = self.count // 2
+        line, column = index // 2, lax.rem(index, 2)
+        return (1 - column) * line + column * (2 * length - 1 - line)
+
+    def device(self, position):
+        if self.columns == 1:
+            return position
+        length = self.count // 2
+        column, line = position // length, lax.rem(position, length)
+        return 2 * ((1 - column) * line + column * (length - 1 - line)) + column
+
+    def chunk(self, direction, step):
+        return self.device(lax.rem(self.place + 2 * self.count - direction * (2 + step), self.count))
+
+
+def seq_remote(source, target, send, receive, device):
+    return pltpu.make_async_remote_copy(
+        src_ref=source, dst_ref=target, send_sem=send, recv_sem=receive,
+        device_id={"seq": device}, device_id_type=MESH,
+    )
+
+
+class RingStream:
+    def __init__(self, ring, direction, source, columns, out, scratch):
+        self.ring, self.direction, self.source, self.columns, self.out = ring, direction, source, columns, out
+        self.sent, self.got, self.send, self.receive = scratch
+        self.rows = source.shape[0] // ring.count
+
+    def copy(self, step):
+        device = self.ring.ahead if self.direction == 1 else self.ring.behind
+        return seq_remote(
+            self.sent.at[step], self.got.at[step], self.send.at[step], self.receive.at[step], device
+        )
+
+    def own(self, step):
+        chunk = self.ring.chunk(self.direction, step)
+        where = pl.ds(pl.multiple_of(chunk * self.rows, self.rows), self.rows)
+        return self.source[where, self.columns]
+
+    def start(self):
+        self.sent[0] = self.own(-1)
+        self.copy(0).start()
+
+    def advance(self, step):
+        self.copy(step).wait_recv()
+        value = self.got[step].astype(f32) + self.own(step).astype(f32)
+
+        @pl.when(step < self.ring.count - 2)
+        def _():
+            self.sent[step + 1] = value.astype(bf16)
+            self.copy(step + 1).start()
+
+        @pl.when(step == self.ring.count - 2)
+        def _():
+            self.out[...] = value
+
+    def drain(self, step):
+        self.copy(step).wait_send()
+
+
+def stream_scratch(count, rows, columns):
+    return [
+        pltpu.VMEM((count - 1, rows, columns), bf16),
+        pltpu.VMEM((count - 1, rows, columns), bf16),
+        pltpu.SemaphoreType.DMA((count - 1,)),
+        pltpu.SemaphoreType.DMA((count - 1,)),
+    ]
+
+
+def tail_kernel(count, streams, state_rows, *refs):
+    lefts = refs[:4]
+    zx_weight, bc_weight, bcs_weight = refs[4:7]
+    refs = refs[7:]
+    inner = lefts[0].shape[1]
+    bc_width = bc_weight.shape[1]
+    rights = (
+        (zx_weight, slice(0, inner)),
+        (zx_weight, slice(inner, 2 * inner)),
+        (bcs_weight, slice(0, bc_width)),
+        (bcs_weight, slice(bc_width, bc_width + LANES)),
+    )
+    dense_ref, small_ref, inner_ref, step_ref, bc_ref, tokens_ref, rms_ref = refs[:7]
+    out_ref, total_ref, small_out_ref, bc_out_ref, gain_out_ref = refs[7:12]
+    stream_outs = refs[12 : 12 + len(streams) - 1]
+    scratch = list(refs[12 + len(streams) - 1 :])
+
+    def take(number):
+        taken = scratch[:number]
+        del scratch[:number]
+        return taken
+
+    place = HeadPlace(count)
+    ring = SeqRing(small_out_ref.shape[0])
+    scatter = TwoLevelScatter(place, lefts, rights, True, out_ref, take(8))
+    scalars = ScalarSum(place, dense_ref, *take(5))
+    bc_sum, bc_split, bc_far, bsend, breceive = take(5)
+    ssend, sreceive = take(2)
+    gains, gsend, greceive = take(3)
+    sources = {"inner": inner_ref, "step": step_ref, "bc": bc_ref}
+    outs = list(stream_outs) + [bc_sum]
+    flows = []
+    for (name, direction, columns), out in zip(streams, outs):
+        flows.append(RingStream(ring, direction, sources[name], slice(*columns), out, take(4)))
+
+    def small_copy(step):
+        block = ring.device(lax.rem(ring.place + ring.count - step, ring.count))
+        return seq_remote(
+            small_out_ref.at[block], small_out_ref.at[block], ssend.at[step], sreceive.at[step], ring.ahead
+        )
+
+    def gain_copy(step):
+        return seq_remote(
+            gains.at[ring.me], gains.at[ring.me], gsend.at[step - 1], greceive.at[step - 1],
+            lax.rem(ring.me + step, ring.count),
+        )
+
+    def collected(part):
+        scatter.collect(part)
+        where = part_rows(part)
+        value = tokens_ref[where, :].astype(f32) * rms_ref[where, 0:1] * out_ref[where, :]
+        gains[ring.me, 0:1, :] += jnp.sum(value, axis=0, keepdims=True)
+
+    def bc_copy(step):
+        other = lax.rem(place.me + step, count)
+        return remote(bc_split.at[other], bc_far.at[step - 1], bsend.at[step - 1], breceive.at[step - 1], other)
+
+    barrier = pltpu.get_barrier_semaphore()
+    for step in range(1, count):
+        pl.semaphore_signal(
+            barrier, inc=1, device_id={"head": lax.rem(place.me + step, count)}, device_id_type=MESH
+        )
+    for step in range(1, ring.count):
+        pl.semaphore_signal(
+            barrier, inc=1, device_id={"seq": lax.rem(ring.me + step, ring.count)}, device_id_type=MESH
+        )
+    pl.semaphore_wait(barrier, count - 1 + ring.count - 1)
+
+    scalars.start()
+    for flow in flows:
+        flow.start()
+    scatter.compute(0)
+    scalars.middle()
+    total = scalars.total()
+    total_ref[...] = total
+    small_out_ref[ring.me] = small_ref[...]
+    small_out_ref[ring.me, 0:state_rows, :] = total[total.shape[0] - state_rows :, :]
+    small_copy(0).start()
+    gains[ring.me] = jnp.zeros(gains.shape[1:], f32)
+
+    def turn(step):
+        for flow in flows:
+            flow.advance(step)
+        small_copy(step).wait_recv()
+
+        @pl.when(step < ring.count - 2)
+        def _():
+            small_copy(step + 1).start()
+
+    def forward(part):
+        turn(part - 1)
+        scatter.compute(part)
+        scatter.combine(part - 1)
+
+    repeat(1, scatter.parts, forward)
+    scatter.combine(scatter.parts - 1)
+
+    def collect(part):
+        turn(scatter.parts - 1 + part)
+        collected(part)
+
+    both = min(scatter.parts, ring.count - scatter.parts)
+    repeat(0, both, collect)
+    repeat(both, scatter.parts, collected)
+    repeat(1, ring.count, lambda step: gain_copy(step).start())
+    repeat(scatter.parts - 1 + both, ring.count - 1, turn)
+    shared = bc_out_ref.shape[0]
+    whole = bc_sum[...]
+    for who in range(count):
+        bc_split[who] = whole[who * shared : (who + 1) * shared, :]
+    for step in range(1, count):
+        bc_copy(step).start()
+    repeat(1, ring.count, lambda step: gain_copy(step).wait_recv())
+    gained = gains[0]
+    for index in range(1, ring.count):
+        gained = gained + gains[index]
+    gain_out_ref[...] = gained
+    repeat(1, ring.count, lambda step: gain_copy(step).wait_send())
+    scalars.finish()
+    repeat(0, scatter.parts, scatter.drain)
+    for flow in flows:
+        repeat(0, ring.count - 1, flow.drain)
+    repeat(0, ring.count - 1, lambda step: small_copy(step).wait_send())
+    value = bc_split[place.me]
+    for step in range(1, count):
+        bc_copy(step).wait_recv()
+        value = value + bc_far[step - 1]
+    bc_out_ref[...] = value
+    for step in range(1, count):
+        bc_copy(step).wait_send()
+
+
+def tail(lefts, zx_weight, bc_weight, bcs_weight, sums, state, small, inner_grad, step_grad, bc_grad, tokens, rms, count, ident):
+    rows = lefts[0].shape[0]
+    features = D // count
+    chips = count // 2
+    shards = lax.axis_size("seq")
+    inner = inner_grad.shape[1]
+    width = bc_grad.shape[0]
+    total = inner + LANES + width
+    first = min(inner, (total + 2 * LANES - 1) // (2 * LANES) * LANES)
+    streams = [("inner", 1, (0, first))]
+    if first < inner:
+        streams.append(("inner", -1, (first, inner)))
+    streams.append(("step", -1, (0, LANES)))
+    streams.append(("bc", -1, (0, D)))
+    per = D // shards
+    bc_rows = width // shards
+    shared = bc_rows // count
+    state_rows = state.shape[0]
+    dense = rows // LANES + state_rows
+    sizes = [(bc_rows if name == "bc" else per, stop - start) for name, way, (start, stop) in streams]
+    flops = sum(2 * rows * D * left.shape[1] for left in lefts)
+    block = jnp.concatenate([sums.reshape(rows // LANES, LANES), state], axis=0)
+    return pl.pallas_call(
+        partial(tail_kernel, count, streams, state_rows),
+        in_specs=[VMEM] * 14,
+        out_specs=[VMEM] * (5 + len(streams) - 1),
+        out_shape=[
+            jax.ShapeDtypeStruct((rows, features), f32),
+            jax.ShapeDtypeStruct((dense, LANES), f32),
+            jax.ShapeDtypeStruct((shards,) + small.shape, f32),
+            jax.ShapeDtypeStruct((shared, D), f32),
+            jax.ShapeDtypeStruct((8, features), f32),
+        ]
+        + [jax.ShapeDtypeStruct(size, f32) for size in sizes[:-1]],
+        scratch_shapes=scatter_scratch(count, rows, features)
+        + scalar_scratch(chips, dense)
+        + [
+            pltpu.VMEM((bc_rows, D), f32),
+            pltpu.VMEM((count, shared, D), f32),
+            pltpu.VMEM((count - 1, shared, D), f32),
+            pltpu.SemaphoreType.DMA((count - 1,)),
+            pltpu.SemaphoreType.DMA((count - 1,)),
+            pltpu.SemaphoreType.DMA((shards - 1,)),
+            pltpu.SemaphoreType.DMA((shards - 1,)),
+            pltpu.VMEM((shards, 8, features), f32),
+            pltpu.SemaphoreType.DMA((shards - 1,)),
+            pltpu.SemaphoreType.DMA((shards - 1,)),
+        ]
+        + [item for size in sizes for item in stream_scratch(shards, *size)],
+        compiler_params=comm_params(ident),
+        cost_estimate=cost(flops, 40e6),
+        name="tail",
+    )(*lefts, zx_weight, bc_weight, bcs_weight, block, small, inner_grad, step_grad, bc_grad, tokens, rms)
 
 
 def matmul_scatter(lefts, rights, sums, transposed, count, ident, name):
     rows = lefts[0].shape[0]
     features = D // count
-    chips = count // 2
     dense = rows // LANES
-    parts = rows // CHUNK
     flops = sum(2 * rows * D * left.shape[1] for left in lefts)
     return pl.pallas_call(
         partial(scatter_kernel, count, len(lefts), transposed),
@@ -1070,17 +1364,7 @@
             jax.ShapeDtypeStruct((rows, features), f32),
             jax.ShapeDtypeStruct((dense, LANES), f32),
         ],
-        scratch_shapes=[
-            pltpu.VMEM((count, rows, features), bf16),
-            pltpu.VMEM((chips, rows, features), bf16),
-            pltpu.VMEM((max(chips - 1, 1), rows, features), bf16),
-            pltpu.VMEM((max(chips - 1, 1), rows, features), bf16),
-            pltpu.SemaphoreType.DMA((chips * parts,)),
-            pltpu.SemaphoreType.DMA((chips * parts,)),
-            pltpu.SemaphoreType.DMA((max(chips - 1, 1) * parts,)),
-            pltpu.SemaphoreType.DMA((max(chips - 1, 1) * parts,)),
-        ]
-        + scalar_scratch(chips, dense),
+        scratch_shapes=scatter_scratch(count, rows, features) + scalar_scratch(count // 2, dense),
         compiler_params=comm_params(ident),
         cost_estimate=cost(flops, 20e6),
         name=name,
@@ -1181,9 +1465,8 @@
     segc_window = window[:, None]
     segc = local_seg[:, None]
     segr = local_seg[None, :]
-    key_last = window[SPAN - 1 :: SPAN].reshape(reach + 1, blocks)
-    query_first = local_seg[::SPAN]
-    low_blocks = jnp.sum((key_last[None] < query_first[:, None, None]).astype(jnp.int32), axis=2).reshape(-1)
+    key_last = window[SPAN - 1 :: SPAN]
+    low_blocks = jnp.sum((key_last[None, :] < local_seg[::SPAN][:, None]).astype(jnp.int32), axis=1)
 
     owner = jnp.arange(inner, dtype=jnp.int32)[None, :] // SSM_DIM
     wide = (owner == jnp.arange(LANES, dtype=jnp.int32)[:, None]).astype(f32)
@@ -1198,14 +1481,15 @@
         tall,
     )
     count = lax.axis_size("head")
-    gate_weight, inner_weight = proj_zx[:, 0, :], proj_zx[:, 1, :]
+    zx_weight = proj_zx.reshape(D, 2 * inner)
     bcs_weight = jnp.concatenate([proj_bc, fit(proj_step, LANES, 1)], axis=1)
     qkv_weight = fit(proj_qkv, att_pad, 2).reshape(D, 3 * att_pad)
     att_weight = fit(attention_out, att_pad, 0)
 
     first_full, first_rms, zed, inner_x, bcs = first_gather(
-        tokens, first_gain, (gate_weight, inner_weight, bcs_weight), 0
-    )
+        tokens, first_gain, zx_weight, bcs_weight, 0
+    )
+    rms_columns = first_rms
     first_rms = first_rms[:, 0:1]
     cot_full = lax.all_gather(cotangent, "head")
     edge_rows = jnp.concatenate([inner_x[rows - 8 :], bcs[rows - 8 :, :bc_width]], axis=1)
@@ -1238,32 +1522,24 @@
     moved = [from_behind(key_value, "seq", back) for back in range(1, reach + 1)]
 
     back_attended = gathered_product(cot_full, att_weight, "back_attended")
-    pieces = [(projected, pairs)] + [(array, 0) for array in moved]
-    attended, back_query, back_key, back_value, *back_moved = attention(
-        low_blocks, projected, back_attended, pieces, segc_window, segr, att_pad, rows
+    near_pair, far_pair = moved
+    attended, back_query, back_pair, *back_moved = attention(
+        low_blocks, projected, back_attended, near_pair, far_pair, segc_window, segr, att_pad
     )
     out_part = spread_product(attended, att_weight, count, "output_product")
+    (grad_att,) = weight_grad(cot_full, (attended,), "grad_attention_out")
+
+    returned = [from_behind(back_moved[back - 1], "seq", -back) for back in range(1, reach + 1)]
+    *returned, out_part, grad_att = lax.optimization_barrier((*returned, out_part, grad_att))
+    back_pair = back_pair + sum(pair.astype(f32) for pair in returned)
+    back_projected = jnp.concatenate([back_query, back_pair], axis=1).astype(bf16)
     output = (
         hidden_one + lax.psum_scatter(out_part, "head", scatter_dimension=0).astype(f32)
     ).astype(bf16)
-    (grad_att,) = weight_grad(cot_full, (attended,), "grad_attention_out")
-
-    for back in range(1, reach + 1):
-        pair = jnp.concatenate(back_moved[2 * back - 2 : 2 * back], axis=1)
-        pair = from_behind(pair, "seq", -back).astype(f32)
-        back_key = back_key + pair[:, :att_pad]
-        back_value = back_value + pair[:, att_pad:]
-    back_projected = jnp.concatenate([back_query, back_key, back_value], axis=1).astype(bf16)
     second_sums = jnp.sum(back_projected.astype(f32) * projected.astype(f32), axis=1)
     back_second, second_dots = matmul_scatter(
         (back_projected,), (qkv_weight,), second_sums, True, count, 3, "second_scatter"
     )
-    (grad_qkv,) = weight_grad(
-        second_full, ((back_projected.astype(f32) * second_rms).astype(bf16),), "grad_qkv"
-    )
-    if att != att_pad:
-        grad_att = grad_att[:, :att]
-        grad_qkv = grad_qkv.reshape(D, 3, att_pad)[:, :, :att].reshape(D, 3 * att)
     grad_second_gain = jnp.sum(hidden_one * second_rms * back_second, axis=0)
     back_hidden_one = (
         cotangent.astype(f32)
@@ -1271,9 +1547,13 @@
         - hidden_one * (second_rms * second_rms / D * second_dots.reshape(rows, 1))
     )
     back_low = back_hidden_one.astype(bf16)
-    back_branch, gate_dots, back_gated = gather_matmul(
-        back_low, jnp.sum(back_low.astype(f32) * branch, axis=1), proj_out, True, False, 4, "branch_gather"
-    )
+    back_branch, gate_dots, back_gated, grad_qkv = gather_matmul(
+        back_low, jnp.sum(back_low.astype(f32) * branch, axis=1), proj_out, True, False, 4, "branch_gather",
+        (second_full, (back_projected.astype(f32) * second_rms).astype(bf16)),
+    )
+    if att != att_pad:
+        grad_att = grad_att[:, :att]
+        grad_qkv = grad_qkv.reshape(D, 3, att_pad)[:, :, :att].reshape(D, 3 * att)
     coefficients = fit(
         jnp.concatenate([gate_rms, gate_rms * gate_rms / INNER * gate_dots.reshape(rows, 1)], axis=1), 8, 1
     )
@@ -1290,6 +1570,7 @@
     (grad_out,) = weight_grad(back_branch, (gated,), "grad_out")
     (grad_gate,) = weight_grad(first_full, (back_z,), "grad_gate")
 
+    back_end, grad_out, grad_gate = lax.optimization_barrier((back_end, grad_out, grad_gate))
     back_x, back_bc, back_step, tail_rows, back_edge, grad_conv, grad_heads = ssd_backward(
         *ssd_shared, dy, states, opened, entering, back_end, constants, inner, width
     )
@@ -1303,12 +1584,17 @@
         + jnp.sum(back_bc.astype(f32) * bcs[:, :bc_width], axis=1)
         + jnp.sum(back_step.astype(f32) * bcs[:, bc_width:], axis=1)
     )
-    back_first, first_dots = matmul_scatter(
-        (back_z, back_x, back_bc, back_step),
-        (gate_weight, inner_weight, proj_bc, bcs_weight[:, bc_width:]),
-        first_sums, True, count, 5, "first_scatter",
-    )
-    grad_first_gain = jnp.sum(hidden_zero * first_rms * back_first, axis=0)
+    small_parts = (grad_conv[:5, :inner], grad_gated_gain[0], grad_second_gain, grad_heads[:3].reshape(-1))
+    flat = jnp.concatenate([part.reshape(-1) for part in small_parts])
+    state_rows = 16
+    state = fit(grad_conv[:5, inner:].reshape(-1, LANES), state_rows, 0)
+    lines = -(-flat.size // (8 * LANES)) * 8
+    small = jnp.concatenate([jnp.zeros((state_rows, LANES), f32), fit(flat, lines * LANES, 0).reshape(lines, LANES)], axis=0)
+    back_first, totals, small_all, shared_bc, first_sum, *wide_tail, wide_step = tail(
+        (back_z, back_x, back_bc, back_step), zx_weight, proj_bc, bcs_weight,
+        first_sums, state, small, grad_inner, grad_step, grad_bc.T, tokens, rms_columns, count, 5,
+    )
+    first_dots = totals[: rows // LANES]
     grad_tokens = (
         back_hidden_one
         + first_rms * first_gain * back_first
@@ -1319,40 +1605,38 @@
     wide_qkv = seq_scatter(grad_qkv).reshape(-1, 3, att)
     wide_out = seq_scatter(grad_out).T
     wide_gate = seq_scatter(grad_gate)
-    wide_tail = seq_scatter(jnp.concatenate([grad_inner, grad_step], axis=1))
-    wide_zx = jnp.stack([wide_gate, wide_tail[:, :inner]], axis=1)
-    wide_step = wide_tail[:, inner : inner + heads]
-    shared_bc = lax.psum_scatter(grad_bc, ("seq", "head"), scatter_dimension=1, tiled=True).astype(f32)
-    small = lax.psum(
-        (
-            grad_first_gain,
-            grad_conv[:5],
-            grad_heads[:3, :heads],
-            grad_gated_gain[0],
-            grad_second_gain,
-        ),
-        "seq",
-    )
+    wide_zx = jnp.stack([wide_gate, jnp.concatenate(wide_tail, axis=1)], axis=1)
+    wide_step = wide_step[:, :heads]
+    small = jnp.sum(small_all, axis=0)
+    state_sum = small[:10].reshape(5, bc_width)
+    flat = small[state_rows:].reshape(-1)
+    picked = []
+    at = 0
+    for part in small_parts:
+        picked.append(flat[at : at + part.size].reshape(part.shape))
+        at += part.size
+    conv_sum, gated_sum, second_sum, heads_sum = picked
+    heads_sum = heads_sum.reshape(3, LANES)[:, :heads]
     shared = bc_width // (lax.axis_size("seq") * count)
     shared_at = (lax.axis_index("seq") * count + lax.axis_index("head")) * shared
-    shared_conv = lax.dynamic_slice_in_dim(lax.psum(small[1][:, inner:], "head"), shared_at, shared, 1)
+    shared_conv = lax.dynamic_slice_in_dim(state_sum, shared_at, shared, 1)
     return (
         output,
         grad_tokens,
-        small[0],
+        first_sum[0],
         wide_zx,
-        shared_bc,
+        shared_bc.T,
         wide_step,
-        small[1][:4, :inner],
-        small[1][4, :inner],
+        conv_sum[:4],
+        conv_sum[4],
         shared_conv[:4],
         shared_conv[4],
-        small[2][0],
-        small[2][1],
-        small[2][2],
-        small[3],
+        heads_sum[0],
+        heads_sum[1],
+        heads_sum[2],
+        gated_sum,
         wide_out,
-        small[4],
+        second_sum,
         wide_qkv,
         wide_att,
     )

time: 1050 us -> 805 us (0.77); the launches traced: 1060 us -> 797 us
  waiting for transfers between devices: 490 us -> 235 us
  Pallas kernels: 366 us -> 422 us
  blocking collectives: 45.2 us -> 0 us
  local copies, waits for them, and re-layouts: 61.4 us -> 48.1 us
    reduce_scatter x5 -> x4, waiting for transfers between devices: 243 us -> 79.5 us  [seq_scatter(): lax.psum_scatter(values.astype(bf16), 'seq', scatter_dimension=0, tiled=T...]
    pallas_call x4 -> x5, Pallas kernels: 147 us -> 240 us  [the longest x1 91.8 us: tail(): pl.pallas_call(partial(tail_kernel, count, streams, state_rows), in_specs...]
    psum x2 -> x0, blocking collectives: 45.2 us -> none  [the longest x1 39 us: per_device(): lax.psum((grad_first_gain, grad_conv[:5], grad_heads[:3, :heads], grad_ga...]
    unnamed x9 -> x6, waiting for transfers between devices: 41.7 us -> 1.39 us
    ppermute x10, waiting for transfers between devices: 167 us -> 138 us  [from_behind(): return lax.ppermute(value, axis, pairs)]
    pallas_call x3 -> x2, Pallas kernels: 82.7 us -> 53.3 us  [matmul_scatter(): pl.pallas_call(partial(scatter_kernel, count, len(lefts), transposed), in...]
    reduce_scatter x1, waiting for transfers between devices: 37.6 us -> 16.6 us  [per_device(): lax.psum_scatter(out_part, 'head', scatter_dimension=0).astype(f32)]
    pallas_call x5 -> x4, Pallas kernels: 33.7 us -> 25.5 us  [weight_grad(): pl.pallas_call(partial(weight_grad_kernel, len(rights)), grid=(count,), i...]
  transfers between devices with their start and end apart: 18 -> 16, of which waited for: 14 -> 9; matrix products, arithmetic and copies ran while one was open for 8% -> 9% of each run, Pallas kernels for 27% -> 44%
where the time goes in v3:
time: 805 us; the launch traced here: 797 us
  Pallas kernels  422 us (52%)
  waiting for transfers between devices  235 us (29%)
  other arithmetic  49.7 us (6%)
  local copies, waits for them, and re-layouts  48.1 us (6%)
  starting transfers between devices  27.6 us (3%)
  between operations  15.2 us (2%)
    ppermute x10, waiting for transfers between devices, from_behind(): return lax.ppermute(value, axis, pairs)  138 us
    pallas_call x1, Pallas kernels, tail(): pl.pallas_call(partial(tail_kernel, count, streams, state_rows), in_specs...  91.8 us
    reduce_scatter x4, waiting for transfers between devices, seq_scatter(): lax.psum_scatter(values.astype(bf16), 'seq', scatter_dimension=0, tiled=T...  79.5 us
    pallas_call x2, Pallas kernels, gather_matmul(): pl.pallas_call(partial(gather_kernel, count, transposed, scaled, bool(fil...  78.2 us
    pallas_call x2, Pallas kernels, matmul_scatter(): pl.pallas_call(partial(scatter_kernel, count, len(lefts), transposed), in...  53.3 us
    pallas_call x1, Pallas kernels, ssd_backward(): pl.pallas_call(ssd_backward_kernel, grid_spec=pltpu.PrefetchScalarGridSpe...  52.8 us
    pallas_call x1, Pallas kernels, attention(): pl.pallas_call(partial(attention_kernel, scale=1.0 / math.sqrt(ATT_DIM)),...  37.9 us
    pallas_call x1, Pallas kernels, first_gather(): pl.pallas_call(partial(first_gather_kernel, count), in_specs=[VMEM] * 4,...  32.4 us
  transfers between devices with their start and end apart: 16, of which 9 were waited for; matrix products, arithmetic and copies ran while one was open for 9% of the time, Pallas kernels for 44%

profile of v3, /device:TPU:0, one launch (start us, length us, event | category | flops | bytes accessed | tf_op | source)
XLA Modules:
  0.0 797.2 jit_solution(14977558801950992710)
XLA Ops:
  7.3 5.5 copy.106
  14.8 32.4 %first_gather.1 = (bf16[4,1024,384]{2,1,0:T(8,128)(2,1)}, f32[1024,8]{1,0:T(8,128)}, f32[1024,768]{1,0:T(8,128)}, f32[1024,768]{1,0:T(8,128)}, f32[1024,384]{1,0:T(8,128)}) custom-call(bf16[1024,384]{1,0:T(8,128)(2,1)} %refs_12_.1, f32[8,384]{1,0:T(8,128)} %pad.35.gain_ref, bf16[1536,1536]{1,0:T(8,128)(2,1)} %bitcast.76, bf16[1536,384]{1,0:T(8,128)(2,1)} %fusion.6.bcs_ref.refs_6_), custom_call_target="tpu_custom_call" | custom-call | flops 6039797760 | bytes 30000000 | tf_op jit(solution)/shard_map/first_gather/pallas_call | solution.py:871
  48.6 4.0 collective-permute-start
  61.3 19.5 %ssd_forward.1 = (f32[1024,768]{1,0:T(8,128)}, bf16[1024,128]{1,0:T(8,128)(2,1)}, f32[1024,128]{1,0:T(8,128)}, bf16[3072,128]{1,0:T(8,128)(2,1)}, f32[768,128]{1,0:T(8,128)}, /*index=5*/f32[8,128]{1,0:T(8,128)}) custom-call(s32[4]{0:T(128)} %bitcast.98, s32[4]{0:T(128)} %slice.157.last_ref, f32[1024,768]{1,0:T(8,128)} %get-tuple-element.78.x_ref.xprev_ref, ...), custom_call_target="tpu_custom_call" | custom-call | flops 1207959552 | bytes 9437184 | tf_op jit(solution)/shard_map/ssd_forward/pallas_call | solution.py:486
  83.2 4.1 collective-permute-start.1
  87.9 4.3 copy.94
  92.2 3.9 copy.95.weight_ref.refs_1_
  96.1 3.3 collective-permute-start.2
  100.5 2.6 collective-permute-done.2
  104.0 10.5 %gate_forward.1 = (f32[1024,768]{1,0:T(8,128)}, bf16[1024,768]{1,0:T(8,128)(2,1)}, f32[8,1024]{1,0:T(8,128)}) custom-call(f32[1024,768]{1,0:T(8,128)} %get-tuple-element.80.y_ref, bf16[1024,128]{1,0:T(8,128)(2,1)} %get-tuple-element.81.c_ref, f32[1024,128]{1,0:T(8,128)} %get-tuple-element.82.open_ref.openprev_ref, bf16[768,128]{1,0:T(8,128)(2,1)} %fusion.7.enter_ref, ...), custom_call_target="tpu_custom_call" | custom-call | flops 402653184 | bytes 11010048 | tf_op jit(solution)/shard_map/gate_forward/pallas_call | solution.py:574
  115.8 26.0 %branch_scatter.1 = (f32[1024,384]{1,0:T(8,128)}, f32[8,128]{1,0:T(8,128)}) custom-call(bf16[1024,768]{1,0:T(8,128)(2,1)} %get-tuple-element.86.refs_0_, bf16[768,1536]{1,0:T(8,128)(2,1)} %weight_ref.5, f32[8,128]{1,0:T(8,128)} %bitcast.95), custom_call_target="tpu_custom_call" | custom-call | flops 2415919104 | bytes 20000000 | tf_op jit(solution)/shard_map/branch_scatter/pallas_call | solution.py:1359
  142.6 2.5 multiply_reduce_fusion.4
  146.1 36.2 %second_gather.1 = (bf16[4,1024,384]{2,1,0:T(8,128)(2,1)}, f32[8,128]{1,0:T(8,128)}, bf16[1024,1152]{1,0:T(8,128)(2,1)}) custom-call(bf16[1024,384]{1,0:T(8,128)(2,1)} %multiply_convert_fusion.own_ref, f32[8,128]{1,0:T(8,128)} %bitcast.97, bf16[1536,1152]{1,0:T(8,128)(2,1)} %copy.95.weight_ref.refs_1_), custom_call_target="tpu_custom_call" | custom-call | flops 3623878656 | bytes 20000000 | tf_op jit(solution)/shard_map/second_gather/pallas_call | solution.py:963
  183.9 4.6 collective-permute-start.3
  188.5 4.3 collective-permute-start.4
  193.6 1.7 copy.96.segc_ref
  196.0 5.4 back_attended.1.do_ref
  201.4 18.9 %collective-permute-done.3.near_ref = bf16[1024,768]{1,0:T(8,128)(2,1)} collective-permute-done((bf16[1024,768]{1,0:T(8,128)(2,1)S(1)}, bf16[1024,768]{1,0:T(8,128)(2,1)}, u32[]{:S(2)}, u32[]{:S(2)}) %collective-permute-start.3) | collective-permute-done | bytes 1572896 | tf_op jit(solution)/shard_map/ppermute | solution.py:434
  220.4 4.0 collective-permute-done.4.far_ref
  224.4 37.9 %attention.1 = (bf16[1024,384]{1,0:T(8,128)(2,1)}, f32[1024,384]{1,0:T(8,128)}, f32[1024,768]{1,0:T(8,128)}, bf16[1024,768]{1,0:T(8,128)(2,1)}, bf16[1024,768]{1,0:T(8,128)(2,1)}) custom-call(s32[4]{0:T(128)} %convert_reduce_fusion.low_ref, bf16[1024,1152]{1,0:T(8,128)(2,1)} %get-tuple-element.90.projected_ref, bf16[1024,384]{1,0:T(8,128)(2,1)} %back_attended.1.do_ref, ...), custom_call_target="tpu_custom_call" | custom-call | flops 11274289152 | bytes 11796480 | tf_op jit(solution)/shard_map/attention/pallas_call | solution.py:643
  266.6 5.4 output_product.1
  272.0 5.2 grad_attention_out.1
  277.3 63.0 %collective-permute-done.5 = bf16[1024,768]{1,0:T(8,128)(2,1)} collective-permute-done((bf16[1024,768]{1,0:T(8,128)(2,1)}, bf16[1024,768]{1,0:T(8,128)(2,1)}, u32[]{:S(2)}, u32[]{:S(2)}) %collective-permute-start.5) | collective-permute-done | bytes 1572896 | tf_op jit(solution)/shard_map/ppermute | solution.py:434
  340.2 34.9 %collective-permute-done.6 = bf16[1024,768]{1,0:T(8,128)(2,1)} collective-permute-done((bf16[1024,768]{1,0:T(8,128)(2,1)}, bf16[1024,768]{1,0:T(8,128)(2,1)}, u32[]{:S(2)}, u32[]{:S(2)}) %collective-permute-start.6) | collective-permute-done | bytes 1572896 | tf_op jit(solution)/shard_map/ppermute | solution.py:434
  375.1 3.3 add_convert_fusion
  378.4 1.7 pad_maximum_fusion.refs_0_
  380.9 3.0 fusion.1
  384.0 27.3 %second_scatter.1 = (f32[1024,384]{1,0:T(8,128)}, f32[8,128]{1,0:T(8,128)}) custom-call(bf16[1024,1152]{1,0:T(8,128)(2,1)} %pad_maximum_fusion.refs_0_, bf16[1536,1152]{1,0:T(8,128)(2,1)} %copy.95.weight_ref.refs_1_, f32[8,128]{1,0:T(8,128)} %bitcast.93), custom_call_target="tpu_custom_call" | custom-call | flops 3623878656 | bytes 20000000 | tf_op jit(solution)/shard_map/second_scatter/pallas_call | solution.py:1359
  412.0 3.7 multiply_reduce_fusion.3
  415.7 41.9 %branch_gather.1 = (bf16[4,1024,384]{2,1,0:T(8,128)(2,1)}, f32[8,128]{1,0:T(8,128)}, bf16[1024,768]{1,0:T(8,128)(2,1)}, bf16[1536,1152]{1,0:T(8,128)(2,1)}) custom-call(bf16[1024,384]{1,0:T(8,128)(2,1)} %get-tuple-element.231.own_ref, f32[8,128]{1,0:T(8,128)} %bitcast.96, bf16[768,1536]{1,0:T(8,128)(2,1)} %weight_ref.5, ...), custom_call_target="tpu_custom_call" | custom-call | flops 2415919104 | bytes 20000000 | tf_op jit(solution)/shard_map/branch_gather/pallas_call | solution.py:963
  459.4 8.8 %gate_backward.1 = (bf16[1024,768]{1,0:T(8,128)(2,1)}, bf16[1024,768]{1,0:T(8,128)(2,1)}, bf16[1024,768]{1,0:T(8,128)(2,1)}, f32[1,768]{1,0:T(1,128)}, f32[768,128]{1,0:T(8,128)}) custom-call(bf16[1024,768]{1,0:T(8,128)(2,1)} %get-tuple-element.104.bg_ref, f32[1024,768]{1,0:T(8,128)} %get-tuple-element.105.ssd_ref, f32[1024,768]{1,0:T(8,128)} %get-tuple-element.85.z_ref, ...), custom_call_target="tpu_custom_call" | custom-call | flops 402653184 | bytes 14155776 | tf_op jit(solution)/shard_map/gate_backward/pallas_call | solution.py:605
  471.8 6.4 grad_gate.1
  478.3 6.4 grad_out.1
  484.8 10.6 %collective-permute-done.8 = bf16[768,128]{1,0:T(8,128)(2,1)S(1)} collective-permute-done((bf16[768,128]{1,0:T(8,128)(2,1)S(1)}, bf16[768,128]{1,0:T(8,128)(2,1)S(1)}, u32[]{:S(2)}, u32[]{:S(2)}) %collective-permute-start.8) | collective-permute-done | bytes 196640 | tf_op jit(solution)/shard_map/ppermute | solution.py:434
  499.7 1.8 multiply_reduce_fusion.1
  501.5 52.8 %ssd_backward.1 = (bf16[1024,768]{1,0:T(8,128)(2,1)}, bf16[1024,256]{1,0:T(8,128)(2,1)}, bf16[1024,128]{1,0:T(8,128)(2,1)}, f32[8,1024]{1,0:T(8,128)}, f32[8,102...) custom-call(s32[4]{0:T(128)} %bitcast.99, s32[4]{0:T(128)} %slice.157.last_ref, ...), custom_call_target="tpu_custom_call" | custom-call | flops 2818572288 | bytes 12582912 | tf_op jit(solution)/shard_map/ssd_backward/pallas_call | solution.py:526
  559.9 3.6 collective-permute-done.9
  565.5 7.5 grad_inner.1
  573.0 2.4 copy.100
  577.0 1.8 multiply_reduce_fusion
  579.4 91.8 %tail.1 = (f32[1024,384]{1,0:T(8,128)}, f32[24,128]{1,0:T(8,128)}, f32[8,64,128]{2,1,0:T(8,128)}, f32[8,1536]{1,0:T(8,128)}, f32[8,384]{1,0:T(8,128)}, /*index=5...) custom-call(bf16[1024,768]{1,0:T(8,128)(2,1)} %get-tuple-element.107.refs_0_, ...), custom_call_target="tpu_custom_call" | custom-call | flops 6039797760 | bytes 40000000 | tf_op jit(solution)/shard_map/tail/pallas_call | solution.py:1321
  674.6 1.6 copy.103
  681.2 1.6 convert_bitcast_fusion.1
  683.9 1.9 copy.102
  685.9 1.8 convert_bitcast_fusion
  687.7 16.6 %reduce-scatter.6.cloned.1.call-done = bf16[1,1024,384]{2,1,0:T(8,128)(2,1)} async-done(((bf16[4,1024,384]{2,1,0:T(8,128)(2,1)}), bf16[1,1024,384]{2,1,0:T(8,128)(2,1)}) %reduce-scatter.6.cloned.1.call-update) | async-done | bytes 786448 | tf_op jit(solution)/shard_map/reduce_scatter | solution.py:1537
  704.3 3.5 fusion.4
  707.7 79.5 %reduce-scatter.12.cloned.1.call-done = bf16[192,1152]{1,0:T(8,128)(2,1)} async-done(((bf16[1536,1152]{1,0:T(8,128)(2,1)}), bf16[192,1152]{1,0:T(8,128)(2,1)}) %reduce-scatter.12.cloned.1.call-update) | async-done | bytes 442384 | tf_op jit(solution)/shard_map/reduce_scatter | solution.py:678
  (187 shorter events, 60.6 us)
Async XLA Ops:
  7.2 188.8 %all-gather.3.cloned.1.call-start = ((), (), s32[]{:S(2)}) async-start(), calls=%async_computation.10 | async-start | bytes 3932160 | tf_op jit(solution)/shard_map/all_gather | solution.py:1494
  7.2 5.5 copy-start.17
  7.2 5.8 copy-start.22
  7.3 5.8 copy-start.10
  14.8 38.0 %copy-start.12 = (s32[8192]{0:T(1024)S(1)}, s32[8192]{0:T(1024)}, u32[]{:S(2)}) copy-start(s32[8192]{0:T(1024)} %param.20) | copy-start | bytes 98308
  14.8 38.6 %copy-start.21 = (f32[4,768]{1,0:T(4,128)S(1)}, f32[4,768]{1,0:T(4,128)}, u32[]{:S(2)}) copy-start(f32[4,768]{1,0:T(4,128)} %param.25) | copy-start | bytes 36868
  14.8 38.6 %copy-start.30 = (f32[12]{0:T(128)S(1)}, f32[12]{0:T(128)}, u32[]{:S(2)}) copy-start(f32[12]{0:T(128)} %param.30) | copy-start | bytes 148
  14.8 38.7 %copy-start.25 = (f32[4,256]{1,0:T(4,128)S(1)}, f32[4,256]{1,0:T(4,128)}, u32[]{:S(2)}) copy-start(f32[4,256]{1,0:T(4,128)} %param.27) | copy-start | bytes 12292
  47.2 8.9 %copy-start.26 = (f32[768]{0:T(1024)S(1)}, f32[768]{0:T(1024)}, u32[]{:S(2)}) copy-start(f32[768]{0:T(1024)} %param.26) | copy-start | bytes 9220
  47.2 8.9 %copy-start.28 = (f32[256]{0:T(256)S(1)}, f32[256]{0:T(256)}, u32[]{:S(2)}) copy-start(f32[256]{0:T(256)} %param.28) | copy-start | bytes 3076
  48.6 10.2 %copy-start.29 = (f32[12]{0:T(128)S(1)}, f32[12]{0:T(128)}, u32[]{:S(2)}) copy-start(f32[12]{0:T(128)} %param.31) | copy-start | bytes 148
  48.6 11.5 %copy-start.31 = (f32[12]{0:T(128)S(1)}, f32[12]{0:T(128)}, u32[]{:S(2)}) copy-start(f32[12]{0:T(128)} %param.29) | copy-start | bytes 148
  48.6 12.0 %collective-permute-start = (f32[8,1024]{1,0:T(8,128)S(1)}, f32[8,1024]{1,0:T(8,128)S(1)}, u32[]{:S(2)}, u32[]{:S(2)}) collective-permute-start(f32[8,1024]{1,0:T(8,128)S(1)} %pad_maximum_fusion.4), channel_id=1, source_target_pairs={{0,4},{4,8},{8,12},{12,16},{16,20},{20,24},{24,28},{1,5},{5,9},{9,... | collective-permute-start | bytes 98312 | tf_op jit(solution)/shard_map/ppermute | solution.py:434
  52.7 628.5 %reduce-scatter.14.cloned.1.call-start = ((), (), s32[]{:S(2)}) async-start(), calls=%async_computation.9 | async-start | bytes 1327104 | tf_op jit(solution)/shard_map/reduce_scatter | solution.py:678
  53.0 7.7 copy-start.16
  53.5 7.2 copy-start.15
  60.7 0.6 copy-start.14
  61.3 26.1 %copy-start.24 = (f32[768]{0:T(1024)S(1)}, f32[768]{0:T(1024)}, u32[]{:S(2)}) copy-start(f32[768]{0:T(1024)} %param.32) | copy-start | bytes 9220
  81.8 5.6 copy-start.9
  83.2 16.2 %collective-permute-start.1 = (bf16[776,128]{1,0:T(8,128)(2,1)}, bf16[776,128]{1,0:T(8,128)(2,1)}, u32[]{:S(2)}, u32[]{:S(2)}) collective-permute-start(bf16[776,128]{1,0:T(8,128)(2,1)} %pad_maximum_fusion.3), channel_id=1, source_target_pairs={{0,4},{4,8},{8,12},{12,16},{16,20},{20,24},{24,28},{1,5},{5,9},{9,... | collective-permute-start | bytes 595976 | tf_op jit(solution)/shard_map/ppermute | solution.py:434
  96.1 7.0 collective-permute-start.2
  115.8 26.7 %copy-start.7 = (bf16[1024,384]{1,0:T(8,128)(2,1)S(1)}, bf16[1024,384]{1,0:T(8,128)(2,1)}, u32[]{:S(2)}) copy-start(bf16[1024,384]{1,0:T(8,128)(2,1)} %refs_12_.1) | copy-start | bytes 2359300
  142.6 2.5 copy-start.19
  145.0 267.0 %copy-start.2 = (f32[1024,384]{1,0:T(8,128)}, f32[1024,384]{1,0:T(8,128)S(1)}, u32[]{:S(2)}) copy-start(f32[1024,384]{1,0:T(8,128)S(1)} %get-tuple-element.233) | copy-start | bytes 4718596
  182.4 11.1 %copy-start.13 = (s32[8192]{0:T(1024)S(1)}, s32[8192]{0:T(1024)}, u32[]{:S(2)}) copy-start(s32[8192]{0:T(1024)} %param.20) | copy-start | bytes 98308
  183.9 36.5 %collective-permute-start.3 = (bf16[1024,768]{1,0:T(8,128)(2,1)S(1)}, bf16[1024,768]{1,0:T(8,128)(2,1)}, u32[]{:S(2)}, u32[]{:S(2)}) collective-permute-start(bf16[1024,768]{1,0:T(8,128)(2,1)S(1)} %slice.169), channel_id=1, source_target_pairs={{0,4},{4,8},{8,12},{12,16},{16,20},{20,24},{24,28},{1,5},{5,9},{9,... | collective-permute-start | bytes 4718600 | tf_op jit(solution)/shard_map/ppermute | solution.py:434
  188.5 35.9 %collective-permute-start.4 = (bf16[1024,768]{1,0:T(8,128)(2,1)S(1)}, bf16[1024,768]{1,0:T(8,128)(2,1)}, u32[]{:S(2)}, u32[]{:S(2)}) collective-permute-start(bf16[1024,768]{1,0:T(8,128)(2,1)S(1)} %slice.169), channel_id=1, source_target_pairs={{0,8},{4,12},{8,16},{12,20},{16,24},{20,28},{1,9},{5,13},{9,17},{1... | collective-permute-start | bytes 4718600 | tf_op jit(solution)/shard_map/ppermute | solution.py:434
  201.4 63.7 %copy-start.20 = (f32[8,128]{1,0:T(8,128)S(1)}, f32[8,128]{1,0:T(8,128)}, u32[]{:S(2)}) copy-start(f32[8,128]{1,0:T(8,128)} %get-tuple-element.95) | copy-start | bytes 12292
  262.3 77.9 %collective-permute-start.5 = (bf16[1024,768]{1,0:T(8,128)(2,1)}, bf16[1024,768]{1,0:T(8,128)(2,1)}, u32[]{:S(2)}, u32[]{:S(2)}) collective-permute-start(bf16[1024,768]{1,0:T(8,128)(2,1)} %get-tuple-element.91), channel_id=1, source_target_pairs={{4,0},{8,4},{12,8},{16,12},{20,16},{24,20},{28,24},{5,1},{9,5},{13... | collective-permute-start | bytes 4718600 | tf_op jit(solution)/shard_map/ppermute | solution.py:434
  263.6 111.5 %collective-permute-start.6 = (bf16[1024,768]{1,0:T(8,128)(2,1)}, bf16[1024,768]{1,0:T(8,128)(2,1)}, u32[]{:S(2)}, u32[]{:S(2)}) collective-permute-start(bf16[1024,768]{1,0:T(8,128)(2,1)} %get-tuple-element.92), channel_id=1, source_target_pairs={{8,0},{12,4},{16,8},{20,12},{24,16},{28,20},{9,1},{13,5},{17,9},{2... | collective-permute-start | bytes 4718600 | tf_op jit(solution)/shard_map/ppermute | solution.py:434
  378.4 2.5 copy-start.6
  383.9 298.9 %reduce-scatter.8.cloned.1.call-start = ((), (), s32[]{:S(2)}) async-start(), calls=%async_computation.6 | async-start | bytes 2654208 | tf_op jit(solution)/shard_map/reduce_scatter | solution.py:678
  384.0 28.0 %copy-start.4 = (bf16[1024,384]{1,0:T(8,128)(2,1)S(1)}, bf16[1024,384]{1,0:T(8,128)(2,1)}, u32[]{:S(2)}) copy-start(bf16[1024,384]{1,0:T(8,128)(2,1)} %param.37) | copy-start | bytes 2359300
  469.2 26.2 %collective-permute-start.8 = (bf16[768,128]{1,0:T(8,128)(2,1)S(1)}, bf16[768,128]{1,0:T(8,128)(2,1)S(1)}, u32[]{:S(2)}, u32[]{:S(2)}) collective-permute-start(bf16[768,128]{1,0:T(8,128)(2,1)S(1)} %convert_element_type.145), channel_id=1, source_target_pairs={{8,0},{12,4},{16,8},{20,12},{24,16},{28,20},{9,1},{13,5},{17,9},{2... | collective-permute-start | bytes 589832 | tf_op jit(solution)/shard_map/ppermute | solution.py:434
  470.5 14.1 %collective-permute-start.7 = (bf16[776,128]{1,0:T(8,128)(2,1)S(1)}, bf16[776,128]{1,0:T(8,128)(2,1)S(1)}, u32[]{:S(2)}, u32[]{:S(2)}) collective-permute-start(bf16[776,128]{1,0:T(8,128)(2,1)S(1)} %pad_maximum_fusion.2), channel_id=1, source_target_pairs={{4,0},{8,4},{12,8},{16,12},{20,16},{24,20},{28,24},{5,1},{9,5},{13... | collective-permute-start | bytes 595976 | tf_op jit(solution)/shard_map/ppermute | solution.py:434
  496.4 189.5 %reduce-scatter.10.cloned.1.call-start = ((), (), s32[]{:S(2)}) async-start(), calls=%async_computation.7 | async-start | bytes 2654208 | tf_op jit(solution)/shard_map/reduce_scatter | solution.py:678
  496.9 207.3 %reduce-scatter.6.cloned.1.call-start = ((), (), s32[]{:S(2)}) async-start(), calls=%async_computation.5 | async-start | bytes 3932160 | tf_op jit(solution)/shard_map/reduce_scatter | solution.py:1537
  497.5 289.7 %reduce-scatter.12.cloned.1.call-start = ((), (), s32[]{:S(2)}) async-start(), calls=%async_computation.8 | async-start | bytes 3981312 | tf_op jit(solution)/shard_map/reduce_scatter | solution.py:678
  497.8 0.7 copy-start.27
  497.8 1.9 copy-start.1
  554.3 9.3 %collective-permute-start.9 = (f32[8,1024]{1,0:T(8,128)}, f32[8,1024]{1,0:T(8,128)S(1)}, u32[]{:S(2)}, u32[]{:S(2)}) collective-permute-start(f32[8,1024]{1,0:T(8,128)} %get-tuple-element.117), channel_id=1, source_target_pairs={{4,0},{8,4},{12,8},{16,12},{20,16},{24,20},{28,24},{5,1},{9,5},{13... | collective-permute-start | bytes 98312 | tf_op jit(solution)/shard_map/ppermute | solution.py:434
  573.0 4.0 copy-start
  671.3 7.3 copy-start.11
  683.9 20.4 %copy-start.3 = (f32[1024,384]{1,0:T(8,128)S(1)}, f32[1024,384]{1,0:T(8,128)}, u32[]{:S(2)}) copy-start(f32[1024,384]{1,0:T(8,128)} %copy-done.2) | copy-start | bytes 4718596
  683.9 20.3 %copy-start.5 = (bf16[1024,384]{1,0:T(8,128)(2,1)S(1)}, bf16[1024,384]{1,0:T(8,128)(2,1)}, u32[]{:S(2)}) copy-start(bf16[1024,384]{1,0:T(8,128)(2,1)} %param.37) | copy-start | bytes 2359300
  683.9 20.3 %copy-start.8 = (bf16[1024,384]{1,0:T(8,128)(2,1)S(1)}, bf16[1024,384]{1,0:T(8,128)(2,1)}, u32[]{:S(2)}) copy-start(bf16[1024,384]{1,0:T(8,128)(2,1)} %refs_12_.1) | copy-start | bytes 2359300
  683.9 20.3 %copy-start.23 = (f32[384]{0:T(512)S(1)}, f32[384]{0:T(512)}, u32[]{:S(2)}) copy-start(f32[384]{0:T(512)} %param.21) | copy-start | bytes 4612
  707.7 81.6 %copy-start.18 = (f32[8,1536]{1,0:T(8,128)S(1)}, f32[8,1536]{1,0:T(8,128)}, u32[]{:S(2)}) copy-start(f32[8,1536]{1,0:T(8,128)} %get-tuple-element.132) | copy-start | bytes 147460
Sparse Core Ops, SparseCore 0:
  52.8 28.7 all-gather.2
  384.1 80.9 reduce-scatter.13
  496.5 79.5 reduce-scatter.7
  579.4 83.3 reduce-scatter.9
  665.1 39.0 reduce-scatter.5
  707.7 79.4 reduce-scatter.11
